TPU v7x, 32 devices: a whole 2x2x4 slice. The times are simulated.
32 devices in a mesh: dp: 4 (over x, core), mp: 8 (over z, y).
Axes of the slice: x: 2, y: 2, z: 4, core: 2. Of those that a mesh axis runs over, the one named last changes fastest.
Arguments:
- sensitivity: bfloat16 [4096, 16, 1024], P('dp', 'mp'), may hold values from -0.046875 to 0.046875
- observed: float32 [4096], P('dp'), may hold values from -6 to 6
- row_weight: float32 [4096], P('dp'), may hold values from 1 to 8
- model: float32 [2, 16, 1024], P(None, 'mp'), may hold values from -3 to 3
- smooth_weight: float32 [16, 1024], P('mp'), may hold values from 0.5 to 2
- active: int32 [2, 16, 1024], P(None, 'mp'), may hold values 0 or 1
Outputs:
- update: float32 [2, 16, 1024], P(None, 'mp')
- cg_residual: float32 [2, 16, 1024], P(None, 'mp')
All inputs are finite; a program needn't handle non-finite values. No bound on the sum of `active` on one device may be relied on, other than what follows from the above.
Results may differ from a plain program's by a relative error of at most 0.018.
Values sent between devices are 32-bit elements; how exact they have to be, the bound alone decides.
No kernel may reach another device: no remote copies, remote signals or barrier semaphores. Data moves between devices by JAX's collectives and lax.ppermute only.
A program may use at most 64 MiB of HBM per device.

v0:
```python
import jax
import jax.numpy as jnp
from jax import lax
from jax.sharding import PartitionSpec as P

GZ = 16
ITERS = 4


SMOOTHING = 0.25
COUPLING = 0.5


def with_halo(cells, sides, width):
    for axis, dim in sides:
        count = lax.axis_size(axis)
        ends = count - 1
        head = lax.slice_in_dim(cells, 0, width, axis=dim)
        tail = lax.slice_in_dim(cells, cells.shape[dim] - width, cells.shape[dim], axis=dim)
        cells = jnp.concatenate(
            [
                lax.ppermute(tail, axis, [(i, (i + 1) % count) for i in range(ends)]),
                cells,
                lax.ppermute(head, axis, [((i + 1) % count, i) for i in range(ends)]),
            ],
            axis=dim,
        )
    return cells


def inner_sum(field, column_len):
    width = field.shape[-1]
    position = jnp.arange(width) % column_len
    blank_one = jnp.zeros_like(field[..., :1])
    blank_col = jnp.zeros_like(field[..., :column_len])
    later = jnp.where(
        position != column_len - 1, jnp.concatenate([field[..., 1:], blank_one], -1), 0.0
    )
    earlier = jnp.where(position != 0, jnp.concatenate([blank_one, field[..., :-1]], -1), 0.0)
    ahead = jnp.concatenate([field[..., column_len:], blank_col], -1)
    behind = jnp.concatenate([blank_col, field[..., :-column_len]], -1)
    return later + earlier + ahead + behind


def operate(field, smooth_weight):
    padded = with_halo(field, (("mp", 1),), 1)
    beside = padded[:, 2:] + padded[:, :-2] + inner_sum(field, GZ)
    return (
        smooth_weight * field
        + SMOOTHING * (6.0 * field - beside)
        + COUPLING * (field - field[::-1])
    )


def squares(residual):
    return lax.psum(jnp.sum(residual * residual), "mp")


def local(sensitivity, observed, row_weight, model, smooth_weight, active):
    rows = sensitivity.shape[0]
    matrix = sensitivity.reshape(rows, -1)
    gravity_rows = lax.axis_index("dp") < lax.axis_size("dp") * 3 // 4
    free_mask = (1.0 - active.astype(jnp.float32)).reshape(2, -1)
    cell_shape = model.shape

    def forward(field):
        flattened = field.reshape(2, -1)
        chosen = jnp.where(gravity_rows, flattened[0], flattened[1]).astype(jnp.bfloat16)
        partial_rows = jnp.dot(matrix, chosen, preferred_element_type=jnp.float32)
        return lax.psum(partial_rows, "mp")

    def adjoint(values, regular):
        scaled = (row_weight * values).astype(jnp.bfloat16)
        columns = jnp.dot(scaled, matrix, preferred_element_type=jnp.float32)
        contrib = jnp.stack(
            [jnp.where(gravity_rows, columns, 0.0), jnp.where(gravity_rows, 0.0, columns)]
        )
        regular_flat = regular.reshape(2, -1)
        summed = lax.psum(contrib, "dp")
        image = free_mask * (summed + regular_flat)
        return image.reshape(cell_shape)

    predicted = forward(model)
    gradient = adjoint(predicted - observed, operate(model, smooth_weight))
    residual = -gradient
    direction = residual
    solution = jnp.zeros_like(model)
    norm_now = squares(residual)
    for step in range(ITERS):
        image = adjoint(forward(direction), operate(direction, smooth_weight))
        curvature = lax.psum(jnp.sum(direction * image), "mp")
        step_len = norm_now / curvature
        solution = solution + step_len * direction
        residual = residual - step_len * image
        norm_next = squares(residual)
        direction = residual + norm_next / norm_now * direction
        norm_now = norm_next
    return (solution, residual)


def solution(mesh):
    return jax.shard_map(
        local,
        mesh=mesh,
        in_specs=(
            P("dp", "mp", None),
            P("dp"),
            P("dp"),
            P(None, "mp", None),
            P("mp", None),
            P(None, "mp", None),
        ),
        out_specs=(P(None, "mp", None), P(None, "mp", None)),
        check_vma=False,
    )
```

profile of v0, /device:TPU:0, one launch (start us, length us, event | category | flops | bytes accessed | tf_op | source)
XLA Modules:
  0.0 362.9 jit_solution(3560802510243249319)
XLA Ops:
  0.6 0.8 fusion.63
  1.4 1.3 collective-permute-start
  2.7 5.5 %collective-permute-start.1 = (f32[2,1,1024]{2,1,0:T(1,128)S(1)}, f32[2,1,1024]{2,1,0:T(1,128)S(1)}, u32[]{:S(2)}, u32[]{:S(2)}) collective-permute-start(f32[2,1,1024]{2,1,0:T(1,128)S(1)} %get-tuple-element.52), channel_id=1, source_target_pairs={{0,1},{1,2},{2,3},{3,4},{4,5},{5,6},{6,7},{8,9},{9,10},{10,11},{11... | collective-permute-start | bytes 24584 | tf_op jit(solution)/shard_map/ppermute | solution.py:22
  8.3 0.9 fusion.61
  9.2 0.9 fusion.62
  10.1 5.6 %copy.10 = bf16[128,8,2,1024]{3,1,2,0:T(8,128)(2,1)} copy(bf16[128,8,2,1024]{3,2,1,0:T(2,128)(2,1)} %bitcast.88) | data formatting | bytes 8388608
  15.7 3.4 fusion.64
  19.1 20.3 %psum.126 = f32[1024]{0:T(1024)S(1)} all-reduce(f32[1024]{0:T(1024)S(1)} %bitcast.128), channel_id=1, replica_groups=mesh['dp'=4,'mp'=8] {'mp'}, use_global_device_ids=true, to_apply=%region_0.1 | all-reduce | flops 1024 | bytes 8192 | tf_op jit(solution)/shard_map/psum | solution.py:70
  39.3 2.8 fusion.65
  42.2 10.1 %psum.127 = f32[2,2048]{1,0:T(2,128)S(1)} all-reduce(f32[2,2048]{1,0:T(2,128)S(1)} %pad_maximum_fusion.10), channel_id=1, replica_groups=mesh['dp'=4,'mp'=8] {'dp'}, use_global_device_ids=true, to_apply=%region_1.2 | all-reduce | flops 4096 | bytes 32768 | tf_op jit(solution)/shard_map/psum | solution.py:79
  52.8 3.4 fusion.32
  56.2 1.3 collective-permute-start.2
  57.5 4.5 %collective-permute-start.3 = (f32[2,1,1024]{2,1,0:T(1,128)S(1)}, f32[2,1,1024]{2,1,0:T(1,128)S(1)}, u32[]{:S(2)}, u32[]{:S(2)}) collective-permute-start(f32[2,1,1024]{2,1,0:T(1,128)S(1)} %get-tuple-element.46), channel_id=1, source_target_pairs={{0,1},{1,2},{2,3},{3,4},{4,5},{5,6},{6,7},{8,9},{9,10},{10,11},{11... | collective-permute-start | bytes 24584 | tf_op jit(solution)/shard_map/ppermute | solution.py:22
  62.0 17.8 %psum.129 = f32[1024]{0:T(1024)S(1)} all-reduce(f32[1024]{0:T(1024)S(1)} %bitcast.127), channel_id=1, replica_groups=mesh['dp'=4,'mp'=8] {'mp'}, use_global_device_ids=true, to_apply=%region_4.5 | all-reduce | flops 1024 | bytes 8192 | tf_op jit(solution)/shard_map/psum | solution.py:70
  79.8 2.8 fusion.66
  82.7 10.1 %psum.130 = f32[2,2048]{1,0:T(2,128)S(1)} all-reduce(f32[2,2048]{1,0:T(2,128)S(1)} %pad_maximum_fusion.11), channel_id=1, replica_groups=mesh['dp'=4,'mp'=8] {'dp'}, use_global_device_ids=true, to_apply=%region_5.6 | all-reduce | flops 4096 | bytes 32768 | tf_op jit(solution)/shard_map/psum | solution.py:79
  92.9 0.6 multiply_reduce_fusion.6
  93.6 19.1 %all-reduce.20 = (f32[]{:T(128)}, f32[]{:T(128)}) all-reduce(f32[]{:T(128)} %get-tuple-element.3, f32[]{:T(128)} %get-tuple-element.2), channel_id=1, replica_groups=mesh['dp'=4,'mp'=8] {'mp'}, use_global_device_ids=true, to_apply=%region_3.4 | all-reduce | flops 2 | bytes 16 | tf_op jit(solution)/shard_map/psum | solution.py:56
  114.0 0.6 multiply_reduce_fusion.5
  114.7 18.4 %psum.132 = f32[]{:T(128)} all-reduce(f32[]{:T(128)} %get-tuple-element.20), channel_id=1, replica_groups=mesh['dp'=4,'mp'=8] {'mp'}, use_global_device_ids=true, to_apply=%region_9.10 | all-reduce | flops 1 | bytes 8 | tf_op jit(solution)/shard_map/psum | solution.py:56
  134.7 1.3 collective-permute-start.4
  136.0 4.5 %collective-permute-start.5 = (f32[2,1,1024]{2,1,0:T(1,128)S(1)}, f32[2,1,1024]{2,1,0:T(1,128)S(1)}, u32[]{:S(2)}, u32[]{:S(2)}) collective-permute-start(f32[2,1,1024]{2,1,0:T(1,128)S(1)} %get-tuple-element.40), channel_id=1, source_target_pairs={{0,1},{1,2},{2,3},{3,4},{4,5},{5,6},{6,7},{8,9},{9,10},{10,11},{11... | collective-permute-start | bytes 24584 | tf_op jit(solution)/shard_map/ppermute | solution.py:22
  140.6 3.4 fusion.67
  143.9 19.4 %psum.133 = f32[1024]{0:T(1024)S(1)} all-reduce(f32[1024]{0:T(1024)S(1)} %bitcast.129), channel_id=1, replica_groups=mesh['dp'=4,'mp'=8] {'mp'}, use_global_device_ids=true, to_apply=%region_10.11 | all-reduce | flops 1024 | bytes 8192 | tf_op jit(solution)/shard_map/psum | solution.py:70
  163.3 2.8 fusion.68
  166.2 10.1 %psum.134 = f32[2,2048]{1,0:T(2,128)S(1)} all-reduce(f32[2,2048]{1,0:T(2,128)S(1)} %pad_maximum_fusion.12), channel_id=1, replica_groups=mesh['dp'=4,'mp'=8] {'dp'}, use_global_device_ids=true, to_apply=%region_11.12 | all-reduce | flops 4096 | bytes 32768 | tf_op jit(solution)/shard_map/psum | solution.py:79
  176.5 0.6 multiply_reduce_fusion.4
  177.1 17.7 %psum.135 = f32[]{:T(128)} all-reduce(f32[]{:T(128)} %multiply_reduce_fusion.4), channel_id=1, replica_groups=mesh['dp'=4,'mp'=8] {'mp'}, use_global_device_ids=true, to_apply=%region_13.14 | all-reduce | flops 1 | bytes 8 | tf_op jit(solution)/shard_map/psum | solution.py:91
  196.2 0.6 multiply_reduce_fusion.3
  196.8 19.8 %psum.136 = f32[]{:T(128)} all-reduce(f32[]{:T(128)} %get-tuple-element.15), channel_id=1, replica_groups=mesh['dp'=4,'mp'=8] {'mp'}, use_global_device_ids=true, to_apply=%region_15.16 | all-reduce | flops 1 | bytes 8 | tf_op jit(solution)/shard_map/psum | solution.py:56
  218.2 1.3 collective-permute-start.6
  219.5 4.5 %collective-permute-start.7 = (f32[2,1,1024]{2,1,0:T(1,128)S(1)}, f32[2,1,1024]{2,1,0:T(1,128)S(1)}, u32[]{:S(2)}, u32[]{:S(2)}) collective-permute-start(f32[2,1,1024]{2,1,0:T(1,128)S(1)} %get-tuple-element.34), channel_id=1, source_target_pairs={{0,1},{1,2},{2,3},{3,4},{4,5},{5,6},{6,7},{8,9},{9,10},{10,11},{11... | collective-permute-start | bytes 24584 | tf_op jit(solution)/shard_map/ppermute | solution.py:22
  224.0 3.4 fusion.69
  227.4 18.0 %psum.137 = f32[1024]{0:T(1024)S(1)} all-reduce(f32[1024]{0:T(1024)S(1)} %bitcast.130), channel_id=1, replica_groups=mesh['dp'=4,'mp'=8] {'mp'}, use_global_device_ids=true, to_apply=%region_16.17 | all-reduce | flops 1024 | bytes 8192 | tf_op jit(solution)/shard_map/psum | solution.py:70
  245.5 2.8 fusion.70
  248.3 10.1 %psum.138 = f32[2,2048]{1,0:T(2,128)S(1)} all-reduce(f32[2,2048]{1,0:T(2,128)S(1)} %pad_maximum_fusion.13), channel_id=1, replica_groups=mesh['dp'=4,'mp'=8] {'dp'}, use_global_device_ids=true, to_apply=%region_17.18 | all-reduce | flops 4096 | bytes 32768 | tf_op jit(solution)/shard_map/psum | solution.py:79
  258.6 0.6 multiply_reduce_fusion.2
  259.2 18.8 %psum.139 = f32[]{:T(128)} all-reduce(f32[]{:T(128)} %get-tuple-element.11), channel_id=1, replica_groups=mesh['dp'=4,'mp'=8] {'mp'}, use_global_device_ids=true, to_apply=%region_19.20 | all-reduce | flops 1 | bytes 8 | tf_op jit(solution)/shard_map/psum | solution.py:91
  279.4 0.6 multiply_reduce_fusion.1
  280.1 18.7 %psum.140 = f32[]{:T(128)} all-reduce(f32[]{:T(128)} %get-tuple-element.8), channel_id=1, replica_groups=mesh['dp'=4,'mp'=8] {'mp'}, use_global_device_ids=true, to_apply=%region_21.22 | all-reduce | flops 1 | bytes 8 | tf_op jit(solution)/shard_map/psum | solution.py:56
  300.3 1.3 collective-permute-start.8
  301.6 4.5 %collective-permute-start.9 = (f32[2,1,1024]{2,1,0:T(1,128)S(1)}, f32[2,1,1024]{2,1,0:T(1,128)S(1)}, u32[]{:S(2)}, u32[]{:S(2)}) collective-permute-start(f32[2,1,1024]{2,1,0:T(1,128)S(1)} %get-tuple-element.28), channel_id=1, source_target_pairs={{0,1},{1,2},{2,3},{3,4},{4,5},{5,6},{6,7},{8,9},{9,10},{10,11},{11... | collective-permute-start | bytes 24584 | tf_op jit(solution)/shard_map/ppermute | solution.py:22
  306.2 3.4 fusion.71
  309.6 19.1 %psum.141 = f32[1024]{0:T(1024)S(1)} all-reduce(f32[1024]{0:T(1024)S(1)} %bitcast.131), channel_id=1, replica_groups=mesh['dp'=4,'mp'=8] {'mp'}, use_global_device_ids=true, to_apply=%region_22.23 | all-reduce | flops 1024 | bytes 8192 | tf_op jit(solution)/shard_map/psum | solution.py:70
  328.7 2.8 fusion.72
  331.6 10.1 %psum.142 = f32[2,2048]{1,0:T(2,128)S(1)} all-reduce(f32[2,2048]{1,0:T(2,128)S(1)} %pad_maximum_fusion.14), channel_id=1, replica_groups=mesh['dp'=4,'mp'=8] {'dp'}, use_global_device_ids=true, to_apply=%region_23.24 | all-reduce | flops 4096 | bytes 32768 | tf_op jit(solution)/shard_map/psum | solution.py:79
  342.5 17.8 %psum.143 = f32[]{:T(128)} all-reduce(f32[]{:T(128)} %multiply_reduce_fusion), channel_id=1, replica_groups=mesh['dp'=4,'mp'=8] {'mp'}, use_global_device_ids=true, to_apply=%region_25.26 | all-reduce | flops 1 | bytes 8 | tf_op jit(solution)/shard_map/psum | solution.py:91
  361.6 0.6 multiply_add_fusion
  (85 shorter events, 3.2 us)
Async XLA Ops:
  1.4 50.9 %collective-permute-start = (f32[2,1,1024]{2,1,0:T(1,128)S(1)}, f32[2,1,1024]{2,1,0:T(1,128)S(1)}, u32[]{:S(2)}, u32[]{:S(2)}) collective-permute-start(f32[2,1,1024]{2,1,0:T(1,128)S(1)} %get-tuple-element.51), channel_id=1, source_target_pairs={{1,0},{2,1},{3,2},{4,3},{5,4},{6,5},{7,6},{9,8},{10,9},{11,10},{12... | collective-permute-start | bytes 24584 | tf_op jit(solution)/shard_map/ppermute | solution.py:24
  2.7 49.6 %collective-permute-start.1 = (f32[2,1,1024]{2,1,0:T(1,128)S(1)}, f32[2,1,1024]{2,1,0:T(1,128)S(1)}, u32[]{:S(2)}, u32[]{:S(2)}) collective-permute-start(f32[2,1,1024]{2,1,0:T(1,128)S(1)} %get-tuple-element.52), channel_id=1, source_target_pairs={{0,1},{1,2},{2,3},{3,4},{4,5},{5,6},{6,7},{8,9},{9,10},{10,11},{11... | collective-permute-start | bytes 24584 | tf_op jit(solution)/shard_map/ppermute | solution.py:22
  10.0 5.6 %copy-start = (f32[2,2,1024]{2,1,0:T(2,128)S(1)}, f32[2,2,1024]{2,1,0:T(2,128)}, u32[]{:S(2)}) copy-start(f32[2,2,1024]{2,1,0:T(2,128)} %param.9) | copy-start | bytes 49156
  15.6 23.7 %copy-start.2 = (f32[1024]{0:T(1024)S(1)}, f32[1024]{0:T(1024)}, u32[]{:S(2)}) copy-start(f32[1024]{0:T(1024)} %param.8) | copy-start | bytes 12292
  15.6 23.7 %copy-start.4 = (f32[1024]{0:T(1024)S(1)}, f32[1024]{0:T(1024)}, u32[]{:S(2)}) copy-start(f32[1024]{0:T(1024)} %param.7) | copy-start | bytes 12292
  15.6 26.6 %copy-start.3 = (s32[2,2,1024]{2,1,0:T(2,128)S(1)}, s32[2,2,1024]{2,1,0:T(2,128)}, u32[]{:S(2)}) copy-start(s32[2,2,1024]{2,1,0:T(2,128)} %param.11) | copy-start | bytes 49156
  15.7 36.7 %copy-start.1 = (f32[2,1024]{1,0:T(2,128)S(1)}, f32[2,1024]{1,0:T(2,128)}, u32[]{:S(2)}) copy-start(f32[2,1024]{1,0:T(2,128)} %param.10) | copy-start | bytes 24580
  56.2 36.6 %collective-permute-start.2 = (f32[2,1,1024]{2,1,0:T(1,128)S(1)}, f32[2,1,1024]{2,1,0:T(1,128)S(1)}, u32[]{:S(2)}, u32[]{:S(2)}) collective-permute-start(f32[2,1,1024]{2,1,0:T(1,128)S(1)} %get-tuple-element.45), channel_id=1, source_target_pairs={{1,0},{2,1},{3,2},{4,3},{5,4},{6,5},{7,6},{9,8},{10,9},{11,10},{12... | collective-permute-start | bytes 24584 | tf_op jit(solution)/shard_map/ppermute | solution.py:24
  57.5 35.3 %collective-permute-start.3 = (f32[2,1,1024]{2,1,0:T(1,128)S(1)}, f32[2,1,1024]{2,1,0:T(1,128)S(1)}, u32[]{:S(2)}, u32[]{:S(2)}) collective-permute-start(f32[2,1,1024]{2,1,0:T(1,128)S(1)} %get-tuple-element.46), channel_id=1, source_target_pairs={{0,1},{1,2},{2,3},{3,4},{4,5},{5,6},{6,7},{8,9},{9,10},{10,11},{11... | collective-permute-start | bytes 24584 | tf_op jit(solution)/shard_map/ppermute | solution.py:22
  134.7 41.6 %collective-permute-start.4 = (f32[2,1,1024]{2,1,0:T(1,128)S(1)}, f32[2,1,1024]{2,1,0:T(1,128)S(1)}, u32[]{:S(2)}, u32[]{:S(2)}) collective-permute-start(f32[2,1,1024]{2,1,0:T(1,128)S(1)} %get-tuple-element.39), channel_id=1, source_target_pairs={{1,0},{2,1},{3,2},{4,3},{5,4},{6,5},{7,6},{9,8},{10,9},{11,10},{12... | collective-permute-start | bytes 24584 | tf_op jit(solution)/shard_map/ppermute | solution.py:24
  136.0 40.3 %collective-permute-start.5 = (f32[2,1,1024]{2,1,0:T(1,128)S(1)}, f32[2,1,1024]{2,1,0:T(1,128)S(1)}, u32[]{:S(2)}, u32[]{:S(2)}) collective-permute-start(f32[2,1,1024]{2,1,0:T(1,128)S(1)} %get-tuple-element.40), channel_id=1, source_target_pairs={{0,1},{1,2},{2,3},{3,4},{4,5},{5,6},{6,7},{8,9},{9,10},{10,11},{11... | collective-permute-start | bytes 24584 | tf_op jit(solution)/shard_map/ppermute | solution.py:22
  218.2 40.3 %collective-permute-start.6 = (f32[2,1,1024]{2,1,0:T(1,128)S(1)}, f32[2,1,1024]{2,1,0:T(1,128)S(1)}, u32[]{:S(2)}, u32[]{:S(2)}) collective-permute-start(f32[2,1,1024]{2,1,0:T(1,128)S(1)} %get-tuple-element.33), channel_id=1, source_target_pairs={{1,0},{2,1},{3,2},{4,3},{5,4},{6,5},{7,6},{9,8},{10,9},{11,10},{12... | collective-permute-start | bytes 24584 | tf_op jit(solution)/shard_map/ppermute | solution.py:24
  219.5 39.0 %collective-permute-start.7 = (f32[2,1,1024]{2,1,0:T(1,128)S(1)}, f32[2,1,1024]{2,1,0:T(1,128)S(1)}, u32[]{:S(2)}, u32[]{:S(2)}) collective-permute-start(f32[2,1,1024]{2,1,0:T(1,128)S(1)} %get-tuple-element.34), channel_id=1, source_target_pairs={{0,1},{1,2},{2,3},{3,4},{4,5},{5,6},{6,7},{8,9},{9,10},{10,11},{11... | collective-permute-start | bytes 24584 | tf_op jit(solution)/shard_map/ppermute | solution.py:22
  300.3 41.4 %collective-permute-start.8 = (f32[2,1,1024]{2,1,0:T(1,128)S(1)}, f32[2,1,1024]{2,1,0:T(1,128)S(1)}, u32[]{:S(2)}, u32[]{:S(2)}) collective-permute-start(f32[2,1,1024]{2,1,0:T(1,128)S(1)} %get-tuple-element.27), channel_id=1, source_target_pairs={{1,0},{2,1},{3,2},{4,3},{5,4},{6,5},{7,6},{9,8},{10,9},{11,10},{12... | collective-permute-start | bytes 24584 | tf_op jit(solution)/shard_map/ppermute | solution.py:24
  301.6 40.1 %collective-permute-start.9 = (f32[2,1,1024]{2,1,0:T(1,128)S(1)}, f32[2,1,1024]{2,1,0:T(1,128)S(1)}, u32[]{:S(2)}, u32[]{:S(2)}) collective-permute-start(f32[2,1,1024]{2,1,0:T(1,128)S(1)} %get-tuple-element.28), channel_id=1, source_target_pairs={{0,1},{1,2},{2,3},{3,4},{4,5},{5,6},{6,7},{8,9},{9,10},{10,11},{11... | collective-permute-start | bytes 24584 | tf_op jit(solution)/shard_map/ppermute | solution.py:22
where the time goes:
time: 364 us; the launch traced here: 363 us
  blocking collectives  275 us (76%)
  matrix products  31.1 us (9%)
  starting transfers between devices  30.2 us (8%)
  between operations  10.5 us (3%)
  local copies, waits for them, and re-layouts  9.1 us (2%)
  other arithmetic  6.53 us (2%)
    psum x5, blocking collectives, forward(): return lax.psum(partial_rows, 'mp')  94.5 us
    psum x4, blocking collectives, squares(): return lax.psum(jnp.sum(residual * residual), 'mp')  76 us
    psum x3, blocking collectives, local(): curvature = lax.psum(jnp.sum(direction * image), 'mp')  54.4 us
    psum x5, blocking collectives, adjoint(): summed = lax.psum(contrib, 'dp')  50.6 us
    ppermute x5, starting transfers between devices, with_halo(): lax.ppermute(tail, axis, [(i, (i + 1) % count) for i in range(ends)])  23.7 us
    dot_general x5, matrix products, forward(): partial_rows = jnp.dot(matrix, chosen, preferred_element_type=jnp.float32)  16.9 us
    dot_general x5, matrix products, adjoint(): columns = jnp.dot(scaled, matrix, preferred_element_type=jnp.float32)  14.2 us
  transfers between devices with their start and end apart: 10, of which 0 were waited for; matrix products, arithmetic and copies ran while one was open for 10% of the time, Pallas kernels for 0%

commit v1 on v0

v1 whole, which is shorter than its diff:
```python
import jax
import jax.numpy as jnp
from jax import lax
from jax.sharding import PartitionSpec as P

GZ = 16
ITERS = 4


SMOOTHING = 0.25
COUPLING = 0.5
LANES = 128


def inner_sum(field, column_len):
    width = field.shape[-1]
    position = jnp.arange(width) % column_len
    blank_one = jnp.zeros_like(field[..., :1])
    blank_col = jnp.zeros_like(field[..., :column_len])
    later = jnp.where(
        position != column_len - 1, jnp.concatenate([field[..., 1:], blank_one], -1), 0.0
    )
    earlier = jnp.where(position != 0, jnp.concatenate([blank_one, field[..., :-1]], -1), 0.0)
    ahead = jnp.concatenate([field[..., column_len:], blank_col], -1)
    behind = jnp.concatenate([blank_col, field[..., :-column_len]], -1)
    return later + earlier + ahead + behind


def operate_inner(field, smooth_weight):
    padded = jnp.pad(field, ((0, 0), (1, 1), (0, 0)))
    beside = padded[:, 2:] + padded[:, :-2] + inner_sum(field, GZ)
    return (
        smooth_weight * field
        + SMOOTHING * (6.0 * field - beside)
        + COUPLING * (field - field[::-1])
    )


def tree_sum(parts):
    while len(parts) > 1:
        parts = [parts[i] + parts[i + 1] for i in range(0, len(parts), 2)]
    return parts[0]


def local(sensitivity, observed, row_weight, model, smooth_weight, active):
    rows = sensitivity.shape[0]
    matrix = sensitivity.reshape(rows, -1)
    cells = matrix.shape[1]
    width = model.shape[2]
    rank = lax.axis_index("mp")
    owners = lax.axis_size("mp")
    block = lax.axis_index("dp")
    blocks = lax.axis_size("dp")
    split = blocks * 3 // 4
    gravity_rows = block < split
    free_mask = 1.0 - active.astype(jnp.float32)

    def exchange_rows(field, scalars):
        flattened = field.reshape(2, -1)
        chosen = jnp.where(gravity_rows, flattened[0], flattened[1]).astype(jnp.bfloat16)
        partial_rows = jnp.dot(matrix, chosen, preferred_element_type=jnp.float32)
        tail = jnp.stack(scalars) if scalars else jnp.zeros((0,), jnp.float32)
        message = jnp.concatenate(
            [
                partial_rows,
                field[:, 0].reshape(-1),
                field[:, -1].reshape(-1),
                tail,
                jnp.zeros((LANES - tail.shape[0],), jnp.float32),
            ]
        )
        sent = jnp.broadcast_to(message, (owners,) + message.shape)
        got = lax.all_to_all(sent, "mp", 0, 0, tiled=True)
        total = got[:, :rows].sum(0)
        first = got[:, rows : rows + 2 * width].reshape(owners, 2, width)
        last = got[:, rows + 2 * width : rows + 4 * width].reshape(owners, 2, width)
        sums = got[:, rows + 4 * width :].sum(0)
        below = jnp.where(rank > 0, lax.dynamic_index_in_dim(last, jnp.maximum(rank - 1, 0), 0, False), 0.0)
        above = jnp.where(
            rank < owners - 1,
            lax.dynamic_index_in_dim(first, jnp.minimum(rank + 1, owners - 1), 0, False),
            0.0,
        )
        cross = -2.0 * SMOOTHING * jnp.sum(last[:-1] * first[1:])
        return total, below, above, cross, sums

    def exchange_cells(values):
        scaled = (row_weight * values).astype(jnp.bfloat16)
        columns = jnp.dot(scaled, matrix, preferred_element_type=jnp.float32)
        weighed = jnp.sum(values * scaled.astype(jnp.float32))
        message = jnp.concatenate([columns, jnp.broadcast_to(weighed, (LANES,))])
        parts = [message] + [
            lax.ppermute(message, "dp", [(i, i ^ s) for i in range(blocks)])
            for s in range(1, blocks)
        ]
        gravity = [(block ^ s) < split for s in range(blocks)]
        density = tree_sum([jnp.where(g, p[:cells], 0.0) for g, p in zip(gravity, parts)])
        susceptibility = tree_sum([jnp.where(g, 0.0, p[:cells]) for g, p in zip(gravity, parts)])
        summed = jnp.stack([density, susceptibility]).reshape(model.shape)
        return summed, tree_sum([p[cells] for p in parts])

    def finish(inner, below, above):
        inner = inner.at[:, 0].add(-SMOOTHING * below)
        return inner.at[:, -1].add(-SMOOTHING * above)

    inner = operate_inner(model, smooth_weight)
    predicted, below, above, _, _ = exchange_rows(model, [])
    summed, _ = exchange_cells(predicted - observed)
    residual = -free_mask * (summed + finish(inner, below, above))

    direction = jnp.zeros_like(residual)
    imaged = jnp.zeros_like(residual)
    solution = jnp.zeros_like(residual)
    norm_before = None
    curvature = None
    for step in range(ITERS):
        inner = operate_inner(residual, smooth_weight)
        scalars = [
            jnp.sum(residual * residual),
            jnp.sum(residual * inner),
            jnp.sum(residual * imaged),
        ]
        projected, below, above, cross, sums = exchange_rows(residual, scalars)
        summed, weighed = exchange_cells(projected)
        image = free_mask * (summed + finish(inner, below, above))
        norm_now = sums[0]
        own = weighed + sums[1] + cross
        if step:
            ratio = norm_now / norm_before
            curvature = own + ratio * (2.0 * sums[2] + ratio * curvature)
            direction = residual + ratio * direction
            imaged = image + ratio * imaged
        else:
            curvature = own
            direction = residual
            imaged = image
        step_len = norm_now / curvature
        solution = solution + step_len * direction
        residual = residual - step_len * imaged
        norm_before = norm_now
    return (solution, residual)


def solution(mesh):
    return jax.shard_map(
        local,
        mesh=mesh,
        in_specs=(
            P("dp", "mp", None),
            P("dp"),
            P("dp"),
            P(None, "mp", None),
            P("mp", None),
            P(None, "mp", None),
        ),
        out_specs=(P(None, "mp", None), P(None, "mp", None)),
        check_vma=False,
    )
```

time: 364 us -> 164 us (0.45)
  blocking collectives: 275 us -> 42.5 us
  local copies, waits for them, and re-layouts: 9.1 us -> 29.4 us
  between operations: 10.5 us -> 24.8 us
  starting transfers between devices: 30.2 us -> 16.9 us
  waiting for transfers between devices: 0.03 us -> 9.03 us
  other arithmetic: 6.53 us -> 10.8 us
    psum x17 -> x0, blocking collectives: 275 us -> none  [the longest x5 94.5 us: forward(): return lax.psum(partial_rows, 'mp')]
    all_to_all x0 -> x4, blocking collectives: none -> 42.5 us  [exchange_rows(): got = lax.all_to_all(sent, 'mp', 0, 0, tiled=True)]
    ppermute x10 -> x15, starting transfers between devices: 30.2 us -> 9.59 us  [exchange_cells(): lax.ppermute(message, 'dp', [(i, i ^ s) for i in range(blocks)])]
    concatenate x0 -> x9, local copies, waits for them, and re-layouts: none -> 11.2 us  [the longest x4 7.88 us: exchange_rows(): jnp.concatenate([partial_rows, field[:, 0].reshape(-1), field[:, -1].resh...]
    slice x5 -> x26, local copies, waits for them, and re-layouts: 0.87 us -> 9.64 us  [the longest x12 6.25 us: exchange_cells(): return (summed, tree_sum([p[cells] for p in parts]))]
    all_to_all x0 -> x1, starting transfers between devices: none -> 7.31 us  [exchange_rows(): got = lax.all_to_all(sent, 'mp', 0, 0, tiled=True)]
    all_to_all x0 -> x1, waiting for transfers between devices: none -> 7.28 us  [exchange_rows(): got = lax.all_to_all(sent, 'mp', 0, 0, tiled=True)]
    reduce_sum x7 -> x22, other arithmetic: 4.38 us -> 8.82 us  [the longest x5 3.17 us: exchange_cells(): weighed = jnp.sum(values * scaled.astype(jnp.float32))]
  transfers between devices with their start and end apart: 10 -> 16, of which waited for: 0 -> 3; matrix products, arithmetic and copies ran while one was open for 10% -> 5% of each run, Pallas kernels for 0% -> 0%
where the time goes in v1:
time: 164 us; the launch traced here: 162 us
  blocking collectives  42.5 us (26%)
  local copies, waits for them, and re-layouts  29.4 us (18%)
  matrix products  28.8 us (18%)
  between operations  24.8 us (15%)
  starting transfers between devices  16.9 us (10%)
  other arithmetic  10.8 us (7%)
  waiting for transfers between devices  9.03 us (6%)
    all_to_all x4, blocking collectives, exchange_rows(): got = lax.all_to_all(sent, 'mp', 0, 0, tiled=True)  42.5 us
    dot_general x5, matrix products, exchange_rows(): partial_rows = jnp.dot(matrix, chosen, preferred_element_type=jnp.float32)  14.6 us
    dot_general x5, matrix products, exchange_cells(): columns = jnp.dot(scaled, matrix, preferred_element_type=jnp.float32)  14.2 us
    ppermute x15, starting transfers between devices, exchange_cells(): lax.ppermute(message, 'dp', [(i, i ^ s) for i in range(blocks)])  9.59 us
    concatenate x4, local copies, waits for them, and re-layouts, exchange_rows(): jnp.concatenate([partial_rows, field[:, 0].reshape(-1), field[:, -1].resh...  7.88 us
    all_to_all x1, starting transfers between devices, exchange_rows(): got = lax.all_to_all(sent, 'mp', 0, 0, tiled=True)  7.31 us
    all_to_all x1, waiting for transfers between devices, exchange_rows(): got = lax.all_to_all(sent, 'mp', 0, 0, tiled=True)  7.28 us
    slice x12, local copies, waits for them, and re-layouts, exchange_cells(): return (summed, tree_sum([p[cells] for p in parts]))  6.25 us
  transfers between devices with their start and end apart: 16, of which 3 were waited for; matrix products, arithmetic and copies ran while one was open for 5% of the time, Pallas kernels for 0%

profile of v1, /device:TPU:0, one launch (start us, length us, event | category | flops | bytes accessed | tf_op | source)
XLA Modules:
  0.0 162.2 jit_solution(18071046874843764517)
XLA Ops:
  0.6 0.8 fusion.107
  1.5 0.7 fusion.77
  2.2 3.6 %copy.14 = bf16[128,8,2,1024]{3,1,2,0:T(8,128)(2,1)S(1)} copy(bf16[128,8,2,1024]{3,2,1,0:T(2,128)(2,1)} %bitcast.168) | data formatting | bytes 8388608
  5.9 1.9 %copy-done = bf16[128,8,2,1024]{3,1,2,0:T(8,128)(2,1)} copy-done((bf16[128,8,2,1024]{3,1,2,0:T(8,128)(2,1)}, bf16[128,8,2,1024]{3,1,2,0:T(8,128)(2,1)S(1)}, u32[]{:S(2)}) %copy-start) | copy-done | bytes 4194328
  7.7 1.2 fusion.114
  8.9 0.8 broadcast_in_dim.131
  9.7 7.3 %all-to-all-start = ((f32[8,1,5248]{2,1,0:T(1,128)}), f32[8,1,5248]{2,1,0:T(1,128)S(1)}, u32[]{:S(2)}, u32[]{:S(2)}) async-start(f32[8,1,5248]{2,1,0:T(1,128)} %broadcast_in_dim.131), calls=%async_computation | async-start | bytes 335872 | tf_op jit(solution)/shard_map/all_to_all | solution.py:73
  17.3 7.3 %all-to-all-done = f32[8,1,5248]{2,1,0:T(1,128)S(1)} async-done(((f32[8,1,5248]{2,1,0:T(1,128)}), f32[8,1,5248]{2,1,0:T(1,128)S(1)}, u32[]{:S(2)}, u32[]{:S(2)}) %all-to-all-start) | async-done | bytes 167968 | tf_op jit(solution)/shard_map/all_to_all | solution.py:73
  25.3 2.8 %fusion.115 = f32[1,2048]{1,0:T(1,128)S(1)} fusion(bf16[1024,1]{0,1:T(2,128)(2,1)S(1)} %reshape.558, bf16[1024,2048]{1,0:T(8,128)(2,1)} %bitcast.159), kind=kOutput, calls=%fused_computation.201 | convolution fusion | flops 4194304 | bytes 4204544 | tf_op jit(solution)/shard_map/dot_general | solution.py:89
  28.1 0.7 concatenate.116
  28.9 1.6 collective-permute-start.1
  30.9 1.1 collective-permute-done.2
  32.9 3.4 %fusion.116 = f32[1,1024]{1,0:T(1,128)S(1)} fusion(bf16[2048,1]{0,1:T(2,128)(2,1)S(1)} %bitcast.208, bf16[1024,2048]{1,0:T(8,128)(2,1)} %bitcast.160), kind=kOutput, calls=%fused_computation.202 | convolution fusion | flops 4194304 | bytes 4202496 | tf_op jit(solution)/shard_map/dot_general | solution.py:61
  36.3 0.7 multiply_reduce_fusion.9
  37.0 2.0 %concatenate.125 = f32[5248]{0:T(1024)S(1)} concatenate(f32[1024]{0:T(1024)S(1)} %bitcast.223, f32[2048]{0:T(1024)S(1)} %bitcast.215, f32[2048]{0:T(1024)S(1)} %bitcast.214, f32[1]{0:T(128)} %bitcast.11, f32[1]{0:T(128)} %bitcast.12, f32[1]{0:T(128)} %bitcast.13, f32[125]{0:T(128)S(1)} %broadcast.433), dimensions={0} | concatenate | bytes 41984 | tf_op jit(solution)/shard_map/concatenate | solution.py:63
  39.1 11.1 %all_to_all.45 = f32[8,1,5248]{2,1,0:T(1,128)S(1)} all-to-all(f32[8,1,5248]{2,1,0:T(1,128)S(1)} %broadcast_in_dim.137), channel_id=1, replica_groups=mesh['dp'=4,'mp'=8] {'mp'}, dimensions={0} | all-to-all | bytes 335872 | tf_op jit(solution)/shard_map/all_to_all | solution.py:73
  50.3 0.6 fusion.3
  51.6 2.8 %fusion.117 = f32[1,2048]{1,0:T(1,128)S(1)} fusion(bf16[1024,1]{0,1:T(2,128)(2,1)S(1)} %reshape.562, bf16[1024,2048]{1,0:T(8,128)(2,1)} %bitcast.161), kind=kOutput, calls=%fused_computation.203 | convolution fusion | flops 4194304 | bytes 4204544 | tf_op jit(solution)/shard_map/dot_general | solution.py:89
  55.1 0.7 collective-permute-start.4
  55.8 1.1 collective-permute-start.3
  64.1 3.4 %fusion.118 = f32[1,1024]{1,0:T(1,128)S(1)} fusion(bf16[2048,1]{0,1:T(2,128)(2,1)S(1)} %bitcast.209, bf16[1024,2048]{1,0:T(8,128)(2,1)} %bitcast.162), kind=kOutput, calls=%fused_computation.204 | convolution fusion | flops 4194304 | bytes 4202496 | tf_op jit(solution)/shard_map/dot_general | solution.py:61
  67.4 0.8 multiply_reduce_fusion.6
  68.2 1.9 %concatenate.131 = f32[5248]{0:T(1024)S(1)} concatenate(f32[1024]{0:T(1024)S(1)} %bitcast.224, f32[2048]{0:T(1024)S(1)} %bitcast.217, f32[2048]{0:T(1024)S(1)} %bitcast.216, f32[1]{0:T(128)} %bitcast.26, f32[1]{0:T(128)} %bitcast.27, f32[1]{0:T(128)} %bitcast.28, f32[125]{0:T(128)S(1)} %broadcast.433), dimensions={0} | concatenate | bytes 41984 | tf_op jit(solution)/shard_map/concatenate | solution.py:63
  70.2 10.4 %all_to_all.46 = f32[8,1,5248]{2,1,0:T(1,128)S(1)} all-to-all(f32[8,1,5248]{2,1,0:T(1,128)S(1)} %broadcast_in_dim.138), channel_id=1, replica_groups=mesh['dp'=4,'mp'=8] {'mp'}, dimensions={0} | all-to-all | bytes 335872 | tf_op jit(solution)/shard_map/all_to_all | solution.py:73
  81.4 0.7 multiply_reduce_fusion.14
  82.0 2.8 %fusion.119 = f32[1,2048]{1,0:T(1,128)S(1)} fusion(bf16[1024,1]{0,1:T(2,128)(2,1)S(1)} %reshape.566, bf16[1024,2048]{1,0:T(8,128)(2,1)} %bitcast.163), kind=kOutput, calls=%fused_computation.205 | convolution fusion | flops 4194304 | bytes 4204544 | tf_op jit(solution)/shard_map/dot_general | solution.py:89
  84.9 0.7 concatenate.132
  85.7 0.8 collective-permute-start.7
  86.5 1.0 collective-permute-start.6
  96.6 3.4 %fusion.120 = f32[1,1024]{1,0:T(1,128)S(1)} fusion(bf16[2048,1]{0,1:T(2,128)(2,1)S(1)} %bitcast.210, bf16[1024,2048]{1,0:T(8,128)(2,1)} %bitcast.164), kind=kOutput, calls=%fused_computation.206 | convolution fusion | flops 4194304 | bytes 4202496 | tf_op jit(solution)/shard_map/dot_general | solution.py:61
  100.0 0.7 multiply_reduce_fusion.3
  100.7 2.0 %concatenate.137 = f32[5248]{0:T(1024)S(1)} concatenate(f32[1024]{0:T(1024)S(1)} %bitcast.225, f32[2048]{0:T(1024)S(1)} %bitcast.219, f32[2048]{0:T(1024)S(1)} %bitcast.218, f32[1]{0:T(128)} %bitcast.42, f32[1]{0:T(128)} %bitcast.43, f32[1]{0:T(128)} %bitcast.44, f32[125]{0:T(128)S(1)} %broadcast.433), dimensions={0} | concatenate | bytes 41984 | tf_op jit(solution)/shard_map/concatenate | solution.py:63
  102.8 10.5 %all_to_all.47 = f32[8,1,5248]{2,1,0:T(1,128)S(1)} all-to-all(f32[8,1,5248]{2,1,0:T(1,128)S(1)} %broadcast_in_dim.139), channel_id=1, replica_groups=mesh['dp'=4,'mp'=8] {'mp'}, dimensions={0} | all-to-all | bytes 335872 | tf_op jit(solution)/shard_map/all_to_all | solution.py:73
  113.9 0.7 multiply_reduce_fusion.13
  114.6 2.8 %fusion.121 = f32[1,2048]{1,0:T(1,128)S(1)} fusion(bf16[1024,1]{0,1:T(2,128)(2,1)S(1)} %reshape.570, bf16[1024,2048]{1,0:T(8,128)(2,1)} %bitcast.165), kind=kOutput, calls=%fused_computation.207 | convolution fusion | flops 4194304 | bytes 4204544 | tf_op jit(solution)/shard_map/dot_general | solution.py:89
  117.5 0.7 concatenate.138
  118.2 0.8 collective-permute-start.10
  119.1 1.0 collective-permute-start.9
  129.3 3.4 %fusion.122 = f32[1,1024]{1,0:T(1,128)S(1)} fusion(bf16[2048,1]{0,1:T(2,128)(2,1)S(1)} %bitcast.211, bf16[1024,2048]{1,0:T(8,128)(2,1)} %bitcast.166), kind=kOutput, calls=%fused_computation.208 | convolution fusion | flops 4194304 | bytes 4202496 | tf_op jit(solution)/shard_map/dot_general | solution.py:61
  132.7 0.8 multiply_reduce_fusion
  133.5 2.0 %concatenate.143 = f32[5248]{0:T(1024)S(1)} concatenate(f32[1024]{0:T(1024)S(1)} %bitcast.222, f32[2048]{0:T(1024)S(1)} %bitcast.213, f32[2048]{0:T(1024)S(1)} %bitcast.212, f32[1]{0:T(128)} %bitcast.58, f32[1]{0:T(128)} %bitcast.59, f32[1]{0:T(128)} %bitcast.60, f32[125]{0:T(128)S(1)} %broadcast.433), dimensions={0} | concatenate | bytes 41984 | tf_op jit(solution)/shard_map/concatenate | solution.py:63
  135.5 10.5 %all_to_all.48 = f32[8,1,5248]{2,1,0:T(1,128)S(1)} all-to-all(f32[8,1,5248]{2,1,0:T(1,128)S(1)} %broadcast_in_dim.140), channel_id=1, replica_groups=mesh['dp'=4,'mp'=8] {'mp'}, dimensions={0} | all-to-all | bytes 335872 | tf_op jit(solution)/shard_map/all_to_all | solution.py:73
  147.3 2.8 %fusion.123 = f32[1,2048]{1,0:T(1,128)S(1)} fusion(bf16[1024,1]{0,1:T(2,128)(2,1)S(1)} %reshape.574, bf16[1024,2048]{1,0:T(8,128)(2,1)} %bitcast.167), kind=kOutput, calls=%fused_computation.209 | convolution fusion | flops 4194304 | bytes 4204544 | tf_op jit(solution)/shard_map/dot_general | solution.py:89
  150.2 0.7 concatenate.144
  150.9 0.8 collective-permute-start.13
  151.7 1.0 collective-permute-start.12
  152.9 0.7 fusion.110
  161.6 0.7 fusion.38
  (148 shorter events, 16.7 us)
Async XLA Ops:
  5.8 1.9 %copy-start = (bf16[128,8,2,1024]{3,1,2,0:T(8,128)(2,1)}, bf16[128,8,2,1024]{3,1,2,0:T(8,128)(2,1)S(1)}, u32[]{:S(2)}) copy-start(bf16[128,8,2,1024]{3,1,2,0:T(8,128)(2,1)S(1)} %copy.14) | copy-start | bytes 12582916
  5.8 11.2 %copy-start.1 = (f32[2,2,1024]{2,1,0:T(2,128)S(1)}, f32[2,2,1024]{2,1,0:T(2,128)}, u32[]{:S(2)}) copy-start(f32[2,2,1024]{2,1,0:T(2,128)} %param.29) | copy-start | bytes 49156
  5.8 11.3 %copy-start.3 = (f32[2,1024]{1,0:T(2,128)S(1)}, f32[2,1024]{1,0:T(2,128)}, u32[]{:S(2)}) copy-start(f32[2,1024]{1,0:T(2,128)} %param.30) | copy-start | bytes 24580
  5.8 18.8 %copy-start.4 = (f32[1024]{0:T(1024)S(1)}, f32[1024]{0:T(1024)}, u32[]{:S(2)}) copy-start(f32[1024]{0:T(1024)} %param.28) | copy-start | bytes 12292
  5.9 18.8 %copy-start.5 = (f32[1024]{0:T(1024)S(1)}, f32[1024]{0:T(1024)}, u32[]{:S(2)}) copy-start(f32[1024]{0:T(1024)} %param.27) | copy-start | bytes 12292
  7.7 24.9 %copy-start.2 = (s32[2,2,1024]{2,1,0:T(2,128)S(1)}, s32[2,2,1024]{2,1,0:T(2,128)}, u32[]{:S(2)}) copy-start(s32[2,2,1024]{2,1,0:T(2,128)} %param.31) | copy-start | bytes 49156
  9.7 14.9 %all-to-all-start = ((f32[8,1,5248]{2,1,0:T(1,128)}), f32[8,1,5248]{2,1,0:T(1,128)S(1)}, u32[]{:S(2)}, u32[]{:S(2)}) async-start(f32[8,1,5248]{2,1,0:T(1,128)} %broadcast_in_dim.131), calls=%async_computation | async-start | bytes 335872 | tf_op jit(solution)/shard_map/all_to_all | solution.py:73
  28.8 3.3 %collective-permute-start.2 = (f32[2176]{0:T(1024)S(1)}, f32[2176]{0:T(1024)S(1)}, u32[]{:S(2)}, u32[]{:S(2)}) collective-permute-start(f32[2176]{0:T(1024)S(1)} %concatenate.116), channel_id=1, source_target_pairs={{0,24},{8,16},{16,8},{24,0},{1,25},{9,17},{17,9},{25,1},{2,26},{10... | collective-permute-start | bytes 26120 | tf_op jit(solution)/shard_map/ppermute | solution.py:93
  28.9 3.8 %collective-permute-start.1 = (f32[2176]{0:T(1024)S(1)}, f32[2176]{0:T(1024)S(1)}, u32[]{:S(2)}, u32[]{:S(2)}) collective-permute-start(f32[2176]{0:T(1024)S(1)} %concatenate.116), channel_id=1, source_target_pairs={{0,16},{8,24},{16,0},{24,8},{1,17},{9,25},{17,1},{25,9},{2,18},{10... | collective-permute-start | bytes 26120 | tf_op jit(solution)/shard_map/ppermute | solution.py:93
  30.4 2.2 %collective-permute-start = (f32[2176]{0:T(1024)S(1)}, f32[2176]{0:T(1024)S(1)}, u32[]{:S(2)}, u32[]{:S(2)}) collective-permute-start(f32[2176]{0:T(1024)S(1)} %concatenate.116), channel_id=1, source_target_pairs={{0,8},{8,0},{16,24},{24,16},{1,9},{9,1},{17,25},{25,17},{2,10},{10... | collective-permute-start | bytes 26120 | tf_op jit(solution)/shard_map/ppermute | solution.py:93
  55.0 5.1 %collective-permute-start.5 = (f32[2176]{0:T(1024)S(1)}, f32[2176]{0:T(1024)S(1)}, u32[]{:S(2)}, u32[]{:S(2)}) collective-permute-start(f32[2176]{0:T(1024)S(1)} %concatenate.126), channel_id=1, source_target_pairs={{0,24},{8,16},{16,8},{24,0},{1,25},{9,17},{17,9},{25,1},{2,26},{10... | collective-permute-start | bytes 26120 | tf_op jit(solution)/shard_map/ppermute | solution.py:93
  55.1 5.0 %collective-permute-start.4 = (f32[2176]{0:T(1024)S(1)}, f32[2176]{0:T(1024)S(1)}, u32[]{:S(2)}, u32[]{:S(2)}) collective-permute-start(f32[2176]{0:T(1024)S(1)} %concatenate.126), channel_id=1, source_target_pairs={{0,16},{8,24},{16,0},{24,8},{1,17},{9,25},{17,1},{25,9},{2,18},{10... | collective-permute-start | bytes 26120 | tf_op jit(solution)/shard_map/ppermute | solution.py:93
  55.8 2.5 %collective-permute-start.3 = (f32[2176]{0:T(1024)S(1)}, f32[2176]{0:T(1024)S(1)}, u32[]{:S(2)}, u32[]{:S(2)}) collective-permute-start(f32[2176]{0:T(1024)S(1)} %concatenate.126), channel_id=1, source_target_pairs={{0,8},{8,0},{16,24},{24,16},{1,9},{9,1},{17,25},{25,17},{2,10},{10... | collective-permute-start | bytes 26120 | tf_op jit(solution)/shard_map/ppermute | solution.py:93
  85.6 7.1 %collective-permute-start.8 = (f32[2176]{0:T(1024)S(1)}, f32[2176]{0:T(1024)S(1)}, u32[]{:S(2)}, u32[]{:S(2)}) collective-permute-start(f32[2176]{0:T(1024)S(1)} %concatenate.132), channel_id=1, source_target_pairs={{0,24},{8,16},{16,8},{24,0},{1,25},{9,17},{17,9},{25,1},{2,26},{10... | collective-permute-start | bytes 26120 | tf_op jit(solution)/shard_map/ppermute | solution.py:93
  85.7 7.6 %collective-permute-start.7 = (f32[2176]{0:T(1024)S(1)}, f32[2176]{0:T(1024)S(1)}, u32[]{:S(2)}, u32[]{:S(2)}) collective-permute-start(f32[2176]{0:T(1024)S(1)} %concatenate.132), channel_id=1, source_target_pairs={{0,16},{8,24},{16,0},{24,8},{1,17},{9,25},{17,1},{25,9},{2,18},{10... | collective-permute-start | bytes 26120 | tf_op jit(solution)/shard_map/ppermute | solution.py:93
  86.5 4.4 %collective-permute-start.6 = (f32[2176]{0:T(1024)S(1)}, f32[2176]{0:T(1024)S(1)}, u32[]{:S(2)}, u32[]{:S(2)}) collective-permute-start(f32[2176]{0:T(1024)S(1)} %concatenate.132), channel_id=1, source_target_pairs={{0,8},{8,0},{16,24},{24,16},{1,9},{9,1},{17,25},{25,17},{2,10},{10... | collective-permute-start | bytes 26120 | tf_op jit(solution)/shard_map/ppermute | solution.py:93
  118.2 7.3 %collective-permute-start.11 = (f32[2176]{0:T(1024)S(1)}, f32[2176]{0:T(1024)S(1)}, u32[]{:S(2)}, u32[]{:S(2)}) collective-permute-start(f32[2176]{0:T(1024)S(1)} %concatenate.138), channel_id=1, source_target_pairs={{0,24},{8,16},{16,8},{24,0},{1,25},{9,17},{17,9},{25,1},{2,26},{10... | collective-permute-start | bytes 26120 | tf_op jit(solution)/shard_map/ppermute | solution.py:93
  118.2 7.7 %collective-permute-start.10 = (f32[2176]{0:T(1024)S(1)}, f32[2176]{0:T(1024)S(1)}, u32[]{:S(2)}, u32[]{:S(2)}) collective-permute-start(f32[2176]{0:T(1024)S(1)} %concatenate.138), channel_id=1, source_target_pairs={{0,16},{8,24},{16,0},{24,8},{1,17},{9,25},{17,1},{25,9},{2,18},{10... | collective-permute-start | bytes 26120 | tf_op jit(solution)/shard_map/ppermute | solution.py:93
  119.1 4.5 %collective-permute-start.9 = (f32[2176]{0:T(1024)S(1)}, f32[2176]{0:T(1024)S(1)}, u32[]{:S(2)}, u32[]{:S(2)}) collective-permute-start(f32[2176]{0:T(1024)S(1)} %concatenate.138), channel_id=1, source_target_pairs={{0,8},{8,0},{16,24},{24,16},{1,9},{9,1},{17,25},{25,17},{2,10},{10... | collective-permute-start | bytes 26120 | tf_op jit(solution)/shard_map/ppermute | solution.py:93
  150.8 7.1 %collective-permute-start.14 = (f32[2176]{0:T(1024)S(1)}, f32[2176]{0:T(1024)S(1)}, u32[]{:S(2)}, u32[]{:S(2)}) collective-permute-start(f32[2176]{0:T(1024)S(1)} %concatenate.144), channel_id=1, source_target_pairs={{0,24},{8,16},{16,8},{24,0},{1,25},{9,17},{17,9},{25,1},{2,26},{10... | collective-permute-start | bytes 26120 | tf_op jit(solution)/shard_map/ppermute | solution.py:93
  150.9 7.5 %collective-permute-start.13 = (f32[2176]{0:T(1024)S(1)}, f32[2176]{0:T(1024)S(1)}, u32[]{:S(2)}, u32[]{:S(2)}) collective-permute-start(f32[2176]{0:T(1024)S(1)} %concatenate.144), channel_id=1, source_target_pairs={{0,16},{8,24},{16,0},{24,8},{1,17},{9,25},{17,1},{25,9},{2,18},{10... | collective-permute-start | bytes 26120 | tf_op jit(solution)/shard_map/ppermute | solution.py:93
  151.7 4.4 %collective-permute-start.12 = (f32[2176]{0:T(1024)S(1)}, f32[2176]{0:T(1024)S(1)}, u32[]{:S(2)}, u32[]{:S(2)}) collective-permute-start(f32[2176]{0:T(1024)S(1)} %concatenate.144), channel_id=1, source_target_pairs={{0,8},{8,0},{16,24},{24,16},{1,9},{9,1},{17,25},{25,17},{2,10},{10... | collective-permute-start | bytes 26120 | tf_op jit(solution)/shard_map/ppermute | solution.py:93

commit v2 on v0

v2 whole, which is shorter than its diff:
```python
import functools

import jax
import jax.numpy as jnp
from jax import lax
from jax.experimental import pallas as pl
from jax.experimental.pallas import tpu as pltpu
from jax.sharding import PartitionSpec as P

GZ = 16
ITERS = 4


SMOOTHING = 0.25
COUPLING = 0.5
LANES = 128
SUBLANES = 8
KERNEL_VMEM = 16 * 1024 * 1024


def tree_sum(parts):
    while len(parts) > 1:
        parts = [parts[i] + parts[i + 1] for i in range(0, len(parts), 2)]
    return parts[0]


def inner_sum(plane):
    tall = plane.shape[0]
    lane = lax.broadcasted_iota(jnp.int32, plane.shape, 1)
    line = lax.broadcasted_iota(jnp.int32, plane.shape, 0)
    position = lane % GZ
    later = jnp.where(position != GZ - 1, pltpu.roll(plane, LANES - 1, 1), 0.0)
    earlier = jnp.where(position != 0, pltpu.roll(plane, 1, 1), 0.0)
    ahead = pltpu.roll(plane, LANES - GZ, 1)
    over = jnp.where(line < tall - 1, pltpu.roll(ahead, tall - 1, 0), 0.0)
    ahead = jnp.where(lane < LANES - GZ, ahead, over)
    behind = pltpu.roll(plane, GZ, 1)
    under = jnp.where(line > 0, pltpu.roll(behind, 1, 0), 0.0)
    behind = jnp.where(lane >= GZ, behind, under)
    return later + earlier + ahead + behind


def operate_inner(field, smooth_weight):
    layers = len(field[0])
    out = [[], []]
    for f in range(2):
        for i in range(layers):
            own = field[f][i]
            beside = inner_sum(own)
            if i:
                beside = beside + field[f][i - 1]
            if i < layers - 1:
                beside = beside + field[f][i + 1]
            out[f].append(
                smooth_weight[i] * own
                + SMOOTHING * (6.0 * own - beside)
                + COUPLING * (own - field[1 - f][i])
            )
    return out


def load(ref):
    return [[ref[f, i] for i in range(ref.shape[1])] for f in range(2)]


def store(ref, field):
    for f in range(2):
        for i in range(ref.shape[1]):
            ref[f, i] = field[f][i]


def mapped(op, *fields):
    return [[op(*(x[f][i] for x in fields)) for i in range(len(fields[0][0]))] for f in range(2)]


def dot_line(one, two):
    total = None
    for f in range(2):
        for i in range(len(one[0])):
            term = one[f][i] * two[f][i]
            total = term if total is None else total + term
    return jnp.sum(total, axis=0, keepdims=True)


def full(line):
    return jnp.sum(line, axis=1, keepdims=True)


def spread(planes, count):
    return jnp.concatenate(
        [
            jnp.broadcast_to(plane[t : t + 1], (count, LANES))
            for plane in planes
            for t in range(plane.shape[0])
        ],
        axis=1,
    )


def send_rows(place_ref, matrix_ref, field, lines, out_ref):
    owners = out_ref.shape[0]
    rows = matrix_ref.shape[0]
    tall = field[0][0].shape[0]
    gravity_rows = place_ref[1] < place_ref[2]
    chosen = [jnp.where(gravity_rows, d, s) for d, s in zip(field[0], field[1])]
    vector = spread(chosen, LANES).astype(jnp.bfloat16)
    eye = lax.broadcasted_iota(jnp.int32, (LANES, LANES), 0) == lax.broadcasted_iota(
        jnp.int32, (LANES, LANES), 1
    )
    product = lax.dot_general(
        matrix_ref[...], vector, (((1,), (1,)), ((), ())), preferred_element_type=jnp.float32
    )
    pieces = [
        jnp.sum(
            jnp.where(eye, product[b * LANES : (b + 1) * LANES], 0.0), axis=0, keepdims=True
        )
        for b in range(rows // LANES)
    ]
    pieces += [field[0][0], field[1][0], field[0][-1], field[1][-1]]
    pieces += lines
    pieces.append(jnp.zeros((SUBLANES - len(lines), LANES), jnp.float32))
    message = jnp.concatenate(pieces, axis=0)
    for j in range(owners):
        out_ref[j] = message


def start_kernel(place_ref, matrix_ref, model_ref, out_ref):
    send_rows(place_ref, matrix_ref, load(model_ref), [], out_ref)


def rows_kernel(matrix_ref, got_ref, weight_ref, observed_ref, out_ref, *, subtract):
    owners = got_ref.shape[0]
    rows, cells = matrix_ref.shape
    blocks = rows // LANES
    values = got_ref[0, 0:blocks]
    for j in range(1, owners):
        values = values + got_ref[j, 0:blocks]
    if subtract:
        values = values - observed_ref[...]
    scaled = (weight_ref[...] * values).astype(jnp.bfloat16).astype(jnp.float32)
    weighed = jnp.sum(values * scaled, axis=0, keepdims=True)
    vector = spread([scaled], 2 * SUBLANES).astype(jnp.bfloat16)
    columns = jnp.dot(vector, matrix_ref[...], preferred_element_type=jnp.float32)
    pieces = [columns[0:1, t * LANES : (t + 1) * LANES] for t in range(cells // LANES)]
    pieces += [weighed, jnp.zeros((SUBLANES - 1, LANES), jnp.float32)]
    out_ref[...] = jnp.concatenate(pieces, axis=0)


def gathered(place_ref, part_refs, got_ref, inner_ref, mask_ref, base):
    rank = place_ref[0]
    owners = got_ref.shape[0]
    layers, tall = inner_ref.shape[1:3]
    cells = layers * tall
    gravity = [(place_ref[1] ^ s) < place_ref[2] for s in range(len(part_refs))]
    parts = [ref[0:cells] for ref in part_refs]
    data = [
        tree_sum([jnp.where(g, p, 0.0) for g, p in zip(gravity, parts)]),
        tree_sum([jnp.where(g, 0.0, p) for g, p in zip(gravity, parts)]),
    ]
    down = jnp.maximum(rank - 1, 0)
    up = jnp.minimum(rank + 1, owners - 1)
    image = [[], []]
    for f in range(2):
        first = base + f * tall
        last = base + (2 + f) * tall
        below = jnp.where(rank > 0, got_ref[down, last : last + tall], 0.0)
        above = jnp.where(rank < owners - 1, got_ref[up, first : first + tall], 0.0)
        for i in range(layers):
            regular = inner_ref[f, i]
            if i == 0:
                regular = regular - SMOOTHING * below
            if i == layers - 1:
                regular = regular - SMOOTHING * above
            image[f].append(mask_ref[f, i] * (data[f][i * tall : (i + 1) * tall] + regular))
    return image


def first_kernel(place_ref, matrix_ref, *refs, count, base):
    part_refs = refs[:count]
    got_ref, model_ref, smooth_ref, mask_ref, out_ref, residual_ref, inner_ref, held = refs[count:]
    layers = model_ref.shape[1]
    smooth_weight = [smooth_ref[i] for i in range(layers)]
    store(held, operate_inner(load(model_ref), smooth_weight))
    image = gathered(place_ref, part_refs, got_ref, held, mask_ref, base)
    residual = mapped(lambda a: -a, image)
    inner = operate_inner(residual, smooth_weight)
    store(residual_ref, residual)
    store(inner_ref, inner)
    lines = [dot_line(residual, residual), dot_line(residual, inner)]
    send_rows(place_ref, matrix_ref, residual, lines, out_ref)


def cells_kernel(place_ref, matrix_ref, *refs, count, base, begin, final):
    part_refs = refs[:count]
    got_ref, smooth_ref, mask_ref, residual_in, inner_in = refs[count : count + 5]
    refs = refs[count + 5 :]
    if not begin:
        direction_in, imaged_in, solution_in, norms_in = refs[:4]
        refs = refs[4:]
    solution_ref, residual_ref = refs[:2]
    owners = got_ref.shape[0]
    layers, tall = inner_in.shape[1:3]
    cells = layers * tall
    residual = load(residual_in)
    image = gathered(place_ref, part_refs, got_ref, inner_in, mask_ref, base)
    at = base + 4 * tall
    sums = got_ref[0, at : at + SUBLANES]
    for j in range(1, owners):
        sums = sums + got_ref[j, at : at + SUBLANES]
    cross = None
    for j in range(owners - 1):
        term = (
            got_ref[j, base + 2 * tall : base + 4 * tall] * got_ref[j + 1, base : base + 2 * tall]
        )
        cross = term if cross is None else cross + term
    weighed = tree_sum([ref[cells : cells + 1] for ref in part_refs])
    line = weighed + sums[1:2]
    line = line - 2.0 * SMOOTHING * jnp.sum(cross, axis=0, keepdims=True)
    norm_now = full(sums[0:1])
    curvature = full(line)
    if begin:
        direction, imaged = residual, image
    else:
        ratio = norm_now / norms_in[0:1, 0:1]
        curvature = curvature + ratio * (2.0 * full(sums[2:3]) + ratio * norms_in[1:2, 0:1])
        direction = mapped(lambda r, d: r + ratio * d, residual, load(direction_in))
        imaged = mapped(lambda r, d: r + ratio * d, image, load(imaged_in))
    step_len = norm_now / curvature
    if begin:
        update = mapped(lambda d: step_len * d, direction)
    else:
        update = mapped(lambda x, d: x + step_len * d, load(solution_in), direction)
    residual = mapped(lambda r, s: r - step_len * s, residual, imaged)
    store(solution_ref, update)
    store(residual_ref, residual)
    if final:
        return
    direction_ref, imaged_ref, norms_ref, inner_ref, out_ref = refs[2:]
    store(direction_ref, direction)
    store(imaged_ref, imaged)
    norms_ref[0:1] = jnp.broadcast_to(norm_now, (1, LANES))
    norms_ref[1:2] = jnp.broadcast_to(curvature, (1, LANES))
    inner = operate_inner(residual, [smooth_ref[i] for i in range(layers)])
    store(inner_ref, inner)
    lines = [dot_line(residual, residual), dot_line(residual, inner), dot_line(residual, imaged)]
    send_rows(place_ref, matrix_ref, residual, lines, out_ref)


def local(sensitivity, observed, row_weight, model, smooth_weight, active):
    rows = sensitivity.shape[0]
    matrix = sensitivity.reshape(rows, -1)
    layers, width = smooth_weight.shape
    tall = width // LANES
    owners = lax.axis_size("mp")
    blocks = lax.axis_size("dp")
    place = jnp.stack(
        [lax.axis_index("mp"), lax.axis_index("dp"), jnp.int32(blocks * 3 // 4)]
    ).astype(jnp.int32)
    base = rows // LANES

    def planes(x):
        return x.reshape(x.shape[:-1] + (tall, LANES))

    mask = planes(1.0 - active.astype(jnp.float32))
    smooth = planes(smooth_weight)
    weight = row_weight.reshape(base, LANES)
    target = observed.reshape(base, LANES)
    start = planes(model)
    matrix = pltpu.with_memory_space_constraint(matrix, pltpu.VMEM)

    cell = jax.ShapeDtypeStruct(start.shape, jnp.float32)
    message = jax.ShapeDtypeStruct(
        (owners, base + 4 * tall + SUBLANES, LANES), jnp.float32
    )
    columns = jax.ShapeDtypeStruct((layers * tall + SUBLANES, LANES), jnp.float32)
    norms = jax.ShapeDtypeStruct((2, LANES), jnp.float32)
    smem = pl.BlockSpec(memory_space=pltpu.SMEM)
    vmem = pl.BlockSpec(memory_space=pltpu.VMEM)

    def call(kernel, out_shape, *operands, name, scratch=(), scalars=True):
        specs = [smem] * scalars + [vmem] * len(operands)
        operands = ((place,) if scalars else ()) + operands
        return pl.pallas_call(
            kernel,
            out_shape=out_shape,
            in_specs=specs,
            out_specs=jax.tree.map(lambda _: vmem, out_shape),
            scratch_shapes=scratch,
            compiler_params=pltpu.CompilerParams(vmem_limit_bytes=KERNEL_VMEM),
            name=name,
        )(*operands)

    def across(sent):
        return lax.all_to_all(sent, "mp", 0, 0, tiled=True)

    def along(got, subtract):
        sent = call(
            functools.partial(rows_kernel, subtract=subtract),
            columns,
            matrix,
            got,
            weight,
            target,
            name="rows",
            scalars=False,
        )
        return [sent] + [
            lax.ppermute(sent, "dp", [(i, i ^ s) for i in range(blocks)])
            for s in range(1, blocks)
        ]

    got = across(call(start_kernel, message, matrix, start, name="start"))
    parts = along(got, True)
    sent, residual, inner = call(
        functools.partial(first_kernel, count=blocks, base=base),
        (message, cell, cell),
        matrix,
        *parts,
        got,
        start,
        smooth,
        mask,
        name="first",
        scratch=[pltpu.VMEM(start.shape, jnp.float32)],
    )
    carried = ()
    for step in range(ITERS):
        got = across(sent)
        parts = along(got, False)
        final = step == ITERS - 1
        outs = (cell, cell) if final else (cell, cell, cell, cell, norms, cell, message)
        result = call(
            functools.partial(
                cells_kernel, count=blocks, base=base, begin=step == 0, final=final
            ),
            outs,
            matrix,
            *parts,
            got,
            smooth,
            mask,
            residual,
            inner,
            *carried,
            name="cells",
        )
        if final:
            update, residual = result
        else:
            update, residual, direction, imaged, scalars, inner, sent = result
            carried = (direction, imaged, update, scalars)
    return (update.reshape(model.shape), residual.reshape(model.shape))


def solution(mesh):
    return jax.shard_map(
        local,
        mesh=mesh,
        in_specs=(
            P("dp", "mp", None),
            P("dp"),
            P("dp"),
            P(None, "mp", None),
            P("mp", None),
            P(None, "mp", None),
        ),
        out_specs=(P(None, "mp", None), P(None, "mp", None)),
        check_vma=False,
    )
```

time: 364 us -> 102 us (0.28)
  blocking collectives: 275 us -> 60.4 us
  matrix products: 31.1 us -> 0 us
  starting transfers between devices: 30.2 us -> 9.37 us
  Pallas kernels: 0 us -> 13.4 us
  between operations: 10.5 us -> 0.75 us
  waiting for transfers between devices: 0.03 us -> 9.3 us
  other arithmetic: 6.53 us -> 0.09 us
    psum x17 -> x0, blocking collectives: 275 us -> none  [the longest x5 94.5 us: forward(): return lax.psum(partial_rows, 'mp')]
    all_to_all x0 -> x5, blocking collectives: none -> 60.4 us  [across(): return lax.all_to_all(sent, 'mp', 0, 0, tiled=True)]
    dot_general x10 -> x0, matrix products: 31.1 us -> none  [the longest x5 16.9 us: forward(): partial_rows = jnp.dot(matrix, chosen, preferred_element_type=jnp.float32)]
    ppermute x10 -> x15, starting transfers between devices: 30.2 us -> 9.37 us  [along(): lax.ppermute(sent, 'dp', [(i, i ^ s) for i in range(blocks)])]
    pallas_call x0 -> x11, Pallas kernels: none -> 13.4 us  [call(): pl.pallas_call(kernel, out_shape=out_shape, in_specs=specs, out_specs=jax...]
    ppermute x10 -> x15, waiting for transfers between devices: 0.03 us -> 9.3 us  [along(): lax.ppermute(sent, 'dp', [(i, i ^ s) for i in range(blocks)])]
    reduce_sum x7 -> x0, other arithmetic: 4.38 us -> none  [the longest x4 2.5 us: local(): curvature = lax.psum(jnp.sum(direction * image), 'mp')]
  transfers between devices with their start and end apart: 10 -> 15, of which waited for: 0 -> 10; matrix products, arithmetic and copies ran while one was open for 10% -> 0% of each run, Pallas kernels for 0% -> 0%
where the time goes in v2:
time: 102 us; the launch traced here: 101 us
  blocking collectives  60.4 us (59%)
  Pallas kernels  13.4 us (13%)
  starting transfers between devices  9.37 us (9%)
  waiting for transfers between devices  9.3 us (9%)
  local copies, waits for them, and re-layouts  7.82 us (8%)
    all_to_all x5, blocking collectives, across(): return lax.all_to_all(sent, 'mp', 0, 0, tiled=True)  60.4 us
    pallas_call x11, Pallas kernels, call(): pl.pallas_call(kernel, out_shape=out_shape, in_specs=specs, out_specs=jax...  13.4 us
    ppermute x15, starting transfers between devices, along(): lax.ppermute(sent, 'dp', [(i, i ^ s) for i in range(blocks)])  9.37 us
    ppermute x15, waiting for transfers between devices, along(): lax.ppermute(sent, 'dp', [(i, i ^ s) for i in range(blocks)])  9.3 us
    unnamed x16, local copies, waits for them, and re-layouts  5.84 us
  transfers between devices with their start and end apart: 15, of which 10 were waited for; matrix products, arithmetic and copies ran while one was open for 0% of the time, Pallas kernels for 0%

profile of v2, /device:TPU:0, one launch (start us, length us, event | category | flops | bytes accessed | tf_op | source)
XLA Modules:
  0.0 101.2 jit_solution(16332717471877177909)
XLA Ops:
  0.6 0.7 reshape.29.model_ref.refs_5_
  1.4 3.6 %copy.8 = bf16[128,8,2,1024]{3,1,2,0:T(8,128)(2,1)S(1)} copy(bf16[128,8,2,1024]{3,2,1,0:T(2,128)(2,1)} %bitcast.40) | data formatting | bytes 8388608
  5.0 0.0 copy-start.3
  5.0 0.0 copy-start.4
  5.0 0.1 pad_add_fusion.place_ref
  5.1 1.8 %start.1 = f32[8,48,128]{2,1,0:T(8,128)S(1)} custom-call(s32[3]{0:T(128)S(1)} %pad_add_fusion.place_ref, bf16[1024,2048]{1,0:T(8,128)(2,1)S(1)} %bitcast.14, f32[2,2,8,128]{3,2,1,0:T(8,128)S(1)} %reshape.29.model_ref.refs_5_), custom_call_target="tpu_custom_call" | custom-call | tf_op jit(solution)/shard_map/start/pallas_call | solution.py:283
  6.9 15.1 %all_to_all.25.got_ref.refs_4_ = f32[8,48,128]{2,1,0:T(8,128)S(1)} all-to-all(f32[8,48,128]{2,1,0:T(8,128)S(1)} %start.1), channel_id=1, replica_groups=mesh['dp'=4,'mp'=8] {'mp'}, dimensions={0} | all-to-all | bytes 393216 | tf_op jit(solution)/shard_map/all_to_all | solution.py:294
  22.0 0.7 rows.5.refs_0_
  22.6 0.0 collective-permute-start.2
  22.6 1.6 %collective-permute-start.1 = (f32[24,128]{1,0:T(8,128)S(1)}, f32[24,128]{1,0:T(8,128)S(1)}, u32[]{:S(2)}, u32[]{:S(2)}) collective-permute-start(f32[24,128]{1,0:T(8,128)S(1)} %rows.5.refs_0_), channel_id=1, source_target_pairs={{0,16},{8,24},{16,0},{24,8},{1,17},{9,25},{17,1},{25,9},{2,18},{10... | collective-permute-start | bytes 36872 | tf_op jit(solution)/shard_map/ppermute | solution.py:308
  24.2 0.3 collective-permute-start
  24.6 1.3 %collective-permute-done.2.refs_3_ = f32[24,128]{1,0:T(8,128)S(1)} collective-permute-done((f32[24,128]{1,0:T(8,128)S(1)}, f32[24,128]{1,0:T(8,128)S(1)}, u32[]{:S(2)}, u32[]{:S(2)}) %collective-permute-start.2) | collective-permute-done | bytes 12320 | tf_op jit(solution)/shard_map/ppermute | solution.py:308
  25.8 0.6 collective-permute-done.1.refs_2_
  26.4 0.0 collective-permute-done.refs_1_
  26.4 2.2 %copy-done.1 = bf16[128,8,2,1024]{3,1,2,0:T(8,128)(2,1)S(1)} copy-done((bf16[128,8,2,1024]{3,1,2,0:T(8,128)(2,1)S(1)}, bf16[128,8,2,1024]{3,1,2,0:T(8,128)(2,1)}, u32[]{:S(2)}) %copy-start.1) | copy-done | bytes 4194328
  28.6 1.9 %first.1 = (f32[8,48,128]{2,1,0:T(8,128)S(1)}, f32[2,2,8,128]{3,2,1,0:T(8,128)S(1)}, f32[2,2,8,128]{3,2,1,0:T(8,128)S(1)}) custom-call(s32[3]{0:T(128)S(1)} %pad_add_fusion.place_ref, bf16[1024,2048]{1,0:T(8,128)(2,1)S(1)} %bitcast.16, f32[24,128]{1,0:T(8,128)S(1)} %rows.5.refs_0_, f32[24,128]{1,0:T(8,128)S(1)} %collective-permute-done.refs_1_, ...), custom_call_target="tpu_custom_call" | custom-call | tf_op jit(solution)/shard_map/first/pallas_call | solution.py:283
  30.5 11.8 %all_to_all.26.got_ref.refs_4_ = f32[8,48,128]{2,1,0:T(8,128)S(1)} all-to-all(f32[8,48,128]{2,1,0:T(8,128)S(1)} %get-tuple-element.28), channel_id=1, replica_groups=mesh['dp'=4,'mp'=8] {'mp'}, dimensions={0} | all-to-all | bytes 393216 | tf_op jit(solution)/shard_map/all_to_all | solution.py:294
  42.3 0.7 rows.6.refs_0_
  43.0 0.0 collective-permute-start.5
  43.0 0.4 collective-permute-start.4
  43.4 1.4 %collective-permute-start.3 = (f32[24,128]{1,0:T(8,128)S(1)}, f32[24,128]{1,0:T(8,128)S(1)}, u32[]{:S(2)}, u32[]{:S(2)}) collective-permute-start(f32[24,128]{1,0:T(8,128)S(1)} %rows.6.refs_0_), channel_id=1, source_target_pairs={{0,8},{8,0},{16,24},{24,16},{1,9},{9,1},{17,25},{25,17},{2,10},{10... | collective-permute-start | bytes 36872 | tf_op jit(solution)/shard_map/ppermute | solution.py:308
  44.9 1.3 %collective-permute-done.5.refs_3_ = f32[24,128]{1,0:T(8,128)S(1)} collective-permute-done((f32[24,128]{1,0:T(8,128)S(1)}, f32[24,128]{1,0:T(8,128)S(1)}, u32[]{:S(2)}, u32[]{:S(2)}) %collective-permute-start.5) | collective-permute-done | bytes 12320 | tf_op jit(solution)/shard_map/ppermute | solution.py:308
  46.1 0.6 collective-permute-done.4.refs_2_
  46.7 1.9 %cells.4 = (f32[2,2,8,128]{3,2,1,0:T(8,128)S(1)}, f32[2,2,8,128]{3,2,1,0:T(8,128)S(1)}, f32[2,2,8,128]{3,2,1,0:T(8,128)S(1)}, f32[2,2,8,128]{3,2,1,0:T(8,128)S(1...) custom-call(s32[3]{0:T(128)S(1)} %pad_add_fusion.place_ref, ...), custom_call_target="tpu_custom_call" | custom-call | tf_op jit(solution)/shard_map/cells/pallas_call | solution.py:283
  48.7 10.7 %all_to_all.27.got_ref.refs_4_ = f32[8,48,128]{2,1,0:T(8,128)S(1)} all-to-all(f32[8,48,128]{2,1,0:T(8,128)S(1)} %get-tuple-element.31), channel_id=1, replica_groups=mesh['dp'=4,'mp'=8] {'mp'}, dimensions={0} | all-to-all | bytes 393216 | tf_op jit(solution)/shard_map/all_to_all | solution.py:294
  59.4 0.6 rows.7.refs_0_
  60.0 1.7 %collective-permute-start.7 = (f32[24,128]{1,0:T(8,128)S(1)}, f32[24,128]{1,0:T(8,128)S(1)}, u32[]{:S(2)}, u32[]{:S(2)}) collective-permute-start(f32[24,128]{1,0:T(8,128)S(1)} %rows.7.refs_0_), channel_id=1, source_target_pairs={{0,16},{8,24},{16,0},{24,8},{1,17},{9,25},{17,1},{25,9},{2,18},{10... | collective-permute-start | bytes 36872 | tf_op jit(solution)/shard_map/ppermute | solution.py:308
  61.8 0.2 collective-permute-start.6
  61.9 1.3 %collective-permute-done.8.refs_3_ = f32[24,128]{1,0:T(8,128)S(1)} collective-permute-done((f32[24,128]{1,0:T(8,128)S(1)}, f32[24,128]{1,0:T(8,128)S(1)}, u32[]{:S(2)}, u32[]{:S(2)}) %collective-permute-start.8) | collective-permute-done | bytes 12320 | tf_op jit(solution)/shard_map/ppermute | solution.py:308
  63.2 0.6 collective-permute-done.7.refs_2_
  63.8 0.0 collective-permute-done.6.refs_1_
  63.8 2.0 %cells.5 = (f32[2,2,8,128]{3,2,1,0:T(8,128)S(1)}, f32[2,2,8,128]{3,2,1,0:T(8,128)S(1)}, f32[2,2,8,128]{3,2,1,0:T(8,128)S(1)}, f32[2,2,8,128]{3,2,1,0:T(8,128)S(1...) custom-call(s32[3]{0:T(128)S(1)} %pad_add_fusion.place_ref, ...), custom_call_target="tpu_custom_call" | custom-call | tf_op jit(solution)/shard_map/cells/pallas_call | solution.py:283
  65.7 12.0 %all_to_all.28.got_ref.refs_4_ = f32[8,48,128]{2,1,0:T(8,128)S(1)} all-to-all(f32[8,48,128]{2,1,0:T(8,128)S(1)} %get-tuple-element.38), channel_id=1, replica_groups=mesh['dp'=4,'mp'=8] {'mp'}, dimensions={0} | all-to-all | bytes 393216 | tf_op jit(solution)/shard_map/all_to_all | solution.py:294
  77.8 0.6 rows.8.refs_0_
  78.4 0.4 collective-permute-start.10
  78.8 1.5 %collective-permute-start.9 = (f32[24,128]{1,0:T(8,128)S(1)}, f32[24,128]{1,0:T(8,128)S(1)}, u32[]{:S(2)}, u32[]{:S(2)}) collective-permute-start(f32[24,128]{1,0:T(8,128)S(1)} %rows.8.refs_0_), channel_id=1, source_target_pairs={{0,8},{8,0},{16,24},{24,16},{1,9},{9,1},{17,25},{25,17},{2,10},{10... | collective-permute-start | bytes 36872 | tf_op jit(solution)/shard_map/ppermute | solution.py:308
  80.3 1.3 %collective-permute-done.11.refs_3_ = f32[24,128]{1,0:T(8,128)S(1)} collective-permute-done((f32[24,128]{1,0:T(8,128)S(1)}, f32[24,128]{1,0:T(8,128)S(1)}, u32[]{:S(2)}, u32[]{:S(2)}) %collective-permute-start.11) | collective-permute-done | bytes 12320 | tf_op jit(solution)/shard_map/ppermute | solution.py:308
  81.6 0.6 collective-permute-done.10.refs_2_
  82.2 2.0 %cells.6 = (f32[2,2,8,128]{3,2,1,0:T(8,128)S(1)}, f32[2,2,8,128]{3,2,1,0:T(8,128)S(1)}, f32[2,2,8,128]{3,2,1,0:T(8,128)S(1)}, f32[2,2,8,128]{3,2,1,0:T(8,128)S(1...) custom-call(s32[3]{0:T(128)S(1)} %pad_add_fusion.place_ref, ...), custom_call_target="tpu_custom_call" | custom-call | tf_op jit(solution)/shard_map/cells/pallas_call | solution.py:283
  84.1 10.7 %all_to_all.29.got_ref.refs_4_ = f32[8,48,128]{2,1,0:T(8,128)S(1)} all-to-all(f32[8,48,128]{2,1,0:T(8,128)S(1)} %get-tuple-element.45), channel_id=1, replica_groups=mesh['dp'=4,'mp'=8] {'mp'}, dimensions={0} | all-to-all | bytes 393216 | tf_op jit(solution)/shard_map/all_to_all | solution.py:294
  94.9 0.7 rows.9.refs_0_
  95.5 1.7 %collective-permute-start.13 = (f32[24,128]{1,0:T(8,128)S(1)}, f32[24,128]{1,0:T(8,128)S(1)}, u32[]{:S(2)}, u32[]{:S(2)}) collective-permute-start(f32[24,128]{1,0:T(8,128)S(1)} %rows.9.refs_0_), channel_id=1, source_target_pairs={{0,16},{8,24},{16,0},{24,8},{1,17},{9,25},{17,1},{25,9},{2,18},{10... | collective-permute-start | bytes 36872 | tf_op jit(solution)/shard_map/ppermute | solution.py:308
  97.2 0.2 collective-permute-start.12
  97.4 1.3 %collective-permute-done.14.refs_3_ = f32[24,128]{1,0:T(8,128)S(1)} collective-permute-done((f32[24,128]{1,0:T(8,128)S(1)}, f32[24,128]{1,0:T(8,128)S(1)}, u32[]{:S(2)}, u32[]{:S(2)}) %collective-permute-start.14) | collective-permute-done | bytes 12320 | tf_op jit(solution)/shard_map/ppermute | solution.py:308
  98.7 0.6 collective-permute-done.13.refs_2_
  99.3 0.7 cells.7
  100.0 0.6 reshape.34
  100.6 0.6 reshape.35
  (20 shorter events, 0.1 us)
Async XLA Ops:
  5.0 17.6 %copy-start = (bf16[128,8,2,1024]{3,1,2,0:T(8,128)(2,1)}, bf16[128,8,2,1024]{3,1,2,0:T(8,128)(2,1)S(1)}, u32[]{:S(2)}) copy-start(bf16[128,8,2,1024]{3,1,2,0:T(8,128)(2,1)S(1)} %copy.8) | copy-start | bytes 12582916
  5.0 17.0 %copy-start.3 = (f32[1024]{0:T(1024)S(1)}, f32[1024]{0:T(1024)}, u32[]{:S(2)}) copy-start(f32[1024]{0:T(1024)} %param.8) | copy-start | bytes 12292
  5.0 17.0 %copy-start.4 = (f32[1024]{0:T(1024)S(1)}, f32[1024]{0:T(1024)}, u32[]{:S(2)}) copy-start(f32[1024]{0:T(1024)} %param.7) | copy-start | bytes 12292
  5.1 19.4 %copy-start.5 = (s32[2,2,1024]{2,1,0:T(2,128)S(1)}, s32[2,2,1024]{2,1,0:T(2,128)}, u32[]{:S(2)}) copy-start(s32[2,2,1024]{2,1,0:T(2,128)} %param.11) | copy-start | bytes 49156
  5.1 19.4 %copy-start.6 = (f32[2,1024]{1,0:T(2,128)S(1)}, f32[2,1024]{1,0:T(2,128)}, u32[]{:S(2)}) copy-start(f32[2,1024]{1,0:T(2,128)} %param.10) | copy-start | bytes 24580
  22.6 3.2 %collective-permute-start.2 = (f32[24,128]{1,0:T(8,128)S(1)}, f32[24,128]{1,0:T(8,128)S(1)}, u32[]{:S(2)}, u32[]{:S(2)}) collective-permute-start(f32[24,128]{1,0:T(8,128)S(1)} %rows.5.refs_0_), channel_id=1, source_target_pairs={{0,24},{8,16},{16,8},{24,0},{1,25},{9,17},{17,9},{25,1},{2,26},{10... | collective-permute-start | bytes 36872 | tf_op jit(solution)/shard_map/ppermute | solution.py:308
  22.6 3.8 %collective-permute-start.1 = (f32[24,128]{1,0:T(8,128)S(1)}, f32[24,128]{1,0:T(8,128)S(1)}, u32[]{:S(2)}, u32[]{:S(2)}) collective-permute-start(f32[24,128]{1,0:T(8,128)S(1)} %rows.5.refs_0_), channel_id=1, source_target_pairs={{0,16},{8,24},{16,0},{24,8},{1,17},{9,25},{17,1},{25,9},{2,18},{10... | collective-permute-start | bytes 36872 | tf_op jit(solution)/shard_map/ppermute | solution.py:308
  24.2 2.2 %collective-permute-start = (f32[24,128]{1,0:T(8,128)S(1)}, f32[24,128]{1,0:T(8,128)S(1)}, u32[]{:S(2)}, u32[]{:S(2)}) collective-permute-start(f32[24,128]{1,0:T(8,128)S(1)} %rows.5.refs_0_), channel_id=1, source_target_pairs={{0,8},{8,0},{16,24},{24,16},{1,9},{9,1},{17,25},{25,17},{2,10},{10... | collective-permute-start | bytes 36872 | tf_op jit(solution)/shard_map/ppermute | solution.py:308
  26.4 2.2 %copy-start.1 = (bf16[128,8,2,1024]{3,1,2,0:T(8,128)(2,1)S(1)}, bf16[128,8,2,1024]{3,1,2,0:T(8,128)(2,1)}, u32[]{:S(2)}) copy-start(bf16[128,8,2,1024]{3,1,2,0:T(8,128)(2,1)} %copy-done) | copy-start | bytes 12582916
  28.6 13.7 %copy-start.2 = (bf16[128,8,2,1024]{3,1,2,0:T(8,128)(2,1)S(1)}, bf16[128,8,2,1024]{3,1,2,0:T(8,128)(2,1)}, u32[]{:S(2)}) copy-start(bf16[128,8,2,1024]{3,1,2,0:T(8,128)(2,1)} %copy-done) | copy-start | bytes 12582916
  43.0 3.1 %collective-permute-start.5 = (f32[24,128]{1,0:T(8,128)S(1)}, f32[24,128]{1,0:T(8,128)S(1)}, u32[]{:S(2)}, u32[]{:S(2)}) collective-permute-start(f32[24,128]{1,0:T(8,128)S(1)} %rows.6.refs_0_), channel_id=1, source_target_pairs={{0,24},{8,16},{16,8},{24,0},{1,25},{9,17},{17,9},{25,1},{2,26},{10... | collective-permute-start | bytes 36872 | tf_op jit(solution)/shard_map/ppermute | solution.py:308
  43.0 3.7 %collective-permute-start.4 = (f32[24,128]{1,0:T(8,128)S(1)}, f32[24,128]{1,0:T(8,128)S(1)}, u32[]{:S(2)}, u32[]{:S(2)}) collective-permute-start(f32[24,128]{1,0:T(8,128)S(1)} %rows.6.refs_0_), channel_id=1, source_target_pairs={{0,16},{8,24},{16,0},{24,8},{1,17},{9,25},{17,1},{25,9},{2,18},{10... | collective-permute-start | bytes 36872 | tf_op jit(solution)/shard_map/ppermute | solution.py:308
  43.4 3.3 %collective-permute-start.3 = (f32[24,128]{1,0:T(8,128)S(1)}, f32[24,128]{1,0:T(8,128)S(1)}, u32[]{:S(2)}, u32[]{:S(2)}) collective-permute-start(f32[24,128]{1,0:T(8,128)S(1)} %rows.6.refs_0_), channel_id=1, source_target_pairs={{0,8},{8,0},{16,24},{24,16},{1,9},{9,1},{17,25},{25,17},{2,10},{10... | collective-permute-start | bytes 36872 | tf_op jit(solution)/shard_map/ppermute | solution.py:308
  60.0 3.1 %collective-permute-start.8 = (f32[24,128]{1,0:T(8,128)S(1)}, f32[24,128]{1,0:T(8,128)S(1)}, u32[]{:S(2)}, u32[]{:S(2)}) collective-permute-start(f32[24,128]{1,0:T(8,128)S(1)} %rows.7.refs_0_), channel_id=1, source_target_pairs={{0,24},{8,16},{16,8},{24,0},{1,25},{9,17},{17,9},{25,1},{2,26},{10... | collective-permute-start | bytes 36872 | tf_op jit(solution)/shard_map/ppermute | solution.py:308
  60.0 3.7 %collective-permute-start.7 = (f32[24,128]{1,0:T(8,128)S(1)}, f32[24,128]{1,0:T(8,128)S(1)}, u32[]{:S(2)}, u32[]{:S(2)}) collective-permute-start(f32[24,128]{1,0:T(8,128)S(1)} %rows.7.refs_0_), channel_id=1, source_target_pairs={{0,16},{8,24},{16,0},{24,8},{1,17},{9,25},{17,1},{25,9},{2,18},{10... | collective-permute-start | bytes 36872 | tf_op jit(solution)/shard_map/ppermute | solution.py:308
  61.8 2.0 %collective-permute-start.6 = (f32[24,128]{1,0:T(8,128)S(1)}, f32[24,128]{1,0:T(8,128)S(1)}, u32[]{:S(2)}, u32[]{:S(2)}) collective-permute-start(f32[24,128]{1,0:T(8,128)S(1)} %rows.7.refs_0_), channel_id=1, source_target_pairs={{0,8},{8,0},{16,24},{24,16},{1,9},{9,1},{17,25},{25,17},{2,10},{10... | collective-permute-start | bytes 36872 | tf_op jit(solution)/shard_map/ppermute | solution.py:308
  78.4 3.1 %collective-permute-start.11 = (f32[24,128]{1,0:T(8,128)S(1)}, f32[24,128]{1,0:T(8,128)S(1)}, u32[]{:S(2)}, u32[]{:S(2)}) collective-permute-start(f32[24,128]{1,0:T(8,128)S(1)} %rows.8.refs_0_), channel_id=1, source_target_pairs={{0,24},{8,16},{16,8},{24,0},{1,25},{9,17},{17,9},{25,1},{2,26},{10... | collective-permute-start | bytes 36872 | tf_op jit(solution)/shard_map/ppermute | solution.py:308
  78.4 3.7 %collective-permute-start.10 = (f32[24,128]{1,0:T(8,128)S(1)}, f32[24,128]{1,0:T(8,128)S(1)}, u32[]{:S(2)}, u32[]{:S(2)}) collective-permute-start(f32[24,128]{1,0:T(8,128)S(1)} %rows.8.refs_0_), channel_id=1, source_target_pairs={{0,16},{8,24},{16,0},{24,8},{1,17},{9,25},{17,1},{25,9},{2,18},{10... | collective-permute-start | bytes 36872 | tf_op jit(solution)/shard_map/ppermute | solution.py:308
  78.8 3.3 %collective-permute-start.9 = (f32[24,128]{1,0:T(8,128)S(1)}, f32[24,128]{1,0:T(8,128)S(1)}, u32[]{:S(2)}, u32[]{:S(2)}) collective-permute-start(f32[24,128]{1,0:T(8,128)S(1)} %rows.8.refs_0_), channel_id=1, source_target_pairs={{0,8},{8,0},{16,24},{24,16},{1,9},{9,1},{17,25},{25,17},{2,10},{10... | collective-permute-start | bytes 36872 | tf_op jit(solution)/shard_map/ppermute | solution.py:308
  95.5 3.1 %collective-permute-start.14 = (f32[24,128]{1,0:T(8,128)S(1)}, f32[24,128]{1,0:T(8,128)S(1)}, u32[]{:S(2)}, u32[]{:S(2)}) collective-permute-start(f32[24,128]{1,0:T(8,128)S(1)} %rows.9.refs_0_), channel_id=1, source_target_pairs={{0,24},{8,16},{16,8},{24,0},{1,25},{9,17},{17,9},{25,1},{2,26},{10... | collective-permute-start | bytes 36872 | tf_op jit(solution)/shard_map/ppermute | solution.py:308
  95.5 3.7 %collective-permute-start.13 = (f32[24,128]{1,0:T(8,128)S(1)}, f32[24,128]{1,0:T(8,128)S(1)}, u32[]{:S(2)}, u32[]{:S(2)}) collective-permute-start(f32[24,128]{1,0:T(8,128)S(1)} %rows.9.refs_0_), channel_id=1, source_target_pairs={{0,16},{8,24},{16,0},{24,8},{1,17},{9,25},{17,1},{25,9},{2,18},{10... | collective-permute-start | bytes 36872 | tf_op jit(solution)/shard_map/ppermute | solution.py:308
  97.2 2.0 %collective-permute-start.12 = (f32[24,128]{1,0:T(8,128)S(1)}, f32[24,128]{1,0:T(8,128)S(1)}, u32[]{:S(2)}, u32[]{:S(2)}) collective-permute-start(f32[24,128]{1,0:T(8,128)S(1)} %rows.9.refs_0_), channel_id=1, source_target_pairs={{0,8},{8,0},{16,24},{24,16},{1,9},{9,1},{17,25},{25,17},{2,10},{10... | collective-permute-start | bytes 36872 | tf_op jit(solution)/shard_map/ppermute | solution.py:308

commit v3 on v2

--- a/solution.py
+++ b/solution.py
@@ -97,7 +97,32 @@
     )
 
 
-def send_rows(place_ref, matrix_ref, field, lines, out_ref):
+def rows_between(plane, low, count):
+    line = lax.broadcasted_iota(jnp.int32, plane.shape, 0)
+    return (line >= low) & (line < low + count)
+
+
+def share_of(planes, member, members):
+    tall = planes[0].shape[0]
+    count = tall // members
+    out = jnp.zeros_like(planes[0])
+    for n, plane in enumerate(planes):
+        moved = pltpu.roll(plane, (n * count - member * count + tall) % tall, 0)
+        out = jnp.where(rows_between(plane, n * count, count), moved, out)
+    return out
+
+
+def from_shares(shares, members, n):
+    tall = shares[0][1].shape[0]
+    count = tall // members
+    out = jnp.zeros_like(shares[0][1])
+    for member, share in shares:
+        moved = pltpu.roll(share, (member * count - n * count + tall) % tall, 0)
+        out = jnp.where(rows_between(share, member * count, count), moved, out)
+    return out
+
+
+def send_rows(place_ref, matrix_ref, field, lines, out_ref, members):
     owners = out_ref.shape[0]
     rows = matrix_ref.shape[0]
     tall = field[0][0].shape[0]
@@ -116,7 +141,8 @@
         )
         for b in range(rows // LANES)
     ]
-    pieces += [field[0][0], field[1][0], field[0][-1], field[1][-1]]
+    edges = [field[0][0], field[1][0], field[0][-1], field[1][-1]]
+    pieces.append(share_of(edges, place_ref[1], members))
     pieces += lines
     pieces.append(jnp.zeros((SUBLANES - len(lines), LANES), jnp.float32))
     message = jnp.concatenate(pieces, axis=0)
@@ -124,11 +150,33 @@
         out_ref[j] = message
 
 
-def start_kernel(place_ref, matrix_ref, model_ref, out_ref):
-    send_rows(place_ref, matrix_ref, load(model_ref), [], out_ref)
-
-
-def rows_kernel(matrix_ref, got_ref, weight_ref, observed_ref, out_ref, *, subtract):
+def load_layers(ref):
+    layers, width = ref.shape
+    return [
+        jnp.concatenate([ref[i : i + 1, t : t + LANES] for t in range(0, width, LANES)], axis=0)
+        for i in range(layers)
+    ]
+
+
+def load_wide(ref):
+    return [load_layers(ref.at[f]) for f in range(2)]
+
+
+def store_wide(ref, field):
+    for f in range(2):
+        for i in range(ref.shape[1]):
+            for t in range(ref.shape[2] // LANES):
+                ref[f, i : i + 1, t * LANES : (t + 1) * LANES] = field[f][i][t : t + 1]
+
+
+def start_kernel(place_ref, matrix_ref, model_ref, out_ref, *, members):
+    send_rows(place_ref, matrix_ref, load_wide(model_ref), [], out_ref, members)
+
+
+def rows_kernel(
+    place_ref, matrix_ref, got_ref, weight_ref, observed_ref, out_ref, *, subtract, members, tall
+):
+    rank = place_ref[0]
     owners = got_ref.shape[0]
     rows, cells = matrix_ref.shape
     blocks = rows // LANES
@@ -142,29 +190,40 @@
     vector = spread([scaled], 2 * SUBLANES).astype(jnp.bfloat16)
     columns = jnp.dot(vector, matrix_ref[...], preferred_element_type=jnp.float32)
     pieces = [columns[0:1, t * LANES : (t + 1) * LANES] for t in range(cells // LANES)]
-    pieces += [weighed, jnp.zeros((SUBLANES - 1, LANES), jnp.float32)]
+    half = 2 * (tall // members)
+    shares = [got_ref[j, blocks : blocks + tall] for j in range(owners)]
+    lower = rows_between(shares[0], 0, half)
+    upper = rows_between(shares[0], half, half)
+    cross = None
+    for j in range(owners - 1):
+        term = shares[j] * pltpu.roll(shares[j + 1], half, 0)
+        cross = term if cross is None else cross + term
+    cross = jnp.sum(jnp.where(upper, cross, 0.0), axis=0, keepdims=True)
+    weighed = weighed - 2.0 * SMOOTHING * cross
+    down = jnp.maximum(rank - 1, 0)
+    up = jnp.minimum(rank + 1, owners - 1)
+    above = jnp.where(lower & (rank < owners - 1), got_ref[up, blocks : blocks + tall], 0.0)
+    below = jnp.where(upper & (rank > 0), got_ref[down, blocks : blocks + tall], 0.0)
+    pieces += [above + below, weighed, jnp.zeros((SUBLANES - 1, LANES), jnp.float32)]
     out_ref[...] = jnp.concatenate(pieces, axis=0)
 
 
-def gathered(place_ref, part_refs, got_ref, inner_ref, mask_ref, base):
-    rank = place_ref[0]
-    owners = got_ref.shape[0]
+def gathered(place_ref, part_refs, inner_ref, mask_ref):
     layers, tall = inner_ref.shape[1:3]
     cells = layers * tall
-    gravity = [(place_ref[1] ^ s) < place_ref[2] for s in range(len(part_refs))]
+    members = len(part_refs)
+    sources = [place_ref[1] ^ s for s in range(members)]
+    gravity = [q < place_ref[2] for q in sources]
     parts = [ref[0:cells] for ref in part_refs]
     data = [
         tree_sum([jnp.where(g, p, 0.0) for g, p in zip(gravity, parts)]),
         tree_sum([jnp.where(g, 0.0, p) for g, p in zip(gravity, parts)]),
     ]
-    down = jnp.maximum(rank - 1, 0)
-    up = jnp.minimum(rank + 1, owners - 1)
+    shares = [(q, ref[cells : cells + tall]) for q, ref in zip(sources, part_refs)]
     image = [[], []]
     for f in range(2):
-        first = base + f * tall
-        last = base + (2 + f) * tall
-        below = jnp.where(rank > 0, got_ref[down, last : last + tall], 0.0)
-        above = jnp.where(rank < owners - 1, got_ref[up, first : first + tall], 0.0)
+        above = from_shares(shares, members, f)
+        below = from_shares(shares, members, 2 + f)
         for i in range(layers):
             regular = inner_ref[f, i]
             if i == 0:
@@ -175,19 +234,23 @@
     return image
 
 
-def first_kernel(place_ref, matrix_ref, *refs, count, base):
+def first_kernel(place_ref, matrix_ref, *refs, count):
     part_refs = refs[:count]
-    got_ref, model_ref, smooth_ref, mask_ref, out_ref, residual_ref, inner_ref, held = refs[count:]
+    model_ref, weight_ref, active_ref, out_ref, residual_ref, inner_ref = refs[count : count + 6]
+    smooth_ref, mask_ref, held = refs[count + 6 :]
     layers = model_ref.shape[1]
-    smooth_weight = [smooth_ref[i] for i in range(layers)]
-    store(held, operate_inner(load(model_ref), smooth_weight))
-    image = gathered(place_ref, part_refs, got_ref, held, mask_ref, base)
+    smooth_weight = load_layers(weight_ref)
+    for i in range(layers):
+        smooth_ref[i] = smooth_weight[i]
+    store(mask_ref, mapped(lambda a: 1.0 - a.astype(jnp.float32), load_wide(active_ref)))
+    store(held, operate_inner(load_wide(model_ref), smooth_weight))
+    image = gathered(place_ref, part_refs, held, mask_ref)
     residual = mapped(lambda a: -a, image)
     inner = operate_inner(residual, smooth_weight)
     store(residual_ref, residual)
     store(inner_ref, inner)
     lines = [dot_line(residual, residual), dot_line(residual, inner)]
-    send_rows(place_ref, matrix_ref, residual, lines, out_ref)
+    send_rows(place_ref, matrix_ref, residual, lines, out_ref, count)
 
 
 def cells_kernel(place_ref, matrix_ref, *refs, count, base, begin, final):
@@ -202,20 +265,14 @@
     layers, tall = inner_in.shape[1:3]
     cells = layers * tall
     residual = load(residual_in)
-    image = gathered(place_ref, part_refs, got_ref, inner_in, mask_ref, base)
-    at = base + 4 * tall
+    image = gathered(place_ref, part_refs, inner_in, mask_ref)
+    at = base + tall
     sums = got_ref[0, at : at + SUBLANES]
     for j in range(1, owners):
         sums = sums + got_ref[j, at : at + SUBLANES]
-    cross = None
-    for j in range(owners - 1):
-        term = (
-            got_ref[j, base + 2 * tall : base + 4 * tall] * got_ref[j + 1, base : base + 2 * tall]
-        )
-        cross = term if cross is None else cross + term
-    weighed = tree_sum([ref[cells : cells + 1] for ref in part_refs])
+    at = cells + tall
+    weighed = tree_sum([ref[at : at + 1] for ref in part_refs])
     line = weighed + sums[1:2]
-    line = line - 2.0 * SMOOTHING * jnp.sum(cross, axis=0, keepdims=True)
     norm_now = full(sums[0:1])
     curvature = full(line)
     if begin:
@@ -231,10 +288,12 @@
     else:
         update = mapped(lambda x, d: x + step_len * d, load(solution_in), direction)
     residual = mapped(lambda r, s: r - step_len * s, residual, imaged)
+    if final:
+        store_wide(solution_ref, update)
+        store_wide(residual_ref, residual)
+        return
     store(solution_ref, update)
     store(residual_ref, residual)
-    if final:
-        return
     direction_ref, imaged_ref, norms_ref, inner_ref, out_ref = refs[2:]
     store(direction_ref, direction)
     store(imaged_ref, imaged)
@@ -243,7 +302,7 @@
     inner = operate_inner(residual, [smooth_ref[i] for i in range(layers)])
     store(inner_ref, inner)
     lines = [dot_line(residual, residual), dot_line(residual, inner), dot_line(residual, imaged)]
-    send_rows(place_ref, matrix_ref, residual, lines, out_ref)
+    send_rows(place_ref, matrix_ref, residual, lines, out_ref, count)
 
 
 def local(sensitivity, observed, row_weight, model, smooth_weight, active):
@@ -258,83 +317,72 @@
     ).astype(jnp.int32)
     base = rows // LANES
 
-    def planes(x):
-        return x.reshape(x.shape[:-1] + (tall, LANES))
-
-    mask = planes(1.0 - active.astype(jnp.float32))
-    smooth = planes(smooth_weight)
     weight = row_weight.reshape(base, LANES)
     target = observed.reshape(base, LANES)
-    start = planes(model)
-    matrix = pltpu.with_memory_space_constraint(matrix, pltpu.VMEM)
-
-    cell = jax.ShapeDtypeStruct(start.shape, jnp.float32)
-    message = jax.ShapeDtypeStruct(
-        (owners, base + 4 * tall + SUBLANES, LANES), jnp.float32
-    )
-    columns = jax.ShapeDtypeStruct((layers * tall + SUBLANES, LANES), jnp.float32)
+
+    cell = jax.ShapeDtypeStruct((2, layers, tall, LANES), jnp.float32)
+    field = jax.ShapeDtypeStruct(cell.shape[1:], jnp.float32)
+    wide = jax.ShapeDtypeStruct(model.shape, jnp.float32)
+    if tall % blocks or blocks < 4:
+        raise ValueError("boundary shares")
+    message = jax.ShapeDtypeStruct((owners, base + tall + SUBLANES, LANES), jnp.float32)
+    columns = jax.ShapeDtypeStruct(((layers + 1) * tall + SUBLANES, LANES), jnp.float32)
     norms = jax.ShapeDtypeStruct((2, LANES), jnp.float32)
     smem = pl.BlockSpec(memory_space=pltpu.SMEM)
     vmem = pl.BlockSpec(memory_space=pltpu.VMEM)
 
-    def call(kernel, out_shape, *operands, name, scratch=(), scalars=True):
-        specs = [smem] * scalars + [vmem] * len(operands)
-        operands = ((place,) if scalars else ()) + operands
+    def call(kernel, out_shape, *operands, name, scratch=()):
+        held = pltpu.with_memory_space_constraint(matrix, pltpu.VMEM)
         return pl.pallas_call(
             kernel,
             out_shape=out_shape,
-            in_specs=specs,
+            in_specs=[smem] + [vmem] * (1 + len(operands)),
             out_specs=jax.tree.map(lambda _: vmem, out_shape),
             scratch_shapes=scratch,
             compiler_params=pltpu.CompilerParams(vmem_limit_bytes=KERNEL_VMEM),
             name=name,
-        )(*operands)
+        )(place, held, *operands)
 
     def across(sent):
         return lax.all_to_all(sent, "mp", 0, 0, tiled=True)
 
     def along(got, subtract):
         sent = call(
-            functools.partial(rows_kernel, subtract=subtract),
+            functools.partial(rows_kernel, subtract=subtract, members=blocks, tall=tall),
             columns,
-            matrix,
             got,
             weight,
             target,
             name="rows",
-            scalars=False,
         )
         return [sent] + [
             lax.ppermute(sent, "dp", [(i, i ^ s) for i in range(blocks)])
             for s in range(1, blocks)
         ]
 
-    got = across(call(start_kernel, message, matrix, start, name="start"))
+    got = across(call(functools.partial(start_kernel, members=blocks), message, model, name="start"))
     parts = along(got, True)
-    sent, residual, inner = call(
-        functools.partial(first_kernel, count=blocks, base=base),
-        (message, cell, cell),
-        matrix,
+    sent, residual, inner, smooth, mask = call(
+        functools.partial(first_kernel, count=blocks),
+        (message, cell, cell, field, cell),
         *parts,
-        got,
-        start,
-        smooth,
-        mask,
+        model,
+        smooth_weight,
+        active,
         name="first",
-        scratch=[pltpu.VMEM(start.shape, jnp.float32)],
+        scratch=[pltpu.VMEM(cell.shape, jnp.float32)],
     )
     carried = ()
     for step in range(ITERS):
         got = across(sent)
         parts = along(got, False)
         final = step == ITERS - 1
-        outs = (cell, cell) if final else (cell, cell, cell, cell, norms, cell, message)
+        outs = (wide, wide) if final else (cell, cell, cell, cell, norms, cell, message)
         result = call(
             functools.partial(
                 cells_kernel, count=blocks, base=base, begin=step == 0, final=final
             ),
             outs,
-            matrix,
             *parts,
             got,
             smooth,
@@ -349,7 +397,7 @@
         else:
             update, residual, direction, imaged, scalars, inner, sent = result
             carried = (direction, imaged, update, scalars)
-    return (update.reshape(model.shape), residual.reshape(model.shape))
+    return (update, residual)
 
 
 def solution(mesh):

time: 102 us -> 93.1 us (0.913)
  blocking collectives: 60.4 us -> 52.6 us
  local copies, waits for them, and re-layouts: 7.82 us -> 3.65 us
  Pallas kernels: 13.4 us -> 16.8 us
    all_to_all x5, blocking collectives: 60.4 us -> 52.6 us  [across(): return lax.all_to_all(sent, 'mp', 0, 0, tiled=True)]
    pallas_call x11, Pallas kernels: 13.4 us -> 16.8 us  [call(): pl.pallas_call(kernel, out_shape=out_shape, in_specs=[smem] + [vmem] * (1...]
    unnamed x16 -> x11, local copies, waits for them, and re-layouts: 5.84 us -> 3.65 us
    reshape x4 -> x0, local copies, waits for them, and re-layouts: 1.98 us -> none  [the longest x2 1.23 us: local(): return (update.reshape(model.shape), residual.reshape(model.shape))]
where the time goes in v3:
time: 93.1 us; the launch traced here: 92.8 us
  blocking collectives  52.6 us (56%)
  Pallas kernels  16.8 us (18%)
  waiting for transfers between devices  9.58 us (10%)
  starting transfers between devices  9.38 us (10%)
  local copies, waits for them, and re-layouts  3.65 us (4%)
    all_to_all x5, blocking collectives, across(): return lax.all_to_all(sent, 'mp', 0, 0, tiled=True)  52.6 us
    pallas_call x11, Pallas kernels, call(): pl.pallas_call(kernel, out_shape=out_shape, in_specs=[smem] + [vmem] * (1...  16.8 us
    ppermute x15, waiting for transfers between devices, along(): lax.ppermute(sent, 'dp', [(i, i ^ s) for i in range(blocks)])  9.58 us
    ppermute x15, starting transfers between devices, along(): lax.ppermute(sent, 'dp', [(i, i ^ s) for i in range(blocks)])  9.38 us
    unnamed x11, local copies, waits for them, and re-layouts  3.65 us
  transfers between devices with their start and end apart: 15, of which 10 were waited for; matrix products, arithmetic and copies ran while one was open for 0% of the time, Pallas kernels for 0%

profile of v3, /device:TPU:0, one launch (start us, length us, event | category | flops | bytes accessed | tf_op | source)
XLA Modules:
  0.0 92.8 jit_solution(7597054671248890282)
XLA Ops:
  0.6 3.6 %copy.8 = bf16[128,8,2,1024]{3,1,2,0:T(8,128)(2,1)S(1)} copy(bf16[128,8,2,1024]{3,2,1,0:T(2,128)(2,1)} %bitcast.27) | data formatting | bytes 8388608
  4.3 0.0 copy-start
  4.3 0.0 copy-start.1
  4.3 0.1 pad_add_fusion.place_ref
  4.4 1.8 %start.1 = f32[8,24,128]{2,1,0:T(8,128)S(1)} custom-call(s32[3]{0:T(128)S(1)} %pad_add_fusion.place_ref, bf16[1024,2048]{1,0:T(8,128)(2,1)S(1)} %bitcast.6, f32[2,2,1024]{2,1,0:T(2,128)S(1)} %copy-done.2), custom_call_target="tpu_custom_call" | custom-call | tf_op jit(solution)/shard_map/start/pallas_call | solution.py:336
  6.2 14.2 %all_to_all.25.got_ref = f32[8,24,128]{2,1,0:T(8,128)S(1)} all-to-all(f32[8,24,128]{2,1,0:T(8,128)S(1)} %start.1), channel_id=1, replica_groups=mesh['dp'=4,'mp'=8] {'mp'}, dimensions={0} | all-to-all | bytes 196608 | tf_op jit(solution)/shard_map/all_to_all | solution.py:347
  20.4 1.2 %rows.5.refs_0_ = f32[32,128]{1,0:T(8,128)S(1)} custom-call(s32[3]{0:T(128)S(1)} %pad_add_fusion.place_ref, bf16[1024,2048]{1,0:T(8,128)(2,1)S(1)} %bitcast.7, f32[8,24,128]{2,1,0:T(8,128)S(1)} %all_to_all.25.got_ref, f32[8,128]{1,0:T(8,128)S(1)} %bitcast.17, f32[8,128]{1,0:T(8,128)S(1)} %bitcast.22), custom_call_target="tpu_custom_call" | custom-call | tf_op jit(solution)/shard_map/rows/pallas_call | solution.py:336
  21.6 0.0 collective-permute-start.2
  21.6 1.5 %collective-permute-start.1 = (f32[32,128]{1,0:T(8,128)S(1)}, f32[32,128]{1,0:T(8,128)S(1)}, u32[]{:S(2)}, u32[]{:S(2)}) collective-permute-start(f32[32,128]{1,0:T(8,128)S(1)} %rows.5.refs_0_), channel_id=1, source_target_pairs={{0,16},{8,24},{16,0},{24,8},{1,17},{9,25},{17,1},{25,9},{2,18},{10... | collective-permute-start | bytes 49160 | tf_op jit(solution)/shard_map/ppermute | solution.py:359
  23.2 0.3 collective-permute-start
  23.5 1.4 %collective-permute-done.2.refs_3_ = f32[32,128]{1,0:T(8,128)S(1)} collective-permute-done((f32[32,128]{1,0:T(8,128)S(1)}, f32[32,128]{1,0:T(8,128)S(1)}, u32[]{:S(2)}, u32[]{:S(2)}) %collective-permute-start.2) | collective-permute-done | bytes 16416 | tf_op jit(solution)/shard_map/ppermute | solution.py:359
  24.9 0.5 collective-permute-done.1.refs_2_
  25.4 0.0 collective-permute-done.refs_1_
  25.4 1.9 %first.1 = (f32[8,24,128]{2,1,0:T(8,128)S(1)}, f32[2,2,8,128]{3,2,1,0:T(8,128)S(1)}, f32[2,2,8,128]{3,2,1,0:T(8,128)S(1)}, f32[2,8,128]{2,1,0:T(8,128)S(1)}, f32[2,2,8,128]{3,2,1,0:T(8,128)S(1)}) custom-call(s32[3]{0:T(128)S(1)} %pad_add_fusion.place_ref, bf16[1024,2048]{1,0:T(8,128)(2,1)S(1)} %bitcast.8, f32[32,128]{1,0:T(8,128)S(1)} %rows.5.refs_0_, ...), custom_call_target="tpu_custom_call" | custom-call | tf_op jit(solution)/shard_map/first/pallas_call | solution.py:336
  27.3 9.8 %all_to_all.26.got_ref.refs_4_ = f32[8,24,128]{2,1,0:T(8,128)S(1)} all-to-all(f32[8,24,128]{2,1,0:T(8,128)S(1)} %get-tuple-element.28), channel_id=1, replica_groups=mesh['dp'=4,'mp'=8] {'mp'}, dimensions={0} | all-to-all | bytes 196608 | tf_op jit(solution)/shard_map/all_to_all | solution.py:347
  37.1 1.2 %rows.6.refs_0_ = f32[32,128]{1,0:T(8,128)S(1)} custom-call(s32[3]{0:T(128)S(1)} %pad_add_fusion.place_ref, bf16[1024,2048]{1,0:T(8,128)(2,1)S(1)} %bitcast.9, f32[8,24,128]{2,1,0:T(8,128)S(1)} %all_to_all.26.got_ref.refs_4_, f32[8,128]{1,0:T(8,128)S(1)} %bitcast.18, f32[8,128]{1,0:T(8,128)S(1)} %bitcast.23), custom_call_target="tpu_custom_call" | custom-call | tf_op jit(solution)/shard_map/rows/pallas_call | solution.py:336
  38.3 0.0 collective-permute-start.5
  38.3 1.3 %collective-permute-start.4 = (f32[32,128]{1,0:T(8,128)S(1)}, f32[32,128]{1,0:T(8,128)S(1)}, u32[]{:S(2)}, u32[]{:S(2)}) collective-permute-start(f32[32,128]{1,0:T(8,128)S(1)} %rows.6.refs_0_), channel_id=1, source_target_pairs={{0,16},{8,24},{16,0},{24,8},{1,17},{9,25},{17,1},{25,9},{2,18},{10... | collective-permute-start | bytes 49160 | tf_op jit(solution)/shard_map/ppermute | solution.py:359
  39.6 0.6 collective-permute-start.3
  40.2 1.3 %collective-permute-done.5.refs_3_ = f32[32,128]{1,0:T(8,128)S(1)} collective-permute-done((f32[32,128]{1,0:T(8,128)S(1)}, f32[32,128]{1,0:T(8,128)S(1)}, u32[]{:S(2)}, u32[]{:S(2)}) %collective-permute-start.5) | collective-permute-done | bytes 16416 | tf_op jit(solution)/shard_map/ppermute | solution.py:359
  41.5 0.6 collective-permute-done.4.refs_2_
  42.1 0.0 collective-permute-done.3.refs_1_
  42.1 1.9 %cells.4 = (f32[2,2,8,128]{3,2,1,0:T(8,128)S(1)}, f32[2,2,8,128]{3,2,1,0:T(8,128)S(1)}, f32[2,2,8,128]{3,2,1,0:T(8,128)S(1)}, f32[2,2,8,128]{3,2,1,0:T(8,128)S(1...) custom-call(s32[3]{0:T(128)S(1)} %pad_add_fusion.place_ref, ...), custom_call_target="tpu_custom_call" | custom-call | tf_op jit(solution)/shard_map/cells/pallas_call | solution.py:336
  44.0 9.5 %all_to_all.27.got_ref.refs_4_ = f32[8,24,128]{2,1,0:T(8,128)S(1)} all-to-all(f32[8,24,128]{2,1,0:T(8,128)S(1)} %get-tuple-element.33), channel_id=1, replica_groups=mesh['dp'=4,'mp'=8] {'mp'}, dimensions={0} | all-to-all | bytes 196608 | tf_op jit(solution)/shard_map/all_to_all | solution.py:347
  53.5 1.2 %rows.7.refs_0_ = f32[32,128]{1,0:T(8,128)S(1)} custom-call(s32[3]{0:T(128)S(1)} %pad_add_fusion.place_ref, bf16[1024,2048]{1,0:T(8,128)(2,1)S(1)} %bitcast.11, f32[8,24,128]{2,1,0:T(8,128)S(1)} %all_to_all.27.got_ref.refs_4_, f32[8,128]{1,0:T(8,128)S(1)} %bitcast.19, f32[8,128]{1,0:T(8,128)S(1)} %bitcast.24), custom_call_target="tpu_custom_call" | custom-call | tf_op jit(solution)/shard_map/rows/pallas_call | solution.py:336
  54.7 0.0 collective-permute-start.8
  54.7 1.4 %collective-permute-start.7 = (f32[32,128]{1,0:T(8,128)S(1)}, f32[32,128]{1,0:T(8,128)S(1)}, u32[]{:S(2)}, u32[]{:S(2)}) collective-permute-start(f32[32,128]{1,0:T(8,128)S(1)} %rows.7.refs_0_), channel_id=1, source_target_pairs={{0,16},{8,24},{16,0},{24,8},{1,17},{9,25},{17,1},{25,9},{2,18},{10... | collective-permute-start | bytes 49160 | tf_op jit(solution)/shard_map/ppermute | solution.py:359
  56.1 0.5 collective-permute-start.6
  56.6 1.4 %collective-permute-done.8.refs_3_ = f32[32,128]{1,0:T(8,128)S(1)} collective-permute-done((f32[32,128]{1,0:T(8,128)S(1)}, f32[32,128]{1,0:T(8,128)S(1)}, u32[]{:S(2)}, u32[]{:S(2)}) %collective-permute-start.8) | collective-permute-done | bytes 16416 | tf_op jit(solution)/shard_map/ppermute | solution.py:359
  57.9 0.6 collective-permute-done.7.refs_2_
  58.5 0.0 collective-permute-done.6.refs_1_
  58.5 1.9 %cells.5 = (f32[2,2,8,128]{3,2,1,0:T(8,128)S(1)}, f32[2,2,8,128]{3,2,1,0:T(8,128)S(1)}, f32[2,2,8,128]{3,2,1,0:T(8,128)S(1)}, f32[2,2,8,128]{3,2,1,0:T(8,128)S(1...) custom-call(s32[3]{0:T(128)S(1)} %pad_add_fusion.place_ref, ...), custom_call_target="tpu_custom_call" | custom-call | tf_op jit(solution)/shard_map/cells/pallas_call | solution.py:336
  60.4 9.6 %all_to_all.28.got_ref.refs_4_ = f32[8,24,128]{2,1,0:T(8,128)S(1)} all-to-all(f32[8,24,128]{2,1,0:T(8,128)S(1)} %get-tuple-element.40), channel_id=1, replica_groups=mesh['dp'=4,'mp'=8] {'mp'}, dimensions={0} | all-to-all | bytes 196608 | tf_op jit(solution)/shard_map/all_to_all | solution.py:347
  70.0 1.2 %rows.8.refs_0_ = f32[32,128]{1,0:T(8,128)S(1)} custom-call(s32[3]{0:T(128)S(1)} %pad_add_fusion.place_ref, bf16[1024,2048]{1,0:T(8,128)(2,1)S(1)} %bitcast.13, f32[8,24,128]{2,1,0:T(8,128)S(1)} %all_to_all.28.got_ref.refs_4_, f32[8,128]{1,0:T(8,128)S(1)} %bitcast.20, f32[8,128]{1,0:T(8,128)S(1)} %bitcast.25), custom_call_target="tpu_custom_call" | custom-call | tf_op jit(solution)/shard_map/rows/pallas_call | solution.py:336
  71.2 0.0 collective-permute-start.11
  71.2 1.3 %collective-permute-start.10 = (f32[32,128]{1,0:T(8,128)S(1)}, f32[32,128]{1,0:T(8,128)S(1)}, u32[]{:S(2)}, u32[]{:S(2)}) collective-permute-start(f32[32,128]{1,0:T(8,128)S(1)} %rows.8.refs_0_), channel_id=1, source_target_pairs={{0,16},{8,24},{16,0},{24,8},{1,17},{9,25},{17,1},{25,9},{2,18},{10... | collective-permute-start | bytes 49160 | tf_op jit(solution)/shard_map/ppermute | solution.py:359
  72.5 0.6 collective-permute-start.9
  73.1 1.3 %collective-permute-done.11.refs_3_ = f32[32,128]{1,0:T(8,128)S(1)} collective-permute-done((f32[32,128]{1,0:T(8,128)S(1)}, f32[32,128]{1,0:T(8,128)S(1)}, u32[]{:S(2)}, u32[]{:S(2)}) %collective-permute-start.11) | collective-permute-done | bytes 16416 | tf_op jit(solution)/shard_map/ppermute | solution.py:359
  74.4 0.6 collective-permute-done.10.refs_2_
  75.0 1.9 %cells.6 = (f32[2,2,8,128]{3,2,1,0:T(8,128)S(1)}, f32[2,2,8,128]{3,2,1,0:T(8,128)S(1)}, f32[2,2,8,128]{3,2,1,0:T(8,128)S(1)}, f32[2,2,8,128]{3,2,1,0:T(8,128)S(1...) custom-call(s32[3]{0:T(128)S(1)} %pad_add_fusion.place_ref, ...), custom_call_target="tpu_custom_call" | custom-call | tf_op jit(solution)/shard_map/cells/pallas_call | solution.py:336
  77.0 9.5 %all_to_all.29.got_ref.refs_4_ = f32[8,24,128]{2,1,0:T(8,128)S(1)} all-to-all(f32[8,24,128]{2,1,0:T(8,128)S(1)} %get-tuple-element.47), channel_id=1, replica_groups=mesh['dp'=4,'mp'=8] {'mp'}, dimensions={0} | all-to-all | bytes 196608 | tf_op jit(solution)/shard_map/all_to_all | solution.py:347
  86.5 1.2 %rows.9.refs_0_ = f32[32,128]{1,0:T(8,128)S(1)} custom-call(s32[3]{0:T(128)S(1)} %pad_add_fusion.place_ref, bf16[1024,2048]{1,0:T(8,128)(2,1)S(1)} %bitcast.15, f32[8,24,128]{2,1,0:T(8,128)S(1)} %all_to_all.29.got_ref.refs_4_, f32[8,128]{1,0:T(8,128)S(1)} %bitcast.21, f32[8,128]{1,0:T(8,128)S(1)} %bitcast.26), custom_call_target="tpu_custom_call" | custom-call | tf_op jit(solution)/shard_map/rows/pallas_call | solution.py:336
  87.7 1.4 %collective-permute-start.13 = (f32[32,128]{1,0:T(8,128)S(1)}, f32[32,128]{1,0:T(8,128)S(1)}, u32[]{:S(2)}, u32[]{:S(2)}) collective-permute-start(f32[32,128]{1,0:T(8,128)S(1)} %rows.9.refs_0_), channel_id=1, source_target_pairs={{0,16},{8,24},{16,0},{24,8},{1,17},{9,25},{17,1},{25,9},{2,18},{10... | collective-permute-start | bytes 49160 | tf_op jit(solution)/shard_map/ppermute | solution.py:359
  89.1 0.5 collective-permute-start.12
  89.5 1.4 %collective-permute-done.14.refs_3_ = f32[32,128]{1,0:T(8,128)S(1)} collective-permute-done((f32[32,128]{1,0:T(8,128)S(1)}, f32[32,128]{1,0:T(8,128)S(1)}, u32[]{:S(2)}, u32[]{:S(2)}) %collective-permute-start.14) | collective-permute-done | bytes 16416 | tf_op jit(solution)/shard_map/ppermute | solution.py:359
  90.9 0.5 collective-permute-done.13.refs_2_
  91.5 0.0 collective-permute-done.12.refs_1_
  91.5 1.3 %cells.7 = (f32[2,2,1024]{2,1,0:T(2,128)}, f32[2,2,1024]{2,1,0:T(2,128)}) custom-call(s32[3]{0:T(128)S(1)} %pad_add_fusion.place_ref, bf16[1024,2048]{1,0:T(8,128)(2,1)S(1)} %bitcast.16, f32[32,128]{1,0:T(8,128)S(1)} %rows.9.refs_0_, f32[32,128]{1,0:T(8,128)S(1)} %collective-permute-done.12.refs_1_, f32[32,128]{1,0:T(8,128)S(1)} %collective-permute-done.13.refs_2_, ...), custom_call_target="tpu_custom_call" | custom-call | tf_op jit(solution)/shard_map/cells/pallas_call | solution.py:336
  (10 shorter events, 0.0 us)
Async XLA Ops:
  0.6 3.7 %copy-start.2 = (f32[2,2,1024]{2,1,0:T(2,128)S(1)}, f32[2,2,1024]{2,1,0:T(2,128)}, u32[]{:S(2)}) copy-start(f32[2,2,1024]{2,1,0:T(2,128)} %refs_4_.1) | copy-start | bytes 49156
  4.3 16.2 %copy-start = (f32[1024]{0:T(1024)S(1)}, f32[1024]{0:T(1024)}, u32[]{:S(2)}) copy-start(f32[1024]{0:T(1024)} %param.8) | copy-start | bytes 12292
  4.3 16.1 %copy-start.1 = (f32[1024]{0:T(1024)S(1)}, f32[1024]{0:T(1024)}, u32[]{:S(2)}) copy-start(f32[1024]{0:T(1024)} %param.7) | copy-start | bytes 12292
  4.4 21.0 %copy-start.3 = (s32[2,2,1024]{2,1,0:T(2,128)S(1)}, s32[2,2,1024]{2,1,0:T(2,128)}, u32[]{:S(2)}) copy-start(s32[2,2,1024]{2,1,0:T(2,128)} %refs_6_.1) | copy-start | bytes 49156
  4.4 21.0 %copy-start.4 = (f32[2,1024]{1,0:T(2,128)S(1)}, f32[2,1024]{1,0:T(2,128)}, u32[]{:S(2)}) copy-start(f32[2,1024]{1,0:T(2,128)} %refs_5_.1) | copy-start | bytes 24580
  21.6 3.3 %collective-permute-start.2 = (f32[32,128]{1,0:T(8,128)S(1)}, f32[32,128]{1,0:T(8,128)S(1)}, u32[]{:S(2)}, u32[]{:S(2)}) collective-permute-start(f32[32,128]{1,0:T(8,128)S(1)} %rows.5.refs_0_), channel_id=1, source_target_pairs={{0,24},{8,16},{16,8},{24,0},{1,25},{9,17},{17,9},{25,1},{2,26},{10... | collective-permute-start | bytes 49160 | tf_op jit(solution)/shard_map/ppermute | solution.py:359
  21.6 3.8 %collective-permute-start.1 = (f32[32,128]{1,0:T(8,128)S(1)}, f32[32,128]{1,0:T(8,128)S(1)}, u32[]{:S(2)}, u32[]{:S(2)}) collective-permute-start(f32[32,128]{1,0:T(8,128)S(1)} %rows.5.refs_0_), channel_id=1, source_target_pairs={{0,16},{8,24},{16,0},{24,8},{1,17},{9,25},{17,1},{25,9},{2,18},{10... | collective-permute-start | bytes 49160 | tf_op jit(solution)/shard_map/ppermute | solution.py:359
  23.2 2.3 %collective-permute-start = (f32[32,128]{1,0:T(8,128)S(1)}, f32[32,128]{1,0:T(8,128)S(1)}, u32[]{:S(2)}, u32[]{:S(2)}) collective-permute-start(f32[32,128]{1,0:T(8,128)S(1)} %rows.5.refs_0_), channel_id=1, source_target_pairs={{0,8},{8,0},{16,24},{24,16},{1,9},{9,1},{17,25},{25,17},{2,10},{10... | collective-permute-start | bytes 49160 | tf_op jit(solution)/shard_map/ppermute | solution.py:359
  38.3 3.2 %collective-permute-start.5 = (f32[32,128]{1,0:T(8,128)S(1)}, f32[32,128]{1,0:T(8,128)S(1)}, u32[]{:S(2)}, u32[]{:S(2)}) collective-permute-start(f32[32,128]{1,0:T(8,128)S(1)} %rows.6.refs_0_), channel_id=1, source_target_pairs={{0,24},{8,16},{16,8},{24,0},{1,25},{9,17},{17,9},{25,1},{2,26},{10... | collective-permute-start | bytes 49160 | tf_op jit(solution)/shard_map/ppermute | solution.py:359
  38.3 3.8 %collective-permute-start.4 = (f32[32,128]{1,0:T(8,128)S(1)}, f32[32,128]{1,0:T(8,128)S(1)}, u32[]{:S(2)}, u32[]{:S(2)}) collective-permute-start(f32[32,128]{1,0:T(8,128)S(1)} %rows.6.refs_0_), channel_id=1, source_target_pairs={{0,16},{8,24},{16,0},{24,8},{1,17},{9,25},{17,1},{25,9},{2,18},{10... | collective-permute-start | bytes 49160 | tf_op jit(solution)/shard_map/ppermute | solution.py:359
  39.6 2.5 %collective-permute-start.3 = (f32[32,128]{1,0:T(8,128)S(1)}, f32[32,128]{1,0:T(8,128)S(1)}, u32[]{:S(2)}, u32[]{:S(2)}) collective-permute-start(f32[32,128]{1,0:T(8,128)S(1)} %rows.6.refs_0_), channel_id=1, source_target_pairs={{0,8},{8,0},{16,24},{24,16},{1,9},{9,1},{17,25},{25,17},{2,10},{10... | collective-permute-start | bytes 49160 | tf_op jit(solution)/shard_map/ppermute | solution.py:359
  54.7 3.2 %collective-permute-start.8 = (f32[32,128]{1,0:T(8,128)S(1)}, f32[32,128]{1,0:T(8,128)S(1)}, u32[]{:S(2)}, u32[]{:S(2)}) collective-permute-start(f32[32,128]{1,0:T(8,128)S(1)} %rows.7.refs_0_), channel_id=1, source_target_pairs={{0,24},{8,16},{16,8},{24,0},{1,25},{9,17},{17,9},{25,1},{2,26},{10... | collective-permute-start | bytes 49160 | tf_op jit(solution)/shard_map/ppermute | solution.py:359
  54.7 3.8 %collective-permute-start.7 = (f32[32,128]{1,0:T(8,128)S(1)}, f32[32,128]{1,0:T(8,128)S(1)}, u32[]{:S(2)}, u32[]{:S(2)}) collective-permute-start(f32[32,128]{1,0:T(8,128)S(1)} %rows.7.refs_0_), channel_id=1, source_target_pairs={{0,16},{8,24},{16,0},{24,8},{1,17},{9,25},{17,1},{25,9},{2,18},{10... | collective-permute-start | bytes 49160 | tf_op jit(solution)/shard_map/ppermute | solution.py:359
  56.1 2.4 %collective-permute-start.6 = (f32[32,128]{1,0:T(8,128)S(1)}, f32[32,128]{1,0:T(8,128)S(1)}, u32[]{:S(2)}, u32[]{:S(2)}) collective-permute-start(f32[32,128]{1,0:T(8,128)S(1)} %rows.7.refs_0_), channel_id=1, source_target_pairs={{0,8},{8,0},{16,24},{24,16},{1,9},{9,1},{17,25},{25,17},{2,10},{10... | collective-permute-start | bytes 49160 | tf_op jit(solution)/shard_map/ppermute | solution.py:359
  71.2 3.2 %collective-permute-start.11 = (f32[32,128]{1,0:T(8,128)S(1)}, f32[32,128]{1,0:T(8,128)S(1)}, u32[]{:S(2)}, u32[]{:S(2)}) collective-permute-start(f32[32,128]{1,0:T(8,128)S(1)} %rows.8.refs_0_), channel_id=1, source_target_pairs={{0,24},{8,16},{16,8},{24,0},{1,25},{9,17},{17,9},{25,1},{2,26},{10... | collective-permute-start | bytes 49160 | tf_op jit(solution)/shard_map/ppermute | solution.py:359
  71.2 3.8 %collective-permute-start.10 = (f32[32,128]{1,0:T(8,128)S(1)}, f32[32,128]{1,0:T(8,128)S(1)}, u32[]{:S(2)}, u32[]{:S(2)}) collective-permute-start(f32[32,128]{1,0:T(8,128)S(1)} %rows.8.refs_0_), channel_id=1, source_target_pairs={{0,16},{8,24},{16,0},{24,8},{1,17},{9,25},{17,1},{25,9},{2,18},{10... | collective-permute-start | bytes 49160 | tf_op jit(solution)/shard_map/ppermute | solution.py:359
  72.5 2.5 %collective-permute-start.9 = (f32[32,128]{1,0:T(8,128)S(1)}, f32[32,128]{1,0:T(8,128)S(1)}, u32[]{:S(2)}, u32[]{:S(2)}) collective-permute-start(f32[32,128]{1,0:T(8,128)S(1)} %rows.8.refs_0_), channel_id=1, source_target_pairs={{0,8},{8,0},{16,24},{24,16},{1,9},{9,1},{17,25},{25,17},{2,10},{10... | collective-permute-start | bytes 49160 | tf_op jit(solution)/shard_map/ppermute | solution.py:359
  87.7 3.2 %collective-permute-start.14 = (f32[32,128]{1,0:T(8,128)S(1)}, f32[32,128]{1,0:T(8,128)S(1)}, u32[]{:S(2)}, u32[]{:S(2)}) collective-permute-start(f32[32,128]{1,0:T(8,128)S(1)} %rows.9.refs_0_), channel_id=1, source_target_pairs={{0,24},{8,16},{16,8},{24,0},{1,25},{9,17},{17,9},{25,1},{2,26},{10... | collective-permute-start | bytes 49160 | tf_op jit(solution)/shard_map/ppermute | solution.py:359
  87.7 3.8 %collective-permute-start.13 = (f32[32,128]{1,0:T(8,128)S(1)}, f32[32,128]{1,0:T(8,128)S(1)}, u32[]{:S(2)}, u32[]{:S(2)}) collective-permute-start(f32[32,128]{1,0:T(8,128)S(1)} %rows.9.refs_0_), channel_id=1, source_target_pairs={{0,16},{8,24},{16,0},{24,8},{1,17},{9,25},{17,1},{25,9},{2,18},{10... | collective-permute-start | bytes 49160 | tf_op jit(solution)/shard_map/ppermute | solution.py:359
  89.1 2.4 %collective-permute-start.12 = (f32[32,128]{1,0:T(8,128)S(1)}, f32[32,128]{1,0:T(8,128)S(1)}, u32[]{:S(2)}, u32[]{:S(2)}) collective-permute-start(f32[32,128]{1,0:T(8,128)S(1)} %rows.9.refs_0_), channel_id=1, source_target_pairs={{0,8},{8,0},{16,24},{24,16},{1,9},{9,1},{17,25},{25,17},{2,10},{10... | collective-permute-start | bytes 49160 | tf_op jit(solution)/shard_map/ppermute | solution.py:359

commit v4 on v3

--- a/solution.py
+++ b/solution.py
@@ -97,9 +97,9 @@
     )
 
 
-def rows_between(plane, low, count):
-    line = lax.broadcasted_iota(jnp.int32, plane.shape, 0)
-    return (line >= low) & (line < low + count)
+def where_block(shape, count, block, members):
+    line = lax.broadcasted_iota(jnp.int32, shape, 0)
+    return line // count == lax.rem(block, jnp.int32(members))
 
 
 def share_of(planes, member, members):
@@ -107,8 +107,8 @@
     count = tall // members
     out = jnp.zeros_like(planes[0])
     for n, plane in enumerate(planes):
-        moved = pltpu.roll(plane, (n * count - member * count + tall) % tall, 0)
-        out = jnp.where(rows_between(plane, n * count, count), moved, out)
+        moved = pltpu.roll(plane, n * count, 0) if n else plane
+        out = jnp.where(where_block(plane.shape, count, member + n, members), moved, out)
     return out
 
 
@@ -117,16 +117,17 @@
     count = tall // members
     out = jnp.zeros_like(shares[0][1])
     for member, share in shares:
-        moved = pltpu.roll(share, (member * count - n * count + tall) % tall, 0)
-        out = jnp.where(rows_between(share, member * count, count), moved, out)
-    return out
-
-
-def send_rows(place_ref, matrix_ref, field, lines, out_ref, members):
+        out = jnp.where(where_block(share.shape, count, member + n, members), share, out)
+    return pltpu.roll(out, tall - n * count, 0) if n else out
+
+
+def send_rows(matrix_ref, field, lines, out_ref):
     owners = out_ref.shape[0]
     rows = matrix_ref.shape[0]
     tall = field[0][0].shape[0]
-    gravity_rows = place_ref[1] < place_ref[2]
+    block = lax.axis_index("dp")
+    members = lax.axis_size("dp")
+    gravity_rows = block < members * 3 // 4
     chosen = [jnp.where(gravity_rows, d, s) for d, s in zip(field[0], field[1])]
     vector = spread(chosen, LANES).astype(jnp.bfloat16)
     eye = lax.broadcasted_iota(jnp.int32, (LANES, LANES), 0) == lax.broadcasted_iota(
@@ -142,7 +143,7 @@
         for b in range(rows // LANES)
     ]
     edges = [field[0][0], field[1][0], field[0][-1], field[1][-1]]
-    pieces.append(share_of(edges, place_ref[1], members))
+    pieces.append(share_of(edges, block, members))
     pieces += lines
     pieces.append(jnp.zeros((SUBLANES - len(lines), LANES), jnp.float32))
     message = jnp.concatenate(pieces, axis=0)
@@ -169,14 +170,16 @@
                 ref[f, i : i + 1, t * LANES : (t + 1) * LANES] = field[f][i][t : t + 1]
 
 
-def start_kernel(place_ref, matrix_ref, model_ref, out_ref, *, members):
-    send_rows(place_ref, matrix_ref, load_wide(model_ref), [], out_ref, members)
+def start_kernel(matrix_ref, model_ref, out_ref):
+    send_rows(matrix_ref, load_wide(model_ref), [], out_ref)
 
 
 def rows_kernel(
-    place_ref, matrix_ref, got_ref, weight_ref, observed_ref, out_ref, *, subtract, members, tall
+    matrix_ref, got_ref, weight_ref, observed_ref, out_ref, *, subtract, tall
 ):
-    rank = place_ref[0]
+    rank = lax.axis_index("mp")
+    member = lax.axis_index("dp")
+    members = lax.axis_size("dp")
     owners = got_ref.shape[0]
     rows, cells = matrix_ref.shape
     blocks = rows // LANES
@@ -190,13 +193,14 @@
     vector = spread([scaled], 2 * SUBLANES).astype(jnp.bfloat16)
     columns = jnp.dot(vector, matrix_ref[...], preferred_element_type=jnp.float32)
     pieces = [columns[0:1, t * LANES : (t + 1) * LANES] for t in range(cells // LANES)]
-    half = 2 * (tall // members)
+    count = tall // members
     shares = [got_ref[j, blocks : blocks + tall] for j in range(owners)]
-    lower = rows_between(shares[0], 0, half)
-    upper = rows_between(shares[0], half, half)
+    held = [where_block(shares[0].shape, count, member + n, members) for n in range(4)]
+    lower = held[0] | held[1]
+    upper = held[2] | held[3]
     cross = None
     for j in range(owners - 1):
-        term = shares[j] * pltpu.roll(shares[j + 1], half, 0)
+        term = shares[j] * pltpu.roll(shares[j + 1], 2 * count, 0)
         cross = term if cross is None else cross + term
     cross = jnp.sum(jnp.where(upper, cross, 0.0), axis=0, keepdims=True)
     weighed = weighed - 2.0 * SMOOTHING * cross
@@ -208,12 +212,12 @@
     out_ref[...] = jnp.concatenate(pieces, axis=0)
 
 
-def gathered(place_ref, part_refs, inner_ref, mask_ref):
+def gathered(part_refs, inner_ref, mask_ref):
     layers, tall = inner_ref.shape[1:3]
     cells = layers * tall
     members = len(part_refs)
-    sources = [place_ref[1] ^ s for s in range(members)]
-    gravity = [q < place_ref[2] for q in sources]
+    sources = [lax.axis_index("dp") ^ s for s in range(members)]
+    gravity = [q < members * 3 // 4 for q in sources]
     parts = [ref[0:cells] for ref in part_refs]
     data = [
         tree_sum([jnp.where(g, p, 0.0) for g, p in zip(gravity, parts)]),
@@ -234,7 +238,7 @@
     return image
 
 
-def first_kernel(place_ref, matrix_ref, *refs, count):
+def first_kernel(matrix_ref, *refs, count):
     part_refs = refs[:count]
     model_ref, weight_ref, active_ref, out_ref, residual_ref, inner_ref = refs[count : count + 6]
     smooth_ref, mask_ref, held = refs[count + 6 :]
@@ -244,16 +248,16 @@
         smooth_ref[i] = smooth_weight[i]
     store(mask_ref, mapped(lambda a: 1.0 - a.astype(jnp.float32), load_wide(active_ref)))
     store(held, operate_inner(load_wide(model_ref), smooth_weight))
-    image = gathered(place_ref, part_refs, held, mask_ref)
+    image = gathered(part_refs, held, mask_ref)
     residual = mapped(lambda a: -a, image)
     inner = operate_inner(residual, smooth_weight)
     store(residual_ref, residual)
     store(inner_ref, inner)
     lines = [dot_line(residual, residual), dot_line(residual, inner)]
-    send_rows(place_ref, matrix_ref, residual, lines, out_ref, count)
-
-
-def cells_kernel(place_ref, matrix_ref, *refs, count, base, begin, final):
+    send_rows(matrix_ref, residual, lines, out_ref)
+
+
+def cells_kernel(matrix_ref, *refs, count, base, begin, final):
     part_refs = refs[:count]
     got_ref, smooth_ref, mask_ref, residual_in, inner_in = refs[count : count + 5]
     refs = refs[count + 5 :]
@@ -265,7 +269,7 @@
     layers, tall = inner_in.shape[1:3]
     cells = layers * tall
     residual = load(residual_in)
-    image = gathered(place_ref, part_refs, inner_in, mask_ref)
+    image = gathered(part_refs, inner_in, mask_ref)
     at = base + tall
     sums = got_ref[0, at : at + SUBLANES]
     for j in range(1, owners):
@@ -302,7 +306,7 @@
     inner = operate_inner(residual, [smooth_ref[i] for i in range(layers)])
     store(inner_ref, inner)
     lines = [dot_line(residual, residual), dot_line(residual, inner), dot_line(residual, imaged)]
-    send_rows(place_ref, matrix_ref, residual, lines, out_ref, count)
+    send_rows(matrix_ref, residual, lines, out_ref)
 
 
 def local(sensitivity, observed, row_weight, model, smooth_weight, active):
@@ -312,9 +316,6 @@
     tall = width // LANES
     owners = lax.axis_size("mp")
     blocks = lax.axis_size("dp")
-    place = jnp.stack(
-        [lax.axis_index("mp"), lax.axis_index("dp"), jnp.int32(blocks * 3 // 4)]
-    ).astype(jnp.int32)
     base = rows // LANES
 
     weight = row_weight.reshape(base, LANES)
@@ -328,7 +329,6 @@
     message = jax.ShapeDtypeStruct((owners, base + tall + SUBLANES, LANES), jnp.float32)
     columns = jax.ShapeDtypeStruct(((layers + 1) * tall + SUBLANES, LANES), jnp.float32)
     norms = jax.ShapeDtypeStruct((2, LANES), jnp.float32)
-    smem = pl.BlockSpec(memory_space=pltpu.SMEM)
     vmem = pl.BlockSpec(memory_space=pltpu.VMEM)
 
     def call(kernel, out_shape, *operands, name, scratch=()):
@@ -336,19 +336,19 @@
         return pl.pallas_call(
             kernel,
             out_shape=out_shape,
-            in_specs=[smem] + [vmem] * (1 + len(operands)),
+            in_specs=[vmem] * (1 + len(operands)),
             out_specs=jax.tree.map(lambda _: vmem, out_shape),
             scratch_shapes=scratch,
             compiler_params=pltpu.CompilerParams(vmem_limit_bytes=KERNEL_VMEM),
             name=name,
-        )(place, held, *operands)
+        )(held, *operands)
 
     def across(sent):
         return lax.all_to_all(sent, "mp", 0, 0, tiled=True)
 
     def along(got, subtract):
         sent = call(
-            functools.partial(rows_kernel, subtract=subtract, members=blocks, tall=tall),
+            functools.partial(rows_kernel, subtract=subtract, tall=tall),
             columns,
             got,
             weight,
@@ -360,7 +360,7 @@
             for s in range(1, blocks)
         ]
 
-    got = across(call(functools.partial(start_kernel, members=blocks), message, model, name="start"))
+    got = across(call(start_kernel, message, model, name="start"))
     parts = along(got, True)
     sent, residual, inner, smooth, mask = call(
         functools.partial(first_kernel, count=blocks),

time: 93.1 us -> 87.2 us (0.937)
  Pallas kernels: 16.8 us -> 10.8 us
    pallas_call x11, Pallas kernels: 16.8 us -> 10.8 us  [call(): pl.pallas_call(kernel, out_shape=out_shape, in_specs=[vmem] * (1 + len(op...]
where the time goes in v4:
time: 87.2 us; the launch traced here: 86.8 us
  blocking collectives  52.6 us (60%)
  Pallas kernels  10.8 us (12%)
  waiting for transfers between devices  9.54 us (11%)
  starting transfers between devices  9.38 us (11%)
  local copies, waits for them, and re-layouts  3.65 us (4%)
    all_to_all x5, blocking collectives, across(): return lax.all_to_all(sent, 'mp', 0, 0, tiled=True)  52.6 us
    pallas_call x11, Pallas kernels, call(): pl.pallas_call(kernel, out_shape=out_shape, in_specs=[vmem] * (1 + len(op...  10.8 us
    ppermute x15, waiting for transfers between devices, along(): lax.ppermute(sent, 'dp', [(i, i ^ s) for i in range(blocks)])  9.54 us
    ppermute x15, starting transfers between devices, along(): lax.ppermute(sent, 'dp', [(i, i ^ s) for i in range(blocks)])  9.38 us
    unnamed x11, local copies, waits for them, and re-layouts  3.65 us
  transfers between devices with their start and end apart: 15, of which 10 were waited for; matrix products, arithmetic and copies ran while one was open for 0% of the time, Pallas kernels for 0%

profile of v4, /device:TPU:0, one launch (start us, length us, event | category | flops | bytes accessed | tf_op | source)
XLA Modules:
  0.0 86.8 jit_solution(13694186484290963029)
XLA Ops:
  0.6 3.6 %copy.8 = bf16[128,8,2,1024]{3,1,2,0:T(8,128)(2,1)S(1)} copy(bf16[128,8,2,1024]{3,2,1,0:T(2,128)(2,1)} %bitcast.25) | data formatting | bytes 8388608
  4.3 0.0 copy-start
  4.3 0.0 copy-start.1
  4.3 0.0 copy-start.3
  4.3 0.0 copy-start.4
  4.3 1.3 %start.1 = f32[8,24,128]{2,1,0:T(8,128)S(1)} custom-call(bf16[1024,2048]{1,0:T(8,128)(2,1)S(1)} %bitcast.4, f32[2,2,1024]{2,1,0:T(2,128)S(1)} %copy-done.2), custom_call_target="tpu_custom_call" | custom-call | tf_op jit(solution)/shard_map/start/pallas_call | solution.py:336
  5.6 14.2 %all_to_all.25.got_ref = f32[8,24,128]{2,1,0:T(8,128)S(1)} all-to-all(f32[8,24,128]{2,1,0:T(8,128)S(1)} %start.1), channel_id=1, replica_groups=mesh['dp'=4,'mp'=8] {'mp'}, dimensions={0} | all-to-all | bytes 196608 | tf_op jit(solution)/shard_map/all_to_all | solution.py:347
  19.8 0.7 rows.5.refs_0_
  20.5 0.0 collective-permute-start.2
  20.5 1.5 %collective-permute-start.1 = (f32[32,128]{1,0:T(8,128)S(1)}, f32[32,128]{1,0:T(8,128)S(1)}, u32[]{:S(2)}, u32[]{:S(2)}) collective-permute-start(f32[32,128]{1,0:T(8,128)S(1)} %rows.5.refs_0_), channel_id=1, source_target_pairs={{0,16},{8,24},{16,0},{24,8},{1,17},{9,25},{17,1},{25,9},{2,18},{10... | collective-permute-start | bytes 49160 | tf_op jit(solution)/shard_map/ppermute | solution.py:359
  22.0 0.3 collective-permute-start
  22.4 1.4 %collective-permute-done.2.refs_3_ = f32[32,128]{1,0:T(8,128)S(1)} collective-permute-done((f32[32,128]{1,0:T(8,128)S(1)}, f32[32,128]{1,0:T(8,128)S(1)}, u32[]{:S(2)}, u32[]{:S(2)}) %collective-permute-start.2) | collective-permute-done | bytes 16416 | tf_op jit(solution)/shard_map/ppermute | solution.py:359
  23.8 0.5 collective-permute-done.1.refs_2_
  24.3 0.0 collective-permute-done.refs_1_
  24.3 1.4 %first.1 = (f32[8,24,128]{2,1,0:T(8,128)S(1)}, f32[2,2,8,128]{3,2,1,0:T(8,128)S(1)}, f32[2,2,8,128]{3,2,1,0:T(8,128)S(1)}, f32[2,8,128]{2,1,0:T(8,128)S(1)}, f32[2,2,8,128]{3,2,1,0:T(8,128)S(1)}) custom-call(bf16[1024,2048]{1,0:T(8,128)(2,1)S(1)} %bitcast.6, f32[32,128]{1,0:T(8,128)S(1)} %rows.5.refs_0_, f32[32,128]{1,0:T(8,128)S(1)} %collective-permute-done.refs_1_, ...), custom_call_target="tpu_custom_call" | custom-call | tf_op jit(solution)/shard_map/first/pallas_call | solution.py:336
  25.7 9.7 %all_to_all.26.got_ref.refs_4_ = f32[8,24,128]{2,1,0:T(8,128)S(1)} all-to-all(f32[8,24,128]{2,1,0:T(8,128)S(1)} %get-tuple-element.28), channel_id=1, replica_groups=mesh['dp'=4,'mp'=8] {'mp'}, dimensions={0} | all-to-all | bytes 196608 | tf_op jit(solution)/shard_map/all_to_all | solution.py:347
  35.4 0.7 rows.6.refs_0_
  36.1 0.0 collective-permute-start.5
  36.1 1.3 %collective-permute-start.4 = (f32[32,128]{1,0:T(8,128)S(1)}, f32[32,128]{1,0:T(8,128)S(1)}, u32[]{:S(2)}, u32[]{:S(2)}) collective-permute-start(f32[32,128]{1,0:T(8,128)S(1)} %rows.6.refs_0_), channel_id=1, source_target_pairs={{0,16},{8,24},{16,0},{24,8},{1,17},{9,25},{17,1},{25,9},{2,18},{10... | collective-permute-start | bytes 49160 | tf_op jit(solution)/shard_map/ppermute | solution.py:359
  37.3 0.6 collective-permute-start.3
  37.9 1.3 %collective-permute-done.5.refs_3_ = f32[32,128]{1,0:T(8,128)S(1)} collective-permute-done((f32[32,128]{1,0:T(8,128)S(1)}, f32[32,128]{1,0:T(8,128)S(1)}, u32[]{:S(2)}, u32[]{:S(2)}) %collective-permute-start.5) | collective-permute-done | bytes 16416 | tf_op jit(solution)/shard_map/ppermute | solution.py:359
  39.2 0.6 collective-permute-done.4.refs_2_
  39.8 1.4 %cells.4 = (f32[2,2,8,128]{3,2,1,0:T(8,128)S(1)}, f32[2,2,8,128]{3,2,1,0:T(8,128)S(1)}, f32[2,2,8,128]{3,2,1,0:T(8,128)S(1)}, f32[2,2,8,128]{3,2,1,0:T(8,128)S(1...) custom-call(bf16[1024,2048]{1,0:T(8,128)(2,1)S(1)} %bitcast.8, ...), custom_call_target="tpu_custom_call" | custom-call | tf_op jit(solution)/shard_map/cells/pallas_call | solution.py:336
  41.2 9.5 %all_to_all.27.got_ref.refs_4_ = f32[8,24,128]{2,1,0:T(8,128)S(1)} all-to-all(f32[8,24,128]{2,1,0:T(8,128)S(1)} %get-tuple-element.33), channel_id=1, replica_groups=mesh['dp'=4,'mp'=8] {'mp'}, dimensions={0} | all-to-all | bytes 196608 | tf_op jit(solution)/shard_map/all_to_all | solution.py:347
  50.7 0.7 rows.7.refs_0_
  51.4 1.4 %collective-permute-start.7 = (f32[32,128]{1,0:T(8,128)S(1)}, f32[32,128]{1,0:T(8,128)S(1)}, u32[]{:S(2)}, u32[]{:S(2)}) collective-permute-start(f32[32,128]{1,0:T(8,128)S(1)} %rows.7.refs_0_), channel_id=1, source_target_pairs={{0,16},{8,24},{16,0},{24,8},{1,17},{9,25},{17,1},{25,9},{2,18},{10... | collective-permute-start | bytes 49160 | tf_op jit(solution)/shard_map/ppermute | solution.py:359
  52.8 0.5 collective-permute-start.6
  53.3 1.4 %collective-permute-done.8.refs_3_ = f32[32,128]{1,0:T(8,128)S(1)} collective-permute-done((f32[32,128]{1,0:T(8,128)S(1)}, f32[32,128]{1,0:T(8,128)S(1)}, u32[]{:S(2)}, u32[]{:S(2)}) %collective-permute-start.8) | collective-permute-done | bytes 16416 | tf_op jit(solution)/shard_map/ppermute | solution.py:359
  54.6 0.5 collective-permute-done.7.refs_2_
  55.2 1.4 %cells.5 = (f32[2,2,8,128]{3,2,1,0:T(8,128)S(1)}, f32[2,2,8,128]{3,2,1,0:T(8,128)S(1)}, f32[2,2,8,128]{3,2,1,0:T(8,128)S(1)}, f32[2,2,8,128]{3,2,1,0:T(8,128)S(1...) custom-call(bf16[1024,2048]{1,0:T(8,128)(2,1)S(1)} %bitcast.10, ...), custom_call_target="tpu_custom_call" | custom-call | tf_op jit(solution)/shard_map/cells/pallas_call | solution.py:336
  56.6 9.6 %all_to_all.28.got_ref.refs_4_ = f32[8,24,128]{2,1,0:T(8,128)S(1)} all-to-all(f32[8,24,128]{2,1,0:T(8,128)S(1)} %get-tuple-element.40), channel_id=1, replica_groups=mesh['dp'=4,'mp'=8] {'mp'}, dimensions={0} | all-to-all | bytes 196608 | tf_op jit(solution)/shard_map/all_to_all | solution.py:347
  66.2 0.7 rows.8.refs_0_
  66.8 0.0 collective-permute-start.11
  66.8 1.3 %collective-permute-start.10 = (f32[32,128]{1,0:T(8,128)S(1)}, f32[32,128]{1,0:T(8,128)S(1)}, u32[]{:S(2)}, u32[]{:S(2)}) collective-permute-start(f32[32,128]{1,0:T(8,128)S(1)} %rows.8.refs_0_), channel_id=1, source_target_pairs={{0,16},{8,24},{16,0},{24,8},{1,17},{9,25},{17,1},{25,9},{2,18},{10... | collective-permute-start | bytes 49160 | tf_op jit(solution)/shard_map/ppermute | solution.py:359
  68.1 0.6 collective-permute-start.9
  68.7 1.3 %collective-permute-done.11.refs_3_ = f32[32,128]{1,0:T(8,128)S(1)} collective-permute-done((f32[32,128]{1,0:T(8,128)S(1)}, f32[32,128]{1,0:T(8,128)S(1)}, u32[]{:S(2)}, u32[]{:S(2)}) %collective-permute-start.11) | collective-permute-done | bytes 16416 | tf_op jit(solution)/shard_map/ppermute | solution.py:359
  70.0 0.6 collective-permute-done.10.refs_2_
  70.6 0.0 collective-permute-done.9.refs_1_
  70.6 1.4 %cells.6 = (f32[2,2,8,128]{3,2,1,0:T(8,128)S(1)}, f32[2,2,8,128]{3,2,1,0:T(8,128)S(1)}, f32[2,2,8,128]{3,2,1,0:T(8,128)S(1)}, f32[2,2,8,128]{3,2,1,0:T(8,128)S(1...) custom-call(bf16[1024,2048]{1,0:T(8,128)(2,1)S(1)} %bitcast.12, ...), custom_call_target="tpu_custom_call" | custom-call | tf_op jit(solution)/shard_map/cells/pallas_call | solution.py:336
  72.0 9.5 %all_to_all.29.got_ref.refs_4_ = f32[8,24,128]{2,1,0:T(8,128)S(1)} all-to-all(f32[8,24,128]{2,1,0:T(8,128)S(1)} %get-tuple-element.47), channel_id=1, replica_groups=mesh['dp'=4,'mp'=8] {'mp'}, dimensions={0} | all-to-all | bytes 196608 | tf_op jit(solution)/shard_map/all_to_all | solution.py:347
  81.6 0.7 rows.9.refs_0_
  82.2 0.0 collective-permute-start.14
  82.2 1.4 %collective-permute-start.13 = (f32[32,128]{1,0:T(8,128)S(1)}, f32[32,128]{1,0:T(8,128)S(1)}, u32[]{:S(2)}, u32[]{:S(2)}) collective-permute-start(f32[32,128]{1,0:T(8,128)S(1)} %rows.9.refs_0_), channel_id=1, source_target_pairs={{0,16},{8,24},{16,0},{24,8},{1,17},{9,25},{17,1},{25,9},{2,18},{10... | collective-permute-start | bytes 49160 | tf_op jit(solution)/shard_map/ppermute | solution.py:359
  83.6 0.5 collective-permute-start.12
  84.1 1.4 %collective-permute-done.14.refs_3_ = f32[32,128]{1,0:T(8,128)S(1)} collective-permute-done((f32[32,128]{1,0:T(8,128)S(1)}, f32[32,128]{1,0:T(8,128)S(1)}, u32[]{:S(2)}, u32[]{:S(2)}) %collective-permute-start.14) | collective-permute-done | bytes 16416 | tf_op jit(solution)/shard_map/ppermute | solution.py:359
  85.5 0.5 collective-permute-done.13.refs_2_
  86.0 0.0 collective-permute-done.12.refs_1_
  86.0 0.8 cells.7
  (9 shorter events, 0.0 us)
Async XLA Ops:
  0.6 3.7 %copy-start.2 = (f32[2,2,1024]{2,1,0:T(2,128)S(1)}, f32[2,2,1024]{2,1,0:T(2,128)}, u32[]{:S(2)}) copy-start(f32[2,2,1024]{2,1,0:T(2,128)} %refs_4_.1) | copy-start | bytes 49156
  4.3 15.6 %copy-start = (f32[1024]{0:T(1024)S(1)}, f32[1024]{0:T(1024)}, u32[]{:S(2)}) copy-start(f32[1024]{0:T(1024)} %param.8) | copy-start | bytes 12292
  4.3 15.6 %copy-start.1 = (f32[1024]{0:T(1024)S(1)}, f32[1024]{0:T(1024)}, u32[]{:S(2)}) copy-start(f32[1024]{0:T(1024)} %param.7) | copy-start | bytes 12292
  4.3 20.0 %copy-start.3 = (s32[2,2,1024]{2,1,0:T(2,128)S(1)}, s32[2,2,1024]{2,1,0:T(2,128)}, u32[]{:S(2)}) copy-start(s32[2,2,1024]{2,1,0:T(2,128)} %refs_6_.1) | copy-start | bytes 49156
  4.3 20.0 %copy-start.4 = (f32[2,1024]{1,0:T(2,128)S(1)}, f32[2,1024]{1,0:T(2,128)}, u32[]{:S(2)}) copy-start(f32[2,1024]{1,0:T(2,128)} %refs_5_.1) | copy-start | bytes 24580
  20.5 3.3 %collective-permute-start.2 = (f32[32,128]{1,0:T(8,128)S(1)}, f32[32,128]{1,0:T(8,128)S(1)}, u32[]{:S(2)}, u32[]{:S(2)}) collective-permute-start(f32[32,128]{1,0:T(8,128)S(1)} %rows.5.refs_0_), channel_id=1, source_target_pairs={{0,24},{8,16},{16,8},{24,0},{1,25},{9,17},{17,9},{25,1},{2,26},{10... | collective-permute-start | bytes 49160 | tf_op jit(solution)/shard_map/ppermute | solution.py:359
  20.5 3.8 %collective-permute-start.1 = (f32[32,128]{1,0:T(8,128)S(1)}, f32[32,128]{1,0:T(8,128)S(1)}, u32[]{:S(2)}, u32[]{:S(2)}) collective-permute-start(f32[32,128]{1,0:T(8,128)S(1)} %rows.5.refs_0_), channel_id=1, source_target_pairs={{0,16},{8,24},{16,0},{24,8},{1,17},{9,25},{17,1},{25,9},{2,18},{10... | collective-permute-start | bytes 49160 | tf_op jit(solution)/shard_map/ppermute | solution.py:359
  22.0 2.3 %collective-permute-start = (f32[32,128]{1,0:T(8,128)S(1)}, f32[32,128]{1,0:T(8,128)S(1)}, u32[]{:S(2)}, u32[]{:S(2)}) collective-permute-start(f32[32,128]{1,0:T(8,128)S(1)} %rows.5.refs_0_), channel_id=1, source_target_pairs={{0,8},{8,0},{16,24},{24,16},{1,9},{9,1},{17,25},{25,17},{2,10},{10... | collective-permute-start | bytes 49160 | tf_op jit(solution)/shard_map/ppermute | solution.py:359
  36.1 3.2 %collective-permute-start.5 = (f32[32,128]{1,0:T(8,128)S(1)}, f32[32,128]{1,0:T(8,128)S(1)}, u32[]{:S(2)}, u32[]{:S(2)}) collective-permute-start(f32[32,128]{1,0:T(8,128)S(1)} %rows.6.refs_0_), channel_id=1, source_target_pairs={{0,24},{8,16},{16,8},{24,0},{1,25},{9,17},{17,9},{25,1},{2,26},{10... | collective-permute-start | bytes 49160 | tf_op jit(solution)/shard_map/ppermute | solution.py:359
  36.1 3.8 %collective-permute-start.4 = (f32[32,128]{1,0:T(8,128)S(1)}, f32[32,128]{1,0:T(8,128)S(1)}, u32[]{:S(2)}, u32[]{:S(2)}) collective-permute-start(f32[32,128]{1,0:T(8,128)S(1)} %rows.6.refs_0_), channel_id=1, source_target_pairs={{0,16},{8,24},{16,0},{24,8},{1,17},{9,25},{17,1},{25,9},{2,18},{10... | collective-permute-start | bytes 49160 | tf_op jit(solution)/shard_map/ppermute | solution.py:359
  37.3 2.5 %collective-permute-start.3 = (f32[32,128]{1,0:T(8,128)S(1)}, f32[32,128]{1,0:T(8,128)S(1)}, u32[]{:S(2)}, u32[]{:S(2)}) collective-permute-start(f32[32,128]{1,0:T(8,128)S(1)} %rows.6.refs_0_), channel_id=1, source_target_pairs={{0,8},{8,0},{16,24},{24,16},{1,9},{9,1},{17,25},{25,17},{2,10},{10... | collective-permute-start | bytes 49160 | tf_op jit(solution)/shard_map/ppermute | solution.py:359
  51.4 3.2 %collective-permute-start.8 = (f32[32,128]{1,0:T(8,128)S(1)}, f32[32,128]{1,0:T(8,128)S(1)}, u32[]{:S(2)}, u32[]{:S(2)}) collective-permute-start(f32[32,128]{1,0:T(8,128)S(1)} %rows.7.refs_0_), channel_id=1, source_target_pairs={{0,24},{8,16},{16,8},{24,0},{1,25},{9,17},{17,9},{25,1},{2,26},{10... | collective-permute-start | bytes 49160 | tf_op jit(solution)/shard_map/ppermute | solution.py:359
  51.4 3.8 %collective-permute-start.7 = (f32[32,128]{1,0:T(8,128)S(1)}, f32[32,128]{1,0:T(8,128)S(1)}, u32[]{:S(2)}, u32[]{:S(2)}) collective-permute-start(f32[32,128]{1,0:T(8,128)S(1)} %rows.7.refs_0_), channel_id=1, source_target_pairs={{0,16},{8,24},{16,0},{24,8},{1,17},{9,25},{17,1},{25,9},{2,18},{10... | collective-permute-start | bytes 49160 | tf_op jit(solution)/shard_map/ppermute | solution.py:359
  52.8 2.4 %collective-permute-start.6 = (f32[32,128]{1,0:T(8,128)S(1)}, f32[32,128]{1,0:T(8,128)S(1)}, u32[]{:S(2)}, u32[]{:S(2)}) collective-permute-start(f32[32,128]{1,0:T(8,128)S(1)} %rows.7.refs_0_), channel_id=1, source_target_pairs={{0,8},{8,0},{16,24},{24,16},{1,9},{9,1},{17,25},{25,17},{2,10},{10... | collective-permute-start | bytes 49160 | tf_op jit(solution)/shard_map/ppermute | solution.py:359
  66.8 3.2 %collective-permute-start.11 = (f32[32,128]{1,0:T(8,128)S(1)}, f32[32,128]{1,0:T(8,128)S(1)}, u32[]{:S(2)}, u32[]{:S(2)}) collective-permute-start(f32[32,128]{1,0:T(8,128)S(1)} %rows.8.refs_0_), channel_id=1, source_target_pairs={{0,24},{8,16},{16,8},{24,0},{1,25},{9,17},{17,9},{25,1},{2,26},{10... | collective-permute-start | bytes 49160 | tf_op jit(solution)/shard_map/ppermute | solution.py:359
  66.8 3.8 %collective-permute-start.10 = (f32[32,128]{1,0:T(8,128)S(1)}, f32[32,128]{1,0:T(8,128)S(1)}, u32[]{:S(2)}, u32[]{:S(2)}) collective-permute-start(f32[32,128]{1,0:T(8,128)S(1)} %rows.8.refs_0_), channel_id=1, source_target_pairs={{0,16},{8,24},{16,0},{24,8},{1,17},{9,25},{17,1},{25,9},{2,18},{10... | collective-permute-start | bytes 49160 | tf_op jit(solution)/shard_map/ppermute | solution.py:359
  68.1 2.5 %collective-permute-start.9 = (f32[32,128]{1,0:T(8,128)S(1)}, f32[32,128]{1,0:T(8,128)S(1)}, u32[]{:S(2)}, u32[]{:S(2)}) collective-permute-start(f32[32,128]{1,0:T(8,128)S(1)} %rows.8.refs_0_), channel_id=1, source_target_pairs={{0,8},{8,0},{16,24},{24,16},{1,9},{9,1},{17,25},{25,17},{2,10},{10... | collective-permute-start | bytes 49160 | tf_op jit(solution)/shard_map/ppermute | solution.py:359
  82.2 3.2 %collective-permute-start.14 = (f32[32,128]{1,0:T(8,128)S(1)}, f32[32,128]{1,0:T(8,128)S(1)}, u32[]{:S(2)}, u32[]{:S(2)}) collective-permute-start(f32[32,128]{1,0:T(8,128)S(1)} %rows.9.refs_0_), channel_id=1, source_target_pairs={{0,24},{8,16},{16,8},{24,0},{1,25},{9,17},{17,9},{25,1},{2,26},{10... | collective-permute-start | bytes 49160 | tf_op jit(solution)/shard_map/ppermute | solution.py:359
  82.2 3.8 %collective-permute-start.13 = (f32[32,128]{1,0:T(8,128)S(1)}, f32[32,128]{1,0:T(8,128)S(1)}, u32[]{:S(2)}, u32[]{:S(2)}) collective-permute-start(f32[32,128]{1,0:T(8,128)S(1)} %rows.9.refs_0_), channel_id=1, source_target_pairs={{0,16},{8,24},{16,0},{24,8},{1,17},{9,25},{17,1},{25,9},{2,18},{10... | collective-permute-start | bytes 49160 | tf_op jit(solution)/shard_map/ppermute | solution.py:359
  83.6 2.4 %collective-permute-start.12 = (f32[32,128]{1,0:T(8,128)S(1)}, f32[32,128]{1,0:T(8,128)S(1)}, u32[]{:S(2)}, u32[]{:S(2)}) collective-permute-start(f32[32,128]{1,0:T(8,128)S(1)} %rows.9.refs_0_), channel_id=1, source_target_pairs={{0,8},{8,0},{16,24},{24,16},{1,9},{9,1},{17,25},{25,17},{2,10},{10... | collective-permute-start | bytes 49160 | tf_op jit(solution)/shard_map/ppermute | solution.py:359

commit v5 on v4

--- a/solution.py
+++ b/solution.py
@@ -121,29 +121,31 @@
     return pltpu.roll(out, tall - n * count, 0) if n else out
 
 
-def send_rows(matrix_ref, field, lines, out_ref):
+def send_rows(matrix_ref, field, lines, out_ref, ready=None):
     owners = out_ref.shape[0]
     rows = matrix_ref.shape[0]
     tall = field[0][0].shape[0]
-    block = lax.axis_index("dp")
+    member = lax.axis_index("dp")
     members = lax.axis_size("dp")
-    gravity_rows = block < members * 3 // 4
+    gravity_rows = member < members * 3 // 4
     chosen = [jnp.where(gravity_rows, d, s) for d, s in zip(field[0], field[1])]
-    vector = spread(chosen, LANES).astype(jnp.bfloat16)
     eye = lax.broadcasted_iota(jnp.int32, (LANES, LANES), 0) == lax.broadcasted_iota(
         jnp.int32, (LANES, LANES), 1
     )
-    product = lax.dot_general(
-        matrix_ref[...], vector, (((1,), (1,)), ((), ())), preferred_element_type=jnp.float32
-    )
-    pieces = [
-        jnp.sum(
-            jnp.where(eye, product[b * LANES : (b + 1) * LANES], 0.0), axis=0, keepdims=True
-        )
-        for b in range(rows // LANES)
-    ]
+    lines_in = [plane[t : t + 1] for plane in chosen for t in range(tall)]
+    pieces = []
+    for b in range(rows // LANES):
+        if ready is not None:
+            ready(b)
+        total = None
+        for t, line in enumerate(lines_in):
+            block = matrix_ref[b * LANES : (b + 1) * LANES, t * LANES : (t + 1) * LANES]
+            term = block.astype(jnp.float32) * line
+            total = term if total is None else total + term
+        column = jnp.sum(total, axis=1, keepdims=True)
+        pieces.append(jnp.sum(jnp.where(eye, column, 0.0), axis=0, keepdims=True))
     edges = [field[0][0], field[1][0], field[0][-1], field[1][-1]]
-    pieces.append(share_of(edges, block, members))
+    pieces.append(share_of(edges, member, members))
     pieces += lines
     pieces.append(jnp.zeros((SUBLANES - len(lines), LANES), jnp.float32))
     message = jnp.concatenate(pieces, axis=0)
@@ -170,8 +172,24 @@
                 ref[f, i : i + 1, t * LANES : (t + 1) * LANES] = field[f][i][t : t + 1]
 
 
-def start_kernel(matrix_ref, model_ref, out_ref):
-    send_rows(matrix_ref, load_wide(model_ref), [], out_ref)
+def start_kernel(raw_ref, far_ref, matrix_ref, out_ref, chunks, arrived, model_ref, came):
+    def fetch(b):
+        return pltpu.make_async_copy(
+            raw_ref.at[pl.ds(b * LANES, LANES)], chunks.at[b], arrived.at[b]
+        )
+
+    model_copy = pltpu.make_async_copy(far_ref, model_ref, came)
+    model_copy.start()
+    for b in range(chunks.shape[0]):
+        fetch(b).start()
+
+    def ready(b):
+        fetch(b).wait()
+        block = chunks[b]
+        matrix_ref[b * LANES : (b + 1) * LANES] = block.reshape(LANES, -1)
+
+    model_copy.wait()
+    send_rows(matrix_ref, load_wide(model_ref), [], out_ref, ready)
 
 
 def rows_kernel(
@@ -311,7 +329,6 @@
 
 def local(sensitivity, observed, row_weight, model, smooth_weight, active):
     rows = sensitivity.shape[0]
-    matrix = sensitivity.reshape(rows, -1)
     layers, width = smooth_weight.shape
     tall = width // LANES
     owners = lax.axis_size("mp")
@@ -332,16 +349,15 @@
     vmem = pl.BlockSpec(memory_space=pltpu.VMEM)
 
     def call(kernel, out_shape, *operands, name, scratch=()):
-        held = pltpu.with_memory_space_constraint(matrix, pltpu.VMEM)
         return pl.pallas_call(
             kernel,
             out_shape=out_shape,
-            in_specs=[vmem] * (1 + len(operands)),
+            in_specs=[vmem] * len(operands),
             out_specs=jax.tree.map(lambda _: vmem, out_shape),
             scratch_shapes=scratch,
             compiler_params=pltpu.CompilerParams(vmem_limit_bytes=KERNEL_VMEM),
             name=name,
-        )(held, *operands)
+        )(*operands)
 
     def across(sent):
         return lax.all_to_all(sent, "mp", 0, 0, tiled=True)
@@ -350,6 +366,7 @@
         sent = call(
             functools.partial(rows_kernel, subtract=subtract, tall=tall),
             columns,
+            matrix,
             got,
             weight,
             target,
@@ -360,11 +377,27 @@
             for s in range(1, blocks)
         ]
 
-    got = across(call(start_kernel, message, model, name="start"))
+    matrix, sent = pl.pallas_call(
+        start_kernel,
+        out_shape=(jax.ShapeDtypeStruct((rows, layers * width), sensitivity.dtype), message),
+        in_specs=[pl.BlockSpec(memory_space=pltpu.HBM)] * 2,
+        out_specs=(vmem, vmem),
+        scratch_shapes=[
+            pltpu.VMEM((base, LANES) + sensitivity.shape[1:], sensitivity.dtype),
+            pltpu.SemaphoreType.DMA((base,)),
+            pltpu.VMEM(model.shape, jnp.float32),
+            pltpu.SemaphoreType.DMA,
+        ],
+        compiler_params=pltpu.CompilerParams(vmem_limit_bytes=KERNEL_VMEM),
+        name="start",
+    )(*[pltpu.with_memory_space_constraint(x, pltpu.HBM) for x in (sensitivity, model)])
+    matrix = pltpu.with_memory_space_constraint(matrix, pltpu.VMEM)
+    got = across(sent)
     parts = along(got, True)
     sent, residual, inner, smooth, mask = call(
         functools.partial(first_kernel, count=blocks),
         (message, cell, cell, field, cell),
+        matrix,
         *parts,
         model,
         smooth_weight,
@@ -383,6 +416,7 @@
                 cells_kernel, count=blocks, base=base, begin=step == 0, final=final
             ),
             outs,
+            matrix,
             *parts,
             got,
             smooth,

time: 87.2 us -> 85.5 us (0.981)
  local copies, waits for them, and re-layouts: 3.65 us -> 0.02 us
  Pallas kernels: 10.8 us -> 13 us
    unnamed x11 -> x10, local copies, waits for them, and re-layouts: 3.65 us -> 0.02 us
    pallas_call x11, Pallas kernels: 10.8 us -> 13 us  [the longest x10 8.12 us: call(): pl.pallas_call(kernel, out_shape=out_shape, in_specs=[vmem] * len(operand...]
where the time goes in v5:
time: 85.5 us; the launch traced here: 85.2 us
  blocking collectives  52.6 us (62%)
  Pallas kernels  13 us (15%)
  waiting for transfers between devices  9.54 us (11%)
  starting transfers between devices  9.38 us (11%)
    all_to_all x5, blocking collectives, across(): return lax.all_to_all(sent, 'mp', 0, 0, tiled=True)  52.6 us
    ppermute x15, waiting for transfers between devices, along(): lax.ppermute(sent, 'dp', [(i, i ^ s) for i in range(blocks)])  9.54 us
    ppermute x15, starting transfers between devices, along(): lax.ppermute(sent, 'dp', [(i, i ^ s) for i in range(blocks)])  9.38 us
    pallas_call x10, Pallas kernels, call(): pl.pallas_call(kernel, out_shape=out_shape, in_specs=[vmem] * len(operand...  8.12 us
    pallas_call x1, Pallas kernels, local(): pl.pallas_call(start_kernel, out_shape=(jax.ShapeDtypeStruct((rows, layer...  4.83 us
  transfers between devices with their start and end apart: 15, of which 10 were waited for; matrix products, arithmetic and copies ran while one was open for 0% of the time, Pallas kernels for 0%

profile of v5, /device:TPU:0, one launch (start us, length us, event | category | flops | bytes accessed | tf_op | source)
XLA Modules:
  0.0 85.2 jit_solution(8738207992515792893)
XLA Ops:
  0.6 0.0 copy-start.2
  0.7 4.8 %start.1 = (bf16[1024,2048]{1,0:T(8,128)(2,1)S(1)}, f32[8,24,128]{2,1,0:T(8,128)S(1)}) custom-call(bf16[1024,2,1024]{2,1,0:T(2,128)(2,1)} %raw_ref.1, f32[2,2,1024]{2,1,0:T(2,128)} %refs_4_.1), custom_call_target="tpu_custom_call" | custom-call | tf_op jit(solution)/shard_map/start/pallas_call | solution.py:380
  5.5 14.2 %all_to_all.25.got_ref = f32[8,24,128]{2,1,0:T(8,128)S(1)} all-to-all(f32[8,24,128]{2,1,0:T(8,128)S(1)} %get-tuple-element.31), channel_id=1, replica_groups=mesh['dp'=4,'mp'=8] {'mp'}, dimensions={0} | all-to-all | bytes 196608 | tf_op jit(solution)/shard_map/all_to_all | solution.py:363
  19.8 0.7 rows.5.refs_0_
  20.4 0.0 collective-permute-start.2
  20.4 1.5 %collective-permute-start.1 = (f32[32,128]{1,0:T(8,128)S(1)}, f32[32,128]{1,0:T(8,128)S(1)}, u32[]{:S(2)}, u32[]{:S(2)}) collective-permute-start(f32[32,128]{1,0:T(8,128)S(1)} %rows.5.refs_0_), channel_id=1, source_target_pairs={{0,16},{8,24},{16,0},{24,8},{1,17},{9,25},{17,1},{25,9},{2,18},{10... | collective-permute-start | bytes 49160 | tf_op jit(solution)/shard_map/ppermute | solution.py:376
  21.9 0.3 collective-permute-start
  22.3 1.4 %collective-permute-done.2.refs_3_ = f32[32,128]{1,0:T(8,128)S(1)} collective-permute-done((f32[32,128]{1,0:T(8,128)S(1)}, f32[32,128]{1,0:T(8,128)S(1)}, u32[]{:S(2)}, u32[]{:S(2)}) %collective-permute-start.2) | collective-permute-done | bytes 16416 | tf_op jit(solution)/shard_map/ppermute | solution.py:376
  23.7 0.5 collective-permute-done.1.refs_2_
  24.2 0.0 collective-permute-done.refs_1_
  24.2 0.0 copy-done.2
  24.2 1.0 %first.1 = (f32[8,24,128]{2,1,0:T(8,128)S(1)}, f32[2,2,8,128]{3,2,1,0:T(8,128)S(1)}, f32[2,2,8,128]{3,2,1,0:T(8,128)S(1)}, f32[2,8,128]{2,1,0:T(8,128)S(1)}, f32[2,2,8,128]{3,2,1,0:T(8,128)S(1)}) custom-call(bf16[1024,2048]{1,0:T(8,128)(2,1)S(1)} %get-tuple-element.30.matrix_ref, f32[32,128]{1,0:T(8,128)S(1)} %rows.5.refs_0_, ...), custom_call_target="tpu_custom_call" | custom-call | tf_op jit(solution)/shard_map/first/pallas_call | solution.py:352
  25.2 9.8 %all_to_all.26.got_ref.refs_4_ = f32[8,24,128]{2,1,0:T(8,128)S(1)} all-to-all(f32[8,24,128]{2,1,0:T(8,128)S(1)} %get-tuple-element.32), channel_id=1, replica_groups=mesh['dp'=4,'mp'=8] {'mp'}, dimensions={0} | all-to-all | bytes 196608 | tf_op jit(solution)/shard_map/all_to_all | solution.py:363
  35.0 0.6 rows.6.refs_0_
  35.6 0.0 collective-permute-start.5
  35.6 1.3 %collective-permute-start.4 = (f32[32,128]{1,0:T(8,128)S(1)}, f32[32,128]{1,0:T(8,128)S(1)}, u32[]{:S(2)}, u32[]{:S(2)}) collective-permute-start(f32[32,128]{1,0:T(8,128)S(1)} %rows.6.refs_0_), channel_id=1, source_target_pairs={{0,16},{8,24},{16,0},{24,8},{1,17},{9,25},{17,1},{25,9},{2,18},{10... | collective-permute-start | bytes 49160 | tf_op jit(solution)/shard_map/ppermute | solution.py:376
  36.9 0.6 collective-permute-start.3
  37.5 1.3 %collective-permute-done.5.refs_3_ = f32[32,128]{1,0:T(8,128)S(1)} collective-permute-done((f32[32,128]{1,0:T(8,128)S(1)}, f32[32,128]{1,0:T(8,128)S(1)}, u32[]{:S(2)}, u32[]{:S(2)}) %collective-permute-start.5) | collective-permute-done | bytes 16416 | tf_op jit(solution)/shard_map/ppermute | solution.py:376
  38.8 0.6 collective-permute-done.4.refs_2_
  39.4 0.0 collective-permute-done.3.refs_1_
  39.4 1.0 %cells.4 = (f32[2,2,8,128]{3,2,1,0:T(8,128)S(1)}, f32[2,2,8,128]{3,2,1,0:T(8,128)S(1)}, f32[2,2,8,128]{3,2,1,0:T(8,128)S(1)}, f32[2,2,8,128]{3,2,1,0:T(8,128)S(1...) custom-call(bf16[1024,2048]{1,0:T(8,128)(2,1)S(1)} %get-tuple-element.30.matrix_ref, ...), custom_call_target="tpu_custom_call" | custom-call | tf_op jit(solution)/shard_map/cells/pallas_call | solution.py:352
  40.4 9.5 %all_to_all.27.got_ref.refs_4_ = f32[8,24,128]{2,1,0:T(8,128)S(1)} all-to-all(f32[8,24,128]{2,1,0:T(8,128)S(1)} %get-tuple-element.37), channel_id=1, replica_groups=mesh['dp'=4,'mp'=8] {'mp'}, dimensions={0} | all-to-all | bytes 196608 | tf_op jit(solution)/shard_map/all_to_all | solution.py:363
  49.9 0.6 rows.7.refs_0_
  50.6 0.0 collective-permute-start.8
  50.6 1.4 %collective-permute-start.7 = (f32[32,128]{1,0:T(8,128)S(1)}, f32[32,128]{1,0:T(8,128)S(1)}, u32[]{:S(2)}, u32[]{:S(2)}) collective-permute-start(f32[32,128]{1,0:T(8,128)S(1)} %rows.7.refs_0_), channel_id=1, source_target_pairs={{0,16},{8,24},{16,0},{24,8},{1,17},{9,25},{17,1},{25,9},{2,18},{10... | collective-permute-start | bytes 49160 | tf_op jit(solution)/shard_map/ppermute | solution.py:376
  52.0 0.5 collective-permute-start.6
  52.5 1.4 %collective-permute-done.8.refs_3_ = f32[32,128]{1,0:T(8,128)S(1)} collective-permute-done((f32[32,128]{1,0:T(8,128)S(1)}, f32[32,128]{1,0:T(8,128)S(1)}, u32[]{:S(2)}, u32[]{:S(2)}) %collective-permute-start.8) | collective-permute-done | bytes 16416 | tf_op jit(solution)/shard_map/ppermute | solution.py:376
  53.8 0.5 collective-permute-done.7.refs_2_
  54.4 0.0 collective-permute-done.6.refs_1_
  54.4 1.0 %cells.5 = (f32[2,2,8,128]{3,2,1,0:T(8,128)S(1)}, f32[2,2,8,128]{3,2,1,0:T(8,128)S(1)}, f32[2,2,8,128]{3,2,1,0:T(8,128)S(1)}, f32[2,2,8,128]{3,2,1,0:T(8,128)S(1...) custom-call(bf16[1024,2048]{1,0:T(8,128)(2,1)S(1)} %get-tuple-element.30.matrix_ref, ...), custom_call_target="tpu_custom_call" | custom-call | tf_op jit(solution)/shard_map/cells/pallas_call | solution.py:352
  55.4 9.6 %all_to_all.28.got_ref.refs_4_ = f32[8,24,128]{2,1,0:T(8,128)S(1)} all-to-all(f32[8,24,128]{2,1,0:T(8,128)S(1)} %get-tuple-element.44), channel_id=1, replica_groups=mesh['dp'=4,'mp'=8] {'mp'}, dimensions={0} | all-to-all | bytes 196608 | tf_op jit(solution)/shard_map/all_to_all | solution.py:363
  65.0 0.6 rows.8.refs_0_
  65.7 0.0 collective-permute-start.11
  65.7 1.3 %collective-permute-start.10 = (f32[32,128]{1,0:T(8,128)S(1)}, f32[32,128]{1,0:T(8,128)S(1)}, u32[]{:S(2)}, u32[]{:S(2)}) collective-permute-start(f32[32,128]{1,0:T(8,128)S(1)} %rows.8.refs_0_), channel_id=1, source_target_pairs={{0,16},{8,24},{16,0},{24,8},{1,17},{9,25},{17,1},{25,9},{2,18},{10... | collective-permute-start | bytes 49160 | tf_op jit(solution)/shard_map/ppermute | solution.py:376
  67.0 0.6 collective-permute-start.9
  67.6 1.3 %collective-permute-done.11.refs_3_ = f32[32,128]{1,0:T(8,128)S(1)} collective-permute-done((f32[32,128]{1,0:T(8,128)S(1)}, f32[32,128]{1,0:T(8,128)S(1)}, u32[]{:S(2)}, u32[]{:S(2)}) %collective-permute-start.11) | collective-permute-done | bytes 16416 | tf_op jit(solution)/shard_map/ppermute | solution.py:376
  68.9 0.6 collective-permute-done.10.refs_2_
  69.5 0.0 collective-permute-done.9.refs_1_
  69.5 1.0 %cells.6 = (f32[2,2,8,128]{3,2,1,0:T(8,128)S(1)}, f32[2,2,8,128]{3,2,1,0:T(8,128)S(1)}, f32[2,2,8,128]{3,2,1,0:T(8,128)S(1)}, f32[2,2,8,128]{3,2,1,0:T(8,128)S(1...) custom-call(bf16[1024,2048]{1,0:T(8,128)(2,1)S(1)} %get-tuple-element.30.matrix_ref, ...), custom_call_target="tpu_custom_call" | custom-call | tf_op jit(solution)/shard_map/cells/pallas_call | solution.py:352
  70.5 9.5 %all_to_all.29.got_ref.refs_4_ = f32[8,24,128]{2,1,0:T(8,128)S(1)} all-to-all(f32[8,24,128]{2,1,0:T(8,128)S(1)} %get-tuple-element.51), channel_id=1, replica_groups=mesh['dp'=4,'mp'=8] {'mp'}, dimensions={0} | all-to-all | bytes 196608 | tf_op jit(solution)/shard_map/all_to_all | solution.py:363
  80.0 0.7 rows.9.refs_0_
  80.7 0.0 collective-permute-start.14
  80.7 1.4 %collective-permute-start.13 = (f32[32,128]{1,0:T(8,128)S(1)}, f32[32,128]{1,0:T(8,128)S(1)}, u32[]{:S(2)}, u32[]{:S(2)}) collective-permute-start(f32[32,128]{1,0:T(8,128)S(1)} %rows.9.refs_0_), channel_id=1, source_target_pairs={{0,16},{8,24},{16,0},{24,8},{1,17},{9,25},{17,1},{25,9},{2,18},{10... | collective-permute-start | bytes 49160 | tf_op jit(solution)/shard_map/ppermute | solution.py:376
  82.1 0.5 collective-permute-start.12
  82.6 1.4 %collective-permute-done.14.refs_3_ = f32[32,128]{1,0:T(8,128)S(1)} collective-permute-done((f32[32,128]{1,0:T(8,128)S(1)}, f32[32,128]{1,0:T(8,128)S(1)}, u32[]{:S(2)}, u32[]{:S(2)}) %collective-permute-start.14) | collective-permute-done | bytes 16416 | tf_op jit(solution)/shard_map/ppermute | solution.py:376
  83.9 0.5 collective-permute-done.13.refs_2_
  84.5 0.0 collective-permute-done.12.refs_1_
  84.5 0.8 cells.7
  (8 shorter events, 0.0 us)
Async XLA Ops:
  0.6 23.6 %copy-start.2 = (f32[2,2,1024]{2,1,0:T(2,128)S(1)}, f32[2,2,1024]{2,1,0:T(2,128)}, u32[]{:S(2)}) copy-start(f32[2,2,1024]{2,1,0:T(2,128)} %refs_4_.1) | copy-start | bytes 49156
  0.6 19.1 %copy-start = (f32[1024]{0:T(1024)S(1)}, f32[1024]{0:T(1024)}, u32[]{:S(2)}) copy-start(f32[1024]{0:T(1024)} %param.8) | copy-start | bytes 12292
  0.7 19.1 %copy-start.1 = (f32[1024]{0:T(1024)S(1)}, f32[1024]{0:T(1024)}, u32[]{:S(2)}) copy-start(f32[1024]{0:T(1024)} %param.7) | copy-start | bytes 12292
  0.7 23.5 %copy-start.3 = (s32[2,2,1024]{2,1,0:T(2,128)S(1)}, s32[2,2,1024]{2,1,0:T(2,128)}, u32[]{:S(2)}) copy-start(s32[2,2,1024]{2,1,0:T(2,128)} %refs_6_.1) | copy-start | bytes 49156
  0.7 23.5 %copy-start.4 = (f32[2,1024]{1,0:T(2,128)S(1)}, f32[2,1024]{1,0:T(2,128)}, u32[]{:S(2)}) copy-start(f32[2,1024]{1,0:T(2,128)} %refs_5_.1) | copy-start | bytes 24580
  20.4 3.3 %collective-permute-start.2 = (f32[32,128]{1,0:T(8,128)S(1)}, f32[32,128]{1,0:T(8,128)S(1)}, u32[]{:S(2)}, u32[]{:S(2)}) collective-permute-start(f32[32,128]{1,0:T(8,128)S(1)} %rows.5.refs_0_), channel_id=1, source_target_pairs={{0,24},{8,16},{16,8},{24,0},{1,25},{9,17},{17,9},{25,1},{2,26},{10... | collective-permute-start | bytes 49160 | tf_op jit(solution)/shard_map/ppermute | solution.py:376
  20.4 3.8 %collective-permute-start.1 = (f32[32,128]{1,0:T(8,128)S(1)}, f32[32,128]{1,0:T(8,128)S(1)}, u32[]{:S(2)}, u32[]{:S(2)}) collective-permute-start(f32[32,128]{1,0:T(8,128)S(1)} %rows.5.refs_0_), channel_id=1, source_target_pairs={{0,16},{8,24},{16,0},{24,8},{1,17},{9,25},{17,1},{25,9},{2,18},{10... | collective-permute-start | bytes 49160 | tf_op jit(solution)/shard_map/ppermute | solution.py:376
  21.9 2.3 %collective-permute-start = (f32[32,128]{1,0:T(8,128)S(1)}, f32[32,128]{1,0:T(8,128)S(1)}, u32[]{:S(2)}, u32[]{:S(2)}) collective-permute-start(f32[32,128]{1,0:T(8,128)S(1)} %rows.5.refs_0_), channel_id=1, source_target_pairs={{0,8},{8,0},{16,24},{24,16},{1,9},{9,1},{17,25},{25,17},{2,10},{10... | collective-permute-start | bytes 49160 | tf_op jit(solution)/shard_map/ppermute | solution.py:376
  35.6 3.2 %collective-permute-start.5 = (f32[32,128]{1,0:T(8,128)S(1)}, f32[32,128]{1,0:T(8,128)S(1)}, u32[]{:S(2)}, u32[]{:S(2)}) collective-permute-start(f32[32,128]{1,0:T(8,128)S(1)} %rows.6.refs_0_), channel_id=1, source_target_pairs={{0,24},{8,16},{16,8},{24,0},{1,25},{9,17},{17,9},{25,1},{2,26},{10... | collective-permute-start | bytes 49160 | tf_op jit(solution)/shard_map/ppermute | solution.py:376
  35.6 3.8 %collective-permute-start.4 = (f32[32,128]{1,0:T(8,128)S(1)}, f32[32,128]{1,0:T(8,128)S(1)}, u32[]{:S(2)}, u32[]{:S(2)}) collective-permute-start(f32[32,128]{1,0:T(8,128)S(1)} %rows.6.refs_0_), channel_id=1, source_target_pairs={{0,16},{8,24},{16,0},{24,8},{1,17},{9,25},{17,1},{25,9},{2,18},{10... | collective-permute-start | bytes 49160 | tf_op jit(solution)/shard_map/ppermute | solution.py:376
  36.9 2.5 %collective-permute-start.3 = (f32[32,128]{1,0:T(8,128)S(1)}, f32[32,128]{1,0:T(8,128)S(1)}, u32[]{:S(2)}, u32[]{:S(2)}) collective-permute-start(f32[32,128]{1,0:T(8,128)S(1)} %rows.6.refs_0_), channel_id=1, source_target_pairs={{0,8},{8,0},{16,24},{24,16},{1,9},{9,1},{17,25},{25,17},{2,10},{10... | collective-permute-start | bytes 49160 | tf_op jit(solution)/shard_map/ppermute | solution.py:376
  50.6 3.3 %collective-permute-start.8 = (f32[32,128]{1,0:T(8,128)S(1)}, f32[32,128]{1,0:T(8,128)S(1)}, u32[]{:S(2)}, u32[]{:S(2)}) collective-permute-start(f32[32,128]{1,0:T(8,128)S(1)} %rows.7.refs_0_), channel_id=1, source_target_pairs={{0,24},{8,16},{16,8},{24,0},{1,25},{9,17},{17,9},{25,1},{2,26},{10... | collective-permute-start | bytes 49160 | tf_op jit(solution)/shard_map/ppermute | solution.py:376
  50.6 3.8 %collective-permute-start.7 = (f32[32,128]{1,0:T(8,128)S(1)}, f32[32,128]{1,0:T(8,128)S(1)}, u32[]{:S(2)}, u32[]{:S(2)}) collective-permute-start(f32[32,128]{1,0:T(8,128)S(1)} %rows.7.refs_0_), channel_id=1, source_target_pairs={{0,16},{8,24},{16,0},{24,8},{1,17},{9,25},{17,1},{25,9},{2,18},{10... | collective-permute-start | bytes 49160 | tf_op jit(solution)/shard_map/ppermute | solution.py:376
  52.0 2.4 %collective-permute-start.6 = (f32[32,128]{1,0:T(8,128)S(1)}, f32[32,128]{1,0:T(8,128)S(1)}, u32[]{:S(2)}, u32[]{:S(2)}) collective-permute-start(f32[32,128]{1,0:T(8,128)S(1)} %rows.7.refs_0_), channel_id=1, source_target_pairs={{0,8},{8,0},{16,24},{24,16},{1,9},{9,1},{17,25},{25,17},{2,10},{10... | collective-permute-start | bytes 49160 | tf_op jit(solution)/shard_map/ppermute | solution.py:376
  65.7 3.2 %collective-permute-start.11 = (f32[32,128]{1,0:T(8,128)S(1)}, f32[32,128]{1,0:T(8,128)S(1)}, u32[]{:S(2)}, u32[]{:S(2)}) collective-permute-start(f32[32,128]{1,0:T(8,128)S(1)} %rows.8.refs_0_), channel_id=1, source_target_pairs={{0,24},{8,16},{16,8},{24,0},{1,25},{9,17},{17,9},{25,1},{2,26},{10... | collective-permute-start | bytes 49160 | tf_op jit(solution)/shard_map/ppermute | solution.py:376
  65.7 3.8 %collective-permute-start.10 = (f32[32,128]{1,0:T(8,128)S(1)}, f32[32,128]{1,0:T(8,128)S(1)}, u32[]{:S(2)}, u32[]{:S(2)}) collective-permute-start(f32[32,128]{1,0:T(8,128)S(1)} %rows.8.refs_0_), channel_id=1, source_target_pairs={{0,16},{8,24},{16,0},{24,8},{1,17},{9,25},{17,1},{25,9},{2,18},{10... | collective-permute-start | bytes 49160 | tf_op jit(solution)/shard_map/ppermute | solution.py:376
  67.0 2.5 %collective-permute-start.9 = (f32[32,128]{1,0:T(8,128)S(1)}, f32[32,128]{1,0:T(8,128)S(1)}, u32[]{:S(2)}, u32[]{:S(2)}) collective-permute-start(f32[32,128]{1,0:T(8,128)S(1)} %rows.8.refs_0_), channel_id=1, source_target_pairs={{0,8},{8,0},{16,24},{24,16},{1,9},{9,1},{17,25},{25,17},{2,10},{10... | collective-permute-start | bytes 49160 | tf_op jit(solution)/shard_map/ppermute | solution.py:376
  80.7 3.2 %collective-permute-start.14 = (f32[32,128]{1,0:T(8,128)S(1)}, f32[32,128]{1,0:T(8,128)S(1)}, u32[]{:S(2)}, u32[]{:S(2)}) collective-permute-start(f32[32,128]{1,0:T(8,128)S(1)} %rows.9.refs_0_), channel_id=1, source_target_pairs={{0,24},{8,16},{16,8},{24,0},{1,25},{9,17},{17,9},{25,1},{2,26},{10... | collective-permute-start | bytes 49160 | tf_op jit(solution)/shard_map/ppermute | solution.py:376
  80.7 3.8 %collective-permute-start.13 = (f32[32,128]{1,0:T(8,128)S(1)}, f32[32,128]{1,0:T(8,128)S(1)}, u32[]{:S(2)}, u32[]{:S(2)}) collective-permute-start(f32[32,128]{1,0:T(8,128)S(1)} %rows.9.refs_0_), channel_id=1, source_target_pairs={{0,16},{8,24},{16,0},{24,8},{1,17},{9,25},{17,1},{25,9},{2,18},{10... | collective-permute-start | bytes 49160 | tf_op jit(solution)/shard_map/ppermute | solution.py:376
  82.1 2.4 %collective-permute-start.12 = (f32[32,128]{1,0:T(8,128)S(1)}, f32[32,128]{1,0:T(8,128)S(1)}, u32[]{:S(2)}, u32[]{:S(2)}) collective-permute-start(f32[32,128]{1,0:T(8,128)S(1)} %rows.9.refs_0_), channel_id=1, source_target_pairs={{0,8},{8,0},{16,24},{24,16},{1,9},{9,1},{17,25},{25,17},{2,10},{10... | collective-permute-start | bytes 49160 | tf_op jit(solution)/shard_map/ppermute | solution.py:376

commit v6 on v5

--- a/solution.py
+++ b/solution.py
@@ -15,6 +15,9 @@
 COUPLING = 0.5
 LANES = 128
 SUBLANES = 8
+SCALARS = 3
+CHUNK = 64
+IN_FLIGHT = 6
 KERNEL_VMEM = 16 * 1024 * 1024
 
 
@@ -147,10 +150,9 @@
     edges = [field[0][0], field[1][0], field[0][-1], field[1][-1]]
     pieces.append(share_of(edges, member, members))
     pieces += lines
-    pieces.append(jnp.zeros((SUBLANES - len(lines), LANES), jnp.float32))
     message = jnp.concatenate(pieces, axis=0)
     for j in range(owners):
-        out_ref[j] = message
+        out_ref[j, 0 : message.shape[0], 0] = message
 
 
 def load_layers(ref):
@@ -173,20 +175,25 @@
 
 
 def start_kernel(raw_ref, far_ref, matrix_ref, out_ref, chunks, arrived, model_ref, came):
-    def fetch(b):
+    count, height = chunks.shape[:2]
+
+    def fetch(n):
         return pltpu.make_async_copy(
-            raw_ref.at[pl.ds(b * LANES, LANES)], chunks.at[b], arrived.at[b]
+            raw_ref.at[pl.ds(n * height, height)], chunks.at[n], arrived.at[n]
         )
 
     model_copy = pltpu.make_async_copy(far_ref, model_ref, came)
     model_copy.start()
-    for b in range(chunks.shape[0]):
-        fetch(b).start()
+    for n in range(min(IN_FLIGHT, count)):
+        fetch(n).start()
 
     def ready(b):
-        fetch(b).wait()
-        block = chunks[b]
-        matrix_ref[b * LANES : (b + 1) * LANES] = block.reshape(LANES, -1)
+        for n in range(b * LANES // height, (b + 1) * LANES // height):
+            fetch(n).wait()
+            if n + IN_FLIGHT < count:
+                fetch(n + IN_FLIGHT).start()
+            block = chunks[n]
+            matrix_ref[n * height : (n + 1) * height] = block.reshape(height, -1)
 
     model_copy.wait()
     send_rows(matrix_ref, load_wide(model_ref), [], out_ref, ready)
@@ -201,9 +208,9 @@
     owners = got_ref.shape[0]
     rows, cells = matrix_ref.shape
     blocks = rows // LANES
-    values = got_ref[0, 0:blocks]
+    values = got_ref[0, 0:blocks, 0]
     for j in range(1, owners):
-        values = values + got_ref[j, 0:blocks]
+        values = values + got_ref[j, 0:blocks, 0]
     if subtract:
         values = values - observed_ref[...]
     scaled = (weight_ref[...] * values).astype(jnp.bfloat16).astype(jnp.float32)
@@ -212,7 +219,7 @@
     columns = jnp.dot(vector, matrix_ref[...], preferred_element_type=jnp.float32)
     pieces = [columns[0:1, t * LANES : (t + 1) * LANES] for t in range(cells // LANES)]
     count = tall // members
-    shares = [got_ref[j, blocks : blocks + tall] for j in range(owners)]
+    shares = [got_ref[j, blocks : blocks + tall, 0] for j in range(owners)]
     held = [where_block(shares[0].shape, count, member + n, members) for n in range(4)]
     lower = held[0] | held[1]
     upper = held[2] | held[3]
@@ -224,8 +231,8 @@
     weighed = weighed - 2.0 * SMOOTHING * cross
     down = jnp.maximum(rank - 1, 0)
     up = jnp.minimum(rank + 1, owners - 1)
-    above = jnp.where(lower & (rank < owners - 1), got_ref[up, blocks : blocks + tall], 0.0)
-    below = jnp.where(upper & (rank > 0), got_ref[down, blocks : blocks + tall], 0.0)
+    above = jnp.where(lower & (rank < owners - 1), got_ref[up, blocks : blocks + tall, 0], 0.0)
+    below = jnp.where(upper & (rank > 0), got_ref[down, blocks : blocks + tall, 0], 0.0)
     pieces += [above + below, weighed, jnp.zeros((SUBLANES - 1, LANES), jnp.float32)]
     out_ref[...] = jnp.concatenate(pieces, axis=0)
 
@@ -289,9 +296,9 @@
     residual = load(residual_in)
     image = gathered(part_refs, inner_in, mask_ref)
     at = base + tall
-    sums = got_ref[0, at : at + SUBLANES]
+    sums = got_ref[0, at : at + SCALARS, 0]
     for j in range(1, owners):
-        sums = sums + got_ref[j, at : at + SUBLANES]
+        sums = sums + got_ref[j, at : at + SCALARS, 0]
     at = cells + tall
     weighed = tree_sum([ref[at : at + 1] for ref in part_refs])
     line = weighed + sums[1:2]
@@ -343,7 +350,7 @@
     wide = jax.ShapeDtypeStruct(model.shape, jnp.float32)
     if tall % blocks or blocks < 4:
         raise ValueError("boundary shares")
-    message = jax.ShapeDtypeStruct((owners, base + tall + SUBLANES, LANES), jnp.float32)
+    message = jax.ShapeDtypeStruct((owners, base + tall + SCALARS, 1, LANES), jnp.float32)
     columns = jax.ShapeDtypeStruct(((layers + 1) * tall + SUBLANES, LANES), jnp.float32)
     norms = jax.ShapeDtypeStruct((2, LANES), jnp.float32)
     vmem = pl.BlockSpec(memory_space=pltpu.VMEM)
@@ -383,8 +390,8 @@
         in_specs=[pl.BlockSpec(memory_space=pltpu.HBM)] * 2,
         out_specs=(vmem, vmem),
         scratch_shapes=[
-            pltpu.VMEM((base, LANES) + sensitivity.shape[1:], sensitivity.dtype),
-            pltpu.SemaphoreType.DMA((base,)),
+            pltpu.VMEM((rows // CHUNK, CHUNK) + sensitivity.shape[1:], sensitivity.dtype),
+            pltpu.SemaphoreType.DMA((rows // CHUNK,)),
             pltpu.VMEM(model.shape, jnp.float32),
             pltpu.SemaphoreType.DMA,
         ],

time: 85.5 us -> 84.2 us (0.985)
  blocking collectives: 52.6 us -> 51.7 us
    all_to_all x5, blocking collectives: 52.6 us -> 51.7 us  [across(): return lax.all_to_all(sent, 'mp', 0, 0, tiled=True)]
where the time goes in v6:
time: 84.2 us; the launch traced here: 83.9 us
  blocking collectives  51.7 us (61%)
  Pallas kernels  12.5 us (15%)
  waiting for transfers between devices  9.54 us (11%)
  starting transfers between devices  9.38 us (11%)
    all_to_all x5, blocking collectives, across(): return lax.all_to_all(sent, 'mp', 0, 0, tiled=True)  51.7 us
    ppermute x15, waiting for transfers between devices, along(): lax.ppermute(sent, 'dp', [(i, i ^ s) for i in range(blocks)])  9.54 us
    ppermute x15, starting transfers between devices, along(): lax.ppermute(sent, 'dp', [(i, i ^ s) for i in range(blocks)])  9.38 us
    pallas_call x10, Pallas kernels, call(): pl.pallas_call(kernel, out_shape=out_shape, in_specs=[vmem] * len(operand...  8.34 us
    pallas_call x1, Pallas kernels, local(): pl.pallas_call(start_kernel, out_shape=(jax.ShapeDtypeStruct((rows, layer...  4.2 us
  transfers between devices with their start and end apart: 15, of which 10 were waited for; matrix products, arithmetic and copies ran while one was open for 0% of the time, Pallas kernels for 0%

profile of v6, /device:TPU:0, one launch (start us, length us, event | category | flops | bytes accessed | tf_op | source)
XLA Modules:
  0.0 83.9 jit_solution(11281682487386040885)
XLA Ops:
  0.6 0.0 copy-start.2
  0.6 0.0 copy-start
  0.7 4.2 %start.1 = (bf16[1024,2048]{1,0:T(8,128)(2,1)S(1)}, f32[8,19,1,128]{3,2,1,0:T(1,128)S(1)}) custom-call(bf16[1024,2,1024]{2,1,0:T(2,128)(2,1)} %raw_ref.1, f32[2,2,1024]{2,1,0:T(2,128)} %refs_4_.1), custom_call_target="tpu_custom_call" | custom-call | tf_op jit(solution)/shard_map/start/pallas_call | solution.py:387
  4.9 14.1 %all_to_all.25.got_ref = f32[8,19,1,128]{3,2,1,0:T(1,128)S(1)} all-to-all(f32[8,19,1,128]{3,2,1,0:T(1,128)S(1)} %get-tuple-element.31), channel_id=1, replica_groups=mesh['dp'=4,'mp'=8] {'mp'}, dimensions={0} | all-to-all | bytes 155648 | tf_op jit(solution)/shard_map/all_to_all | solution.py:370
  19.0 0.7 rows.5.refs_0_
  19.6 0.0 collective-permute-start.2
  19.7 1.5 %collective-permute-start.1 = (f32[32,128]{1,0:T(8,128)S(1)}, f32[32,128]{1,0:T(8,128)S(1)}, u32[]{:S(2)}, u32[]{:S(2)}) collective-permute-start(f32[32,128]{1,0:T(8,128)S(1)} %rows.5.refs_0_), channel_id=1, source_target_pairs={{0,16},{8,24},{16,0},{24,8},{1,17},{9,25},{17,1},{25,9},{2,18},{10... | collective-permute-start | bytes 49160 | tf_op jit(solution)/shard_map/ppermute | solution.py:383
  21.2 0.3 collective-permute-start
  21.5 1.4 %collective-permute-done.2.refs_3_ = f32[32,128]{1,0:T(8,128)S(1)} collective-permute-done((f32[32,128]{1,0:T(8,128)S(1)}, f32[32,128]{1,0:T(8,128)S(1)}, u32[]{:S(2)}, u32[]{:S(2)}) %collective-permute-start.2) | collective-permute-done | bytes 16416 | tf_op jit(solution)/shard_map/ppermute | solution.py:383
  23.0 0.5 collective-permute-done.1.refs_2_
  23.4 0.0 collective-permute-done.refs_1_
  23.5 1.0 %first.1 = (f32[8,19,1,128]{3,2,1,0:T(1,128)S(1)}, f32[2,2,8,128]{3,2,1,0:T(8,128)S(1)}, f32[2,2,8,128]{3,2,1,0:T(8,128)S(1)}, f32[2,8,128]{2,1,0:T(8,128)S(1)}, f32[2,2,8,128]{3,2,1,0:T(8,128)S(1)}) custom-call(bf16[1024,2048]{1,0:T(8,128)(2,1)S(1)} %get-tuple-element.30.matrix_ref, f32[32,128]{1,0:T(8,128)S(1)} %rows.5.refs_0_, ...), custom_call_target="tpu_custom_call" | custom-call | tf_op jit(solution)/shard_map/first/pallas_call | solution.py:359
  24.5 9.5 %all_to_all.26.got_ref.refs_4_ = f32[8,19,1,128]{3,2,1,0:T(1,128)S(1)} all-to-all(f32[8,19,1,128]{3,2,1,0:T(1,128)S(1)} %get-tuple-element.32), channel_id=1, replica_groups=mesh['dp'=4,'mp'=8] {'mp'}, dimensions={0} | all-to-all | bytes 155648 | tf_op jit(solution)/shard_map/all_to_all | solution.py:370
  33.9 0.7 rows.6.refs_0_
  34.6 0.0 collective-permute-start.5
  34.6 1.4 %collective-permute-start.4 = (f32[32,128]{1,0:T(8,128)S(1)}, f32[32,128]{1,0:T(8,128)S(1)}, u32[]{:S(2)}, u32[]{:S(2)}) collective-permute-start(f32[32,128]{1,0:T(8,128)S(1)} %rows.6.refs_0_), channel_id=1, source_target_pairs={{0,16},{8,24},{16,0},{24,8},{1,17},{9,25},{17,1},{25,9},{2,18},{10... | collective-permute-start | bytes 49160 | tf_op jit(solution)/shard_map/ppermute | solution.py:383
  36.1 0.4 collective-permute-start.3
  36.5 1.4 %collective-permute-done.5.refs_3_ = f32[32,128]{1,0:T(8,128)S(1)} collective-permute-done((f32[32,128]{1,0:T(8,128)S(1)}, f32[32,128]{1,0:T(8,128)S(1)}, u32[]{:S(2)}, u32[]{:S(2)}) %collective-permute-start.5) | collective-permute-done | bytes 16416 | tf_op jit(solution)/shard_map/ppermute | solution.py:383
  37.9 0.5 collective-permute-done.4.refs_2_
  38.4 0.0 collective-permute-done.3.refs_1_
  38.4 1.1 %cells.4 = (f32[2,2,8,128]{3,2,1,0:T(8,128)S(1)}, f32[2,2,8,128]{3,2,1,0:T(8,128)S(1)}, f32[2,2,8,128]{3,2,1,0:T(8,128)S(1)}, f32[2,2,8,128]{3,2,1,0:T(8,128)S(1...) custom-call(bf16[1024,2048]{1,0:T(8,128)(2,1)S(1)} %get-tuple-element.30.matrix_ref, ...), custom_call_target="tpu_custom_call" | custom-call | tf_op jit(solution)/shard_map/cells/pallas_call | solution.py:359
  39.5 9.4 %all_to_all.27.got_ref.refs_4_ = f32[8,19,1,128]{3,2,1,0:T(1,128)S(1)} all-to-all(f32[8,19,1,128]{3,2,1,0:T(1,128)S(1)} %get-tuple-element.37), channel_id=1, replica_groups=mesh['dp'=4,'mp'=8] {'mp'}, dimensions={0} | all-to-all | bytes 155648 | tf_op jit(solution)/shard_map/all_to_all | solution.py:370
  48.8 0.7 rows.7.refs_0_
  49.5 0.0 collective-permute-start.8
  49.5 1.4 %collective-permute-start.7 = (f32[32,128]{1,0:T(8,128)S(1)}, f32[32,128]{1,0:T(8,128)S(1)}, u32[]{:S(2)}, u32[]{:S(2)}) collective-permute-start(f32[32,128]{1,0:T(8,128)S(1)} %rows.7.refs_0_), channel_id=1, source_target_pairs={{0,16},{8,24},{16,0},{24,8},{1,17},{9,25},{17,1},{25,9},{2,18},{10... | collective-permute-start | bytes 49160 | tf_op jit(solution)/shard_map/ppermute | solution.py:383
  51.0 0.4 collective-permute-start.6
  51.4 1.4 %collective-permute-done.8.refs_3_ = f32[32,128]{1,0:T(8,128)S(1)} collective-permute-done((f32[32,128]{1,0:T(8,128)S(1)}, f32[32,128]{1,0:T(8,128)S(1)}, u32[]{:S(2)}, u32[]{:S(2)}) %collective-permute-start.8) | collective-permute-done | bytes 16416 | tf_op jit(solution)/shard_map/ppermute | solution.py:383
  52.8 0.5 collective-permute-done.7.refs_2_
  53.3 0.0 collective-permute-done.6.refs_1_
  53.3 1.1 %cells.5 = (f32[2,2,8,128]{3,2,1,0:T(8,128)S(1)}, f32[2,2,8,128]{3,2,1,0:T(8,128)S(1)}, f32[2,2,8,128]{3,2,1,0:T(8,128)S(1)}, f32[2,2,8,128]{3,2,1,0:T(8,128)S(1...) custom-call(bf16[1024,2048]{1,0:T(8,128)(2,1)S(1)} %get-tuple-element.30.matrix_ref, ...), custom_call_target="tpu_custom_call" | custom-call | tf_op jit(solution)/shard_map/cells/pallas_call | solution.py:359
  54.4 9.4 %all_to_all.28.got_ref.refs_4_ = f32[8,19,1,128]{3,2,1,0:T(1,128)S(1)} all-to-all(f32[8,19,1,128]{3,2,1,0:T(1,128)S(1)} %get-tuple-element.44), channel_id=1, replica_groups=mesh['dp'=4,'mp'=8] {'mp'}, dimensions={0} | all-to-all | bytes 155648 | tf_op jit(solution)/shard_map/all_to_all | solution.py:370
  63.8 0.7 rows.8.refs_0_
  64.4 0.0 collective-permute-start.11
  64.4 1.4 %collective-permute-start.10 = (f32[32,128]{1,0:T(8,128)S(1)}, f32[32,128]{1,0:T(8,128)S(1)}, u32[]{:S(2)}, u32[]{:S(2)}) collective-permute-start(f32[32,128]{1,0:T(8,128)S(1)} %rows.8.refs_0_), channel_id=1, source_target_pairs={{0,16},{8,24},{16,0},{24,8},{1,17},{9,25},{17,1},{25,9},{2,18},{10... | collective-permute-start | bytes 49160 | tf_op jit(solution)/shard_map/ppermute | solution.py:383
  65.9 0.4 collective-permute-start.9
  66.3 1.4 %collective-permute-done.11.refs_3_ = f32[32,128]{1,0:T(8,128)S(1)} collective-permute-done((f32[32,128]{1,0:T(8,128)S(1)}, f32[32,128]{1,0:T(8,128)S(1)}, u32[]{:S(2)}, u32[]{:S(2)}) %collective-permute-start.11) | collective-permute-done | bytes 16416 | tf_op jit(solution)/shard_map/ppermute | solution.py:383
  67.7 0.5 collective-permute-done.10.refs_2_
  68.2 0.0 collective-permute-done.9.refs_1_
  68.2 1.1 %cells.6 = (f32[2,2,8,128]{3,2,1,0:T(8,128)S(1)}, f32[2,2,8,128]{3,2,1,0:T(8,128)S(1)}, f32[2,2,8,128]{3,2,1,0:T(8,128)S(1)}, f32[2,2,8,128]{3,2,1,0:T(8,128)S(1...) custom-call(bf16[1024,2048]{1,0:T(8,128)(2,1)S(1)} %get-tuple-element.30.matrix_ref, ...), custom_call_target="tpu_custom_call" | custom-call | tf_op jit(solution)/shard_map/cells/pallas_call | solution.py:359
  69.3 9.4 %all_to_all.29.got_ref.refs_4_ = f32[8,19,1,128]{3,2,1,0:T(1,128)S(1)} all-to-all(f32[8,19,1,128]{3,2,1,0:T(1,128)S(1)} %get-tuple-element.51), channel_id=1, replica_groups=mesh['dp'=4,'mp'=8] {'mp'}, dimensions={0} | all-to-all | bytes 155648 | tf_op jit(solution)/shard_map/all_to_all | solution.py:370
  78.7 0.6 rows.9.refs_0_
  79.3 0.0 collective-permute-start.14
  79.3 1.4 %collective-permute-start.13 = (f32[32,128]{1,0:T(8,128)S(1)}, f32[32,128]{1,0:T(8,128)S(1)}, u32[]{:S(2)}, u32[]{:S(2)}) collective-permute-start(f32[32,128]{1,0:T(8,128)S(1)} %rows.9.refs_0_), channel_id=1, source_target_pairs={{0,16},{8,24},{16,0},{24,8},{1,17},{9,25},{17,1},{25,9},{2,18},{10... | collective-permute-start | bytes 49160 | tf_op jit(solution)/shard_map/ppermute | solution.py:383
  80.8 0.4 collective-permute-start.12
  81.2 1.4 %collective-permute-done.14.refs_3_ = f32[32,128]{1,0:T(8,128)S(1)} collective-permute-done((f32[32,128]{1,0:T(8,128)S(1)}, f32[32,128]{1,0:T(8,128)S(1)}, u32[]{:S(2)}, u32[]{:S(2)}) %collective-permute-start.14) | collective-permute-done | bytes 16416 | tf_op jit(solution)/shard_map/ppermute | solution.py:383
  82.6 0.5 collective-permute-done.13.refs_2_
  83.1 0.0 collective-permute-done.12.refs_1_
  83.1 0.8 cells.7
  (8 shorter events, 0.0 us)
Async XLA Ops:
  0.6 22.8 %copy-start.2 = (f32[2,2,1024]{2,1,0:T(2,128)S(1)}, f32[2,2,1024]{2,1,0:T(2,128)}, u32[]{:S(2)}) copy-start(f32[2,2,1024]{2,1,0:T(2,128)} %refs_4_.1) | copy-start | bytes 49156
  0.6 18.3 %copy-start = (f32[1024]{0:T(1024)S(1)}, f32[1024]{0:T(1024)}, u32[]{:S(2)}) copy-start(f32[1024]{0:T(1024)} %param.8) | copy-start | bytes 12292
  0.7 18.3 %copy-start.1 = (f32[1024]{0:T(1024)S(1)}, f32[1024]{0:T(1024)}, u32[]{:S(2)}) copy-start(f32[1024]{0:T(1024)} %param.7) | copy-start | bytes 12292
  0.7 22.8 %copy-start.3 = (s32[2,2,1024]{2,1,0:T(2,128)S(1)}, s32[2,2,1024]{2,1,0:T(2,128)}, u32[]{:S(2)}) copy-start(s32[2,2,1024]{2,1,0:T(2,128)} %refs_6_.1) | copy-start | bytes 49156
  0.7 22.8 %copy-start.4 = (f32[2,1024]{1,0:T(2,128)S(1)}, f32[2,1024]{1,0:T(2,128)}, u32[]{:S(2)}) copy-start(f32[2,1024]{1,0:T(2,128)} %refs_5_.1) | copy-start | bytes 24580
  19.6 3.3 %collective-permute-start.2 = (f32[32,128]{1,0:T(8,128)S(1)}, f32[32,128]{1,0:T(8,128)S(1)}, u32[]{:S(2)}, u32[]{:S(2)}) collective-permute-start(f32[32,128]{1,0:T(8,128)S(1)} %rows.5.refs_0_), channel_id=1, source_target_pairs={{0,24},{8,16},{16,8},{24,0},{1,25},{9,17},{17,9},{25,1},{2,26},{10... | collective-permute-start | bytes 49160 | tf_op jit(solution)/shard_map/ppermute | solution.py:383
  19.7 3.8 %collective-permute-start.1 = (f32[32,128]{1,0:T(8,128)S(1)}, f32[32,128]{1,0:T(8,128)S(1)}, u32[]{:S(2)}, u32[]{:S(2)}) collective-permute-start(f32[32,128]{1,0:T(8,128)S(1)} %rows.5.refs_0_), channel_id=1, source_target_pairs={{0,16},{8,24},{16,0},{24,8},{1,17},{9,25},{17,1},{25,9},{2,18},{10... | collective-permute-start | bytes 49160 | tf_op jit(solution)/shard_map/ppermute | solution.py:383
  21.2 2.3 %collective-permute-start = (f32[32,128]{1,0:T(8,128)S(1)}, f32[32,128]{1,0:T(8,128)S(1)}, u32[]{:S(2)}, u32[]{:S(2)}) collective-permute-start(f32[32,128]{1,0:T(8,128)S(1)} %rows.5.refs_0_), channel_id=1, source_target_pairs={{0,8},{8,0},{16,24},{24,16},{1,9},{9,1},{17,25},{25,17},{2,10},{10... | collective-permute-start | bytes 49160 | tf_op jit(solution)/shard_map/ppermute | solution.py:383
  34.6 3.3 %collective-permute-start.5 = (f32[32,128]{1,0:T(8,128)S(1)}, f32[32,128]{1,0:T(8,128)S(1)}, u32[]{:S(2)}, u32[]{:S(2)}) collective-permute-start(f32[32,128]{1,0:T(8,128)S(1)} %rows.6.refs_0_), channel_id=1, source_target_pairs={{0,24},{8,16},{16,8},{24,0},{1,25},{9,17},{17,9},{25,1},{2,26},{10... | collective-permute-start | bytes 49160 | tf_op jit(solution)/shard_map/ppermute | solution.py:383
  34.6 3.8 %collective-permute-start.4 = (f32[32,128]{1,0:T(8,128)S(1)}, f32[32,128]{1,0:T(8,128)S(1)}, u32[]{:S(2)}, u32[]{:S(2)}) collective-permute-start(f32[32,128]{1,0:T(8,128)S(1)} %rows.6.refs_0_), channel_id=1, source_target_pairs={{0,16},{8,24},{16,0},{24,8},{1,17},{9,25},{17,1},{25,9},{2,18},{10... | collective-permute-start | bytes 49160 | tf_op jit(solution)/shard_map/ppermute | solution.py:383
  36.1 2.3 %collective-permute-start.3 = (f32[32,128]{1,0:T(8,128)S(1)}, f32[32,128]{1,0:T(8,128)S(1)}, u32[]{:S(2)}, u32[]{:S(2)}) collective-permute-start(f32[32,128]{1,0:T(8,128)S(1)} %rows.6.refs_0_), channel_id=1, source_target_pairs={{0,8},{8,0},{16,24},{24,16},{1,9},{9,1},{17,25},{25,17},{2,10},{10... | collective-permute-start | bytes 49160 | tf_op jit(solution)/shard_map/ppermute | solution.py:383
  49.5 3.3 %collective-permute-start.8 = (f32[32,128]{1,0:T(8,128)S(1)}, f32[32,128]{1,0:T(8,128)S(1)}, u32[]{:S(2)}, u32[]{:S(2)}) collective-permute-start(f32[32,128]{1,0:T(8,128)S(1)} %rows.7.refs_0_), channel_id=1, source_target_pairs={{0,24},{8,16},{16,8},{24,0},{1,25},{9,17},{17,9},{25,1},{2,26},{10... | collective-permute-start | bytes 49160 | tf_op jit(solution)/shard_map/ppermute | solution.py:383
  49.5 3.8 %collective-permute-start.7 = (f32[32,128]{1,0:T(8,128)S(1)}, f32[32,128]{1,0:T(8,128)S(1)}, u32[]{:S(2)}, u32[]{:S(2)}) collective-permute-start(f32[32,128]{1,0:T(8,128)S(1)} %rows.7.refs_0_), channel_id=1, source_target_pairs={{0,16},{8,24},{16,0},{24,8},{1,17},{9,25},{17,1},{25,9},{2,18},{10... | collective-permute-start | bytes 49160 | tf_op jit(solution)/shard_map/ppermute | solution.py:383
  51.0 2.3 %collective-permute-start.6 = (f32[32,128]{1,0:T(8,128)S(1)}, f32[32,128]{1,0:T(8,128)S(1)}, u32[]{:S(2)}, u32[]{:S(2)}) collective-permute-start(f32[32,128]{1,0:T(8,128)S(1)} %rows.7.refs_0_), channel_id=1, source_target_pairs={{0,8},{8,0},{16,24},{24,16},{1,9},{9,1},{17,25},{25,17},{2,10},{10... | collective-permute-start | bytes 49160 | tf_op jit(solution)/shard_map/ppermute | solution.py:383
  64.4 3.3 %collective-permute-start.11 = (f32[32,128]{1,0:T(8,128)S(1)}, f32[32,128]{1,0:T(8,128)S(1)}, u32[]{:S(2)}, u32[]{:S(2)}) collective-permute-start(f32[32,128]{1,0:T(8,128)S(1)} %rows.8.refs_0_), channel_id=1, source_target_pairs={{0,24},{8,16},{16,8},{24,0},{1,25},{9,17},{17,9},{25,1},{2,26},{10... | collective-permute-start | bytes 49160 | tf_op jit(solution)/shard_map/ppermute | solution.py:383
  64.4 3.8 %collective-permute-start.10 = (f32[32,128]{1,0:T(8,128)S(1)}, f32[32,128]{1,0:T(8,128)S(1)}, u32[]{:S(2)}, u32[]{:S(2)}) collective-permute-start(f32[32,128]{1,0:T(8,128)S(1)} %rows.8.refs_0_), channel_id=1, source_target_pairs={{0,16},{8,24},{16,0},{24,8},{1,17},{9,25},{17,1},{25,9},{2,18},{10... | collective-permute-start | bytes 49160 | tf_op jit(solution)/shard_map/ppermute | solution.py:383
  65.9 2.3 %collective-permute-start.9 = (f32[32,128]{1,0:T(8,128)S(1)}, f32[32,128]{1,0:T(8,128)S(1)}, u32[]{:S(2)}, u32[]{:S(2)}) collective-permute-start(f32[32,128]{1,0:T(8,128)S(1)} %rows.8.refs_0_), channel_id=1, source_target_pairs={{0,8},{8,0},{16,24},{24,16},{1,9},{9,1},{17,25},{25,17},{2,10},{10... | collective-permute-start | bytes 49160 | tf_op jit(solution)/shard_map/ppermute | solution.py:383
  79.3 3.3 %collective-permute-start.14 = (f32[32,128]{1,0:T(8,128)S(1)}, f32[32,128]{1,0:T(8,128)S(1)}, u32[]{:S(2)}, u32[]{:S(2)}) collective-permute-start(f32[32,128]{1,0:T(8,128)S(1)} %rows.9.refs_0_), channel_id=1, source_target_pairs={{0,24},{8,16},{16,8},{24,0},{1,25},{9,17},{17,9},{25,1},{2,26},{10... | collective-permute-start | bytes 49160 | tf_op jit(solution)/shard_map/ppermute | solution.py:383
  79.3 3.8 %collective-permute-start.13 = (f32[32,128]{1,0:T(8,128)S(1)}, f32[32,128]{1,0:T(8,128)S(1)}, u32[]{:S(2)}, u32[]{:S(2)}) collective-permute-start(f32[32,128]{1,0:T(8,128)S(1)} %rows.9.refs_0_), channel_id=1, source_target_pairs={{0,16},{8,24},{16,0},{24,8},{1,17},{9,25},{17,1},{25,9},{2,18},{10... | collective-permute-start | bytes 49160 | tf_op jit(solution)/shard_map/ppermute | solution.py:383
  80.8 2.3 %collective-permute-start.12 = (f32[32,128]{1,0:T(8,128)S(1)}, f32[32,128]{1,0:T(8,128)S(1)}, u32[]{:S(2)}, u32[]{:S(2)}) collective-permute-start(f32[32,128]{1,0:T(8,128)S(1)} %rows.9.refs_0_), channel_id=1, source_target_pairs={{0,8},{8,0},{16,24},{24,16},{1,9},{9,1},{17,25},{25,17},{2,10},{10... | collective-permute-start | bytes 49160 | tf_op jit(solution)/shard_map/ppermute | solution.py:383

commit v7 on v6

--- a/solution.py
+++ b/solution.py
@@ -17,6 +17,7 @@
 SUBLANES = 8
 SCALARS = 3
 CHUNK = 64
+MATRIX_BLOCKS = 2
 IN_FLIGHT = 6
 KERNEL_VMEM = 16 * 1024 * 1024
 
@@ -86,7 +87,7 @@
 
 
 def full(line):
-    return jnp.sum(line, axis=1, keepdims=True)
+    return jnp.broadcast_to(jnp.sum(line, axis=1, keepdims=True), line.shape)
 
 
 def spread(planes, count):
@@ -137,7 +138,17 @@
     )
     lines_in = [plane[t : t + 1] for plane in chosen for t in range(tall)]
     pieces = []
-    for b in range(rows // LANES):
+    first = 0
+    if ready is None:
+        first = MATRIX_BLOCKS
+        vector = spread(chosen, 2 * SUBLANES).astype(jnp.bfloat16)
+        product = lax.dot_general(
+            vector,
+            matrix_ref[0 : first * LANES],
+            (((1,), (1,)), ((), ())),
+            preferred_element_type=jnp.float32,
+        )
+    for b in range(first, rows // LANES):
         if ready is not None:
             ready(b)
         total = None
@@ -147,9 +158,10 @@
             total = term if total is None else total + term
         column = jnp.sum(total, axis=1, keepdims=True)
         pieces.append(jnp.sum(jnp.where(eye, column, 0.0), axis=0, keepdims=True))
+    pieces = [product[0:1, b * LANES : (b + 1) * LANES] for b in range(first)] + pieces
     edges = [field[0][0], field[1][0], field[0][-1], field[1][-1]]
     pieces.append(share_of(edges, member, members))
-    pieces += lines
+    pieces += [full(line) for line in lines]
     message = jnp.concatenate(pieces, axis=0)
     for j in range(owners):
         out_ref[j, 0 : message.shape[0], 0] = message
@@ -233,7 +245,7 @@
     up = jnp.minimum(rank + 1, owners - 1)
     above = jnp.where(lower & (rank < owners - 1), got_ref[up, blocks : blocks + tall, 0], 0.0)
     below = jnp.where(upper & (rank > 0), got_ref[down, blocks : blocks + tall, 0], 0.0)
-    pieces += [above + below, weighed, jnp.zeros((SUBLANES - 1, LANES), jnp.float32)]
+    pieces += [above + below, full(weighed), jnp.zeros((SUBLANES - 1, LANES), jnp.float32)]
     out_ref[...] = jnp.concatenate(pieces, axis=0)
 
 
@@ -301,14 +313,13 @@
         sums = sums + got_ref[j, at : at + SCALARS, 0]
     at = cells + tall
     weighed = tree_sum([ref[at : at + 1] for ref in part_refs])
-    line = weighed + sums[1:2]
-    norm_now = full(sums[0:1])
-    curvature = full(line)
+    norm_now = sums[0:1]
+    curvature = weighed + sums[1:2]
     if begin:
         direction, imaged = residual, image
     else:
-        ratio = norm_now / norms_in[0:1, 0:1]
-        curvature = curvature + ratio * (2.0 * full(sums[2:3]) + ratio * norms_in[1:2, 0:1])
+        ratio = norm_now / norms_in[0:1]
+        curvature = curvature + ratio * (2.0 * sums[2:3] + ratio * norms_in[1:2])
         direction = mapped(lambda r, d: r + ratio * d, residual, load(direction_in))
         imaged = mapped(lambda r, d: r + ratio * d, image, load(imaged_in))
     step_len = norm_now / curvature
@@ -326,8 +337,8 @@
     direction_ref, imaged_ref, norms_ref, inner_ref, out_ref = refs[2:]
     store(direction_ref, direction)
     store(imaged_ref, imaged)
-    norms_ref[0:1] = jnp.broadcast_to(norm_now, (1, LANES))
-    norms_ref[1:2] = jnp.broadcast_to(curvature, (1, LANES))
+    norms_ref[0:1] = norm_now
+    norms_ref[1:2] = curvature
     inner = operate_inner(residual, [smooth_ref[i] for i in range(layers)])
     store(inner_ref, inner)
     lines = [dot_line(residual, residual), dot_line(residual, inner), dot_line(residual, imaged)]

time: 84.2 us -> 83.5 us (level)
  no operation moved by 1% of the time
where the time goes in v7:
time: 83.5 us; the launch traced here: 83.1 us
  blocking collectives  51.7 us (62%)
  Pallas kernels  11.8 us (14%)
  waiting for transfers between devices  9.57 us (11%)
  starting transfers between devices  9.35 us (11%)
    all_to_all x5, blocking collectives, across(): return lax.all_to_all(sent, 'mp', 0, 0, tiled=True)  51.7 us
    ppermute x15, waiting for transfers between devices, along(): lax.ppermute(sent, 'dp', [(i, i ^ s) for i in range(blocks)])  9.57 us
    ppermute x15, starting transfers between devices, along(): lax.ppermute(sent, 'dp', [(i, i ^ s) for i in range(blocks)])  9.35 us
    pallas_call x10, Pallas kernels, call(): pl.pallas_call(kernel, out_shape=out_shape, in_specs=[vmem] * len(operand...  7.58 us
    pallas_call x1, Pallas kernels, local(): pl.pallas_call(start_kernel, out_shape=(jax.ShapeDtypeStruct((rows, layer...  4.2 us
  transfers between devices with their start and end apart: 15, of which 10 were waited for; matrix products, arithmetic and copies ran while one was open for 0% of the time, Pallas kernels for 0%

profile of v7, /device:TPU:0, one launch (start us, length us, event | category | flops | bytes accessed | tf_op | source)
XLA Modules:
  0.0 83.1 jit_solution(12115573349624782989)
XLA Ops:
  0.6 0.0 copy-start.2
  0.7 4.2 %start.1 = (bf16[1024,2048]{1,0:T(8,128)(2,1)S(1)}, f32[8,19,1,128]{3,2,1,0:T(1,128)S(1)}) custom-call(bf16[1024,2,1024]{2,1,0:T(2,128)(2,1)} %raw_ref.1, f32[2,2,1024]{2,1,0:T(2,128)} %refs_4_.1), custom_call_target="tpu_custom_call" | custom-call | tf_op jit(solution)/shard_map/start/pallas_call | solution.py:398
  4.9 14.1 %all_to_all.25.got_ref = f32[8,19,1,128]{3,2,1,0:T(1,128)S(1)} all-to-all(f32[8,19,1,128]{3,2,1,0:T(1,128)S(1)} %get-tuple-element.31), channel_id=1, replica_groups=mesh['dp'=4,'mp'=8] {'mp'}, dimensions={0} | all-to-all | bytes 155648 | tf_op jit(solution)/shard_map/all_to_all | solution.py:381
  19.0 0.7 rows.5.refs_0_
  19.7 0.0 collective-permute-start.2
  19.7 1.5 %collective-permute-start.1 = (f32[32,128]{1,0:T(8,128)S(1)}, f32[32,128]{1,0:T(8,128)S(1)}, u32[]{:S(2)}, u32[]{:S(2)}) collective-permute-start(f32[32,128]{1,0:T(8,128)S(1)} %rows.5.refs_0_), channel_id=1, source_target_pairs={{0,16},{8,24},{16,0},{24,8},{1,17},{9,25},{17,1},{25,9},{2,18},{10... | collective-permute-start | bytes 49160 | tf_op jit(solution)/shard_map/ppermute | solution.py:394
  21.2 0.3 collective-permute-start
  21.5 1.4 %collective-permute-done.2.refs_3_ = f32[32,128]{1,0:T(8,128)S(1)} collective-permute-done((f32[32,128]{1,0:T(8,128)S(1)}, f32[32,128]{1,0:T(8,128)S(1)}, u32[]{:S(2)}, u32[]{:S(2)}) %collective-permute-start.2) | collective-permute-done | bytes 16416 | tf_op jit(solution)/shard_map/ppermute | solution.py:394
  23.0 0.5 collective-permute-done.1.refs_2_
  23.4 0.0 collective-permute-done.refs_1_
  23.4 0.0 copy-done.4
  23.5 1.0 %first.1 = (f32[8,19,1,128]{3,2,1,0:T(1,128)S(1)}, f32[2,2,8,128]{3,2,1,0:T(8,128)S(1)}, f32[2,2,8,128]{3,2,1,0:T(8,128)S(1)}, f32[2,8,128]{2,1,0:T(8,128)S(1)}, f32[2,2,8,128]{3,2,1,0:T(8,128)S(1)}) custom-call(bf16[1024,2048]{1,0:T(8,128)(2,1)S(1)} %get-tuple-element.30.matrix_ref, f32[32,128]{1,0:T(8,128)S(1)} %rows.5.refs_0_, ...), custom_call_target="tpu_custom_call" | custom-call | tf_op jit(solution)/shard_map/first/pallas_call | solution.py:370
  24.4 9.5 %all_to_all.26.got_ref.refs_4_ = f32[8,19,1,128]{3,2,1,0:T(1,128)S(1)} all-to-all(f32[8,19,1,128]{3,2,1,0:T(1,128)S(1)} %get-tuple-element.32), channel_id=1, replica_groups=mesh['dp'=4,'mp'=8] {'mp'}, dimensions={0} | all-to-all | bytes 155648 | tf_op jit(solution)/shard_map/all_to_all | solution.py:381
  33.9 0.7 rows.6.refs_0_
  34.5 0.0 collective-permute-start.5
  34.5 1.5 %collective-permute-start.4 = (f32[32,128]{1,0:T(8,128)S(1)}, f32[32,128]{1,0:T(8,128)S(1)}, u32[]{:S(2)}, u32[]{:S(2)}) collective-permute-start(f32[32,128]{1,0:T(8,128)S(1)} %rows.6.refs_0_), channel_id=1, source_target_pairs={{0,16},{8,24},{16,0},{24,8},{1,17},{9,25},{17,1},{25,9},{2,18},{10... | collective-permute-start | bytes 49160 | tf_op jit(solution)/shard_map/ppermute | solution.py:394
  36.0 0.4 collective-permute-start.3
  36.4 1.4 %collective-permute-done.5.refs_3_ = f32[32,128]{1,0:T(8,128)S(1)} collective-permute-done((f32[32,128]{1,0:T(8,128)S(1)}, f32[32,128]{1,0:T(8,128)S(1)}, u32[]{:S(2)}, u32[]{:S(2)}) %collective-permute-start.5) | collective-permute-done | bytes 16416 | tf_op jit(solution)/shard_map/ppermute | solution.py:394
  37.9 0.5 collective-permute-done.4.refs_2_
  38.3 0.0 collective-permute-done.3.refs_1_
  38.3 0.9 %cells.4 = (f32[2,2,8,128]{3,2,1,0:T(8,128)S(1)}, f32[2,2,8,128]{3,2,1,0:T(8,128)S(1)}, f32[2,2,8,128]{3,2,1,0:T(8,128)S(1)}, f32[2,2,8,128]{3,2,1,0:T(8,128)S(1...) custom-call(bf16[1024,2048]{1,0:T(8,128)(2,1)S(1)} %get-tuple-element.30.matrix_ref, ...), custom_call_target="tpu_custom_call" | custom-call | tf_op jit(solution)/shard_map/cells/pallas_call | solution.py:370
  39.2 9.4 %all_to_all.27.got_ref.refs_4_ = f32[8,19,1,128]{3,2,1,0:T(1,128)S(1)} all-to-all(f32[8,19,1,128]{3,2,1,0:T(1,128)S(1)} %get-tuple-element.37), channel_id=1, replica_groups=mesh['dp'=4,'mp'=8] {'mp'}, dimensions={0} | all-to-all | bytes 155648 | tf_op jit(solution)/shard_map/all_to_all | solution.py:381
  48.6 0.7 rows.7.refs_0_
  49.2 0.0 collective-permute-start.8
  49.3 1.5 %collective-permute-start.7 = (f32[32,128]{1,0:T(8,128)S(1)}, f32[32,128]{1,0:T(8,128)S(1)}, u32[]{:S(2)}, u32[]{:S(2)}) collective-permute-start(f32[32,128]{1,0:T(8,128)S(1)} %rows.7.refs_0_), channel_id=1, source_target_pairs={{0,16},{8,24},{16,0},{24,8},{1,17},{9,25},{17,1},{25,9},{2,18},{10... | collective-permute-start | bytes 49160 | tf_op jit(solution)/shard_map/ppermute | solution.py:394
  50.7 0.4 collective-permute-start.6
  51.1 1.4 %collective-permute-done.8.refs_3_ = f32[32,128]{1,0:T(8,128)S(1)} collective-permute-done((f32[32,128]{1,0:T(8,128)S(1)}, f32[32,128]{1,0:T(8,128)S(1)}, u32[]{:S(2)}, u32[]{:S(2)}) %collective-permute-start.8) | collective-permute-done | bytes 16416 | tf_op jit(solution)/shard_map/ppermute | solution.py:394
  52.6 0.5 collective-permute-done.7.refs_2_
  53.0 0.0 collective-permute-done.6.refs_1_
  53.0 0.9 %cells.5 = (f32[2,2,8,128]{3,2,1,0:T(8,128)S(1)}, f32[2,2,8,128]{3,2,1,0:T(8,128)S(1)}, f32[2,2,8,128]{3,2,1,0:T(8,128)S(1)}, f32[2,2,8,128]{3,2,1,0:T(8,128)S(1...) custom-call(bf16[1024,2048]{1,0:T(8,128)(2,1)S(1)} %get-tuple-element.30.matrix_ref, ...), custom_call_target="tpu_custom_call" | custom-call | tf_op jit(solution)/shard_map/cells/pallas_call | solution.py:370
  53.9 9.4 %all_to_all.28.got_ref.refs_4_ = f32[8,19,1,128]{3,2,1,0:T(1,128)S(1)} all-to-all(f32[8,19,1,128]{3,2,1,0:T(1,128)S(1)} %get-tuple-element.44), channel_id=1, replica_groups=mesh['dp'=4,'mp'=8] {'mp'}, dimensions={0} | all-to-all | bytes 155648 | tf_op jit(solution)/shard_map/all_to_all | solution.py:381
  63.3 0.7 rows.8.refs_0_
  64.0 0.0 collective-permute-start.11
  64.0 1.5 %collective-permute-start.10 = (f32[32,128]{1,0:T(8,128)S(1)}, f32[32,128]{1,0:T(8,128)S(1)}, u32[]{:S(2)}, u32[]{:S(2)}) collective-permute-start(f32[32,128]{1,0:T(8,128)S(1)} %rows.8.refs_0_), channel_id=1, source_target_pairs={{0,16},{8,24},{16,0},{24,8},{1,17},{9,25},{17,1},{25,9},{2,18},{10... | collective-permute-start | bytes 49160 | tf_op jit(solution)/shard_map/ppermute | solution.py:394
  65.4 0.4 collective-permute-start.9
  65.8 1.4 %collective-permute-done.11.refs_3_ = f32[32,128]{1,0:T(8,128)S(1)} collective-permute-done((f32[32,128]{1,0:T(8,128)S(1)}, f32[32,128]{1,0:T(8,128)S(1)}, u32[]{:S(2)}, u32[]{:S(2)}) %collective-permute-start.11) | collective-permute-done | bytes 16416 | tf_op jit(solution)/shard_map/ppermute | solution.py:394
  67.3 0.5 collective-permute-done.10.refs_2_
  67.7 0.0 collective-permute-done.9.refs_1_
  67.7 0.9 %cells.6 = (f32[2,2,8,128]{3,2,1,0:T(8,128)S(1)}, f32[2,2,8,128]{3,2,1,0:T(8,128)S(1)}, f32[2,2,8,128]{3,2,1,0:T(8,128)S(1)}, f32[2,2,8,128]{3,2,1,0:T(8,128)S(1...) custom-call(bf16[1024,2048]{1,0:T(8,128)(2,1)S(1)} %get-tuple-element.30.matrix_ref, ...), custom_call_target="tpu_custom_call" | custom-call | tf_op jit(solution)/shard_map/cells/pallas_call | solution.py:370
  68.6 9.4 %all_to_all.29.got_ref.refs_4_ = f32[8,19,1,128]{3,2,1,0:T(1,128)S(1)} all-to-all(f32[8,19,1,128]{3,2,1,0:T(1,128)S(1)} %get-tuple-element.51), channel_id=1, replica_groups=mesh['dp'=4,'mp'=8] {'mp'}, dimensions={0} | all-to-all | bytes 155648 | tf_op jit(solution)/shard_map/all_to_all | solution.py:381
  78.0 0.7 rows.9.refs_0_
  78.7 0.0 collective-permute-start.14
  78.7 1.5 %collective-permute-start.13 = (f32[32,128]{1,0:T(8,128)S(1)}, f32[32,128]{1,0:T(8,128)S(1)}, u32[]{:S(2)}, u32[]{:S(2)}) collective-permute-start(f32[32,128]{1,0:T(8,128)S(1)} %rows.9.refs_0_), channel_id=1, source_target_pairs={{0,16},{8,24},{16,0},{24,8},{1,17},{9,25},{17,1},{25,9},{2,18},{10... | collective-permute-start | bytes 49160 | tf_op jit(solution)/shard_map/ppermute | solution.py:394
  80.1 0.4 collective-permute-start.12
  80.5 1.4 %collective-permute-done.14.refs_3_ = f32[32,128]{1,0:T(8,128)S(1)} collective-permute-done((f32[32,128]{1,0:T(8,128)S(1)}, f32[32,128]{1,0:T(8,128)S(1)}, u32[]{:S(2)}, u32[]{:S(2)}) %collective-permute-start.14) | collective-permute-done | bytes 16416 | tf_op jit(solution)/shard_map/ppermute | solution.py:394
  82.0 0.5 collective-permute-done.13.refs_2_
  82.4 0.0 collective-permute-done.12.refs_1_
  82.4 0.7 cells.7
  (8 shorter events, 0.0 us)
Async XLA Ops:
  0.6 22.8 %copy-start.2 = (f32[2,2,1024]{2,1,0:T(2,128)S(1)}, f32[2,2,1024]{2,1,0:T(2,128)}, u32[]{:S(2)}) copy-start(f32[2,2,1024]{2,1,0:T(2,128)} %refs_4_.1) | copy-start | bytes 49156
  0.6 18.3 %copy-start = (f32[1024]{0:T(1024)S(1)}, f32[1024]{0:T(1024)}, u32[]{:S(2)}) copy-start(f32[1024]{0:T(1024)} %param.8) | copy-start | bytes 12292
  0.7 18.3 %copy-start.1 = (f32[1024]{0:T(1024)S(1)}, f32[1024]{0:T(1024)}, u32[]{:S(2)}) copy-start(f32[1024]{0:T(1024)} %param.7) | copy-start | bytes 12292
  0.7 22.8 %copy-start.3 = (s32[2,2,1024]{2,1,0:T(2,128)S(1)}, s32[2,2,1024]{2,1,0:T(2,128)}, u32[]{:S(2)}) copy-start(s32[2,2,1024]{2,1,0:T(2,128)} %refs_6_.1) | copy-start | bytes 49156
  0.7 22.8 %copy-start.4 = (f32[2,1024]{1,0:T(2,128)S(1)}, f32[2,1024]{1,0:T(2,128)}, u32[]{:S(2)}) copy-start(f32[2,1024]{1,0:T(2,128)} %refs_5_.1) | copy-start | bytes 24580
  19.7 3.3 %collective-permute-start.2 = (f32[32,128]{1,0:T(8,128)S(1)}, f32[32,128]{1,0:T(8,128)S(1)}, u32[]{:S(2)}, u32[]{:S(2)}) collective-permute-start(f32[32,128]{1,0:T(8,128)S(1)} %rows.5.refs_0_), channel_id=1, source_target_pairs={{0,24},{8,16},{16,8},{24,0},{1,25},{9,17},{17,9},{25,1},{2,26},{10... | collective-permute-start | bytes 49160 | tf_op jit(solution)/shard_map/ppermute | solution.py:394
  19.7 3.8 %collective-permute-start.1 = (f32[32,128]{1,0:T(8,128)S(1)}, f32[32,128]{1,0:T(8,128)S(1)}, u32[]{:S(2)}, u32[]{:S(2)}) collective-permute-start(f32[32,128]{1,0:T(8,128)S(1)} %rows.5.refs_0_), channel_id=1, source_target_pairs={{0,16},{8,24},{16,0},{24,8},{1,17},{9,25},{17,1},{25,9},{2,18},{10... | collective-permute-start | bytes 49160 | tf_op jit(solution)/shard_map/ppermute | solution.py:394
  21.2 2.3 %collective-permute-start = (f32[32,128]{1,0:T(8,128)S(1)}, f32[32,128]{1,0:T(8,128)S(1)}, u32[]{:S(2)}, u32[]{:S(2)}) collective-permute-start(f32[32,128]{1,0:T(8,128)S(1)} %rows.5.refs_0_), channel_id=1, source_target_pairs={{0,8},{8,0},{16,24},{24,16},{1,9},{9,1},{17,25},{25,17},{2,10},{10... | collective-permute-start | bytes 49160 | tf_op jit(solution)/shard_map/ppermute | solution.py:394
  34.5 3.3 %collective-permute-start.5 = (f32[32,128]{1,0:T(8,128)S(1)}, f32[32,128]{1,0:T(8,128)S(1)}, u32[]{:S(2)}, u32[]{:S(2)}) collective-permute-start(f32[32,128]{1,0:T(8,128)S(1)} %rows.6.refs_0_), channel_id=1, source_target_pairs={{0,24},{8,16},{16,8},{24,0},{1,25},{9,17},{17,9},{25,1},{2,26},{10... | collective-permute-start | bytes 49160 | tf_op jit(solution)/shard_map/ppermute | solution.py:394
  34.5 3.8 %collective-permute-start.4 = (f32[32,128]{1,0:T(8,128)S(1)}, f32[32,128]{1,0:T(8,128)S(1)}, u32[]{:S(2)}, u32[]{:S(2)}) collective-permute-start(f32[32,128]{1,0:T(8,128)S(1)} %rows.6.refs_0_), channel_id=1, source_target_pairs={{0,16},{8,24},{16,0},{24,8},{1,17},{9,25},{17,1},{25,9},{2,18},{10... | collective-permute-start | bytes 49160 | tf_op jit(solution)/shard_map/ppermute | solution.py:394
  36.0 2.3 %collective-permute-start.3 = (f32[32,128]{1,0:T(8,128)S(1)}, f32[32,128]{1,0:T(8,128)S(1)}, u32[]{:S(2)}, u32[]{:S(2)}) collective-permute-start(f32[32,128]{1,0:T(8,128)S(1)} %rows.6.refs_0_), channel_id=1, source_target_pairs={{0,8},{8,0},{16,24},{24,16},{1,9},{9,1},{17,25},{25,17},{2,10},{10... | collective-permute-start | bytes 49160 | tf_op jit(solution)/shard_map/ppermute | solution.py:394
  49.2 3.3 %collective-permute-start.8 = (f32[32,128]{1,0:T(8,128)S(1)}, f32[32,128]{1,0:T(8,128)S(1)}, u32[]{:S(2)}, u32[]{:S(2)}) collective-permute-start(f32[32,128]{1,0:T(8,128)S(1)} %rows.7.refs_0_), channel_id=1, source_target_pairs={{0,24},{8,16},{16,8},{24,0},{1,25},{9,17},{17,9},{25,1},{2,26},{10... | collective-permute-start | bytes 49160 | tf_op jit(solution)/shard_map/ppermute | solution.py:394
  49.3 3.8 %collective-permute-start.7 = (f32[32,128]{1,0:T(8,128)S(1)}, f32[32,128]{1,0:T(8,128)S(1)}, u32[]{:S(2)}, u32[]{:S(2)}) collective-permute-start(f32[32,128]{1,0:T(8,128)S(1)} %rows.7.refs_0_), channel_id=1, source_target_pairs={{0,16},{8,24},{16,0},{24,8},{1,17},{9,25},{17,1},{25,9},{2,18},{10... | collective-permute-start | bytes 49160 | tf_op jit(solution)/shard_map/ppermute | solution.py:394
  50.7 2.3 %collective-permute-start.6 = (f32[32,128]{1,0:T(8,128)S(1)}, f32[32,128]{1,0:T(8,128)S(1)}, u32[]{:S(2)}, u32[]{:S(2)}) collective-permute-start(f32[32,128]{1,0:T(8,128)S(1)} %rows.7.refs_0_), channel_id=1, source_target_pairs={{0,8},{8,0},{16,24},{24,16},{1,9},{9,1},{17,25},{25,17},{2,10},{10... | collective-permute-start | bytes 49160 | tf_op jit(solution)/shard_map/ppermute | solution.py:394
  64.0 3.3 %collective-permute-start.11 = (f32[32,128]{1,0:T(8,128)S(1)}, f32[32,128]{1,0:T(8,128)S(1)}, u32[]{:S(2)}, u32[]{:S(2)}) collective-permute-start(f32[32,128]{1,0:T(8,128)S(1)} %rows.8.refs_0_), channel_id=1, source_target_pairs={{0,24},{8,16},{16,8},{24,0},{1,25},{9,17},{17,9},{25,1},{2,26},{10... | collective-permute-start | bytes 49160 | tf_op jit(solution)/shard_map/ppermute | solution.py:394
  64.0 3.8 %collective-permute-start.10 = (f32[32,128]{1,0:T(8,128)S(1)}, f32[32,128]{1,0:T(8,128)S(1)}, u32[]{:S(2)}, u32[]{:S(2)}) collective-permute-start(f32[32,128]{1,0:T(8,128)S(1)} %rows.8.refs_0_), channel_id=1, source_target_pairs={{0,16},{8,24},{16,0},{24,8},{1,17},{9,25},{17,1},{25,9},{2,18},{10... | collective-permute-start | bytes 49160 | tf_op jit(solution)/shard_map/ppermute | solution.py:394
  65.4 2.3 %collective-permute-start.9 = (f32[32,128]{1,0:T(8,128)S(1)}, f32[32,128]{1,0:T(8,128)S(1)}, u32[]{:S(2)}, u32[]{:S(2)}) collective-permute-start(f32[32,128]{1,0:T(8,128)S(1)} %rows.8.refs_0_), channel_id=1, source_target_pairs={{0,8},{8,0},{16,24},{24,16},{1,9},{9,1},{17,25},{25,17},{2,10},{10... | collective-permute-start | bytes 49160 | tf_op jit(solution)/shard_map/ppermute | solution.py:394
  78.7 3.3 %collective-permute-start.14 = (f32[32,128]{1,0:T(8,128)S(1)}, f32[32,128]{1,0:T(8,128)S(1)}, u32[]{:S(2)}, u32[]{:S(2)}) collective-permute-start(f32[32,128]{1,0:T(8,128)S(1)} %rows.9.refs_0_), channel_id=1, source_target_pairs={{0,24},{8,16},{16,8},{24,0},{1,25},{9,17},{17,9},{25,1},{2,26},{10... | collective-permute-start | bytes 49160 | tf_op jit(solution)/shard_map/ppermute | solution.py:394
  78.7 3.8 %collective-permute-start.13 = (f32[32,128]{1,0:T(8,128)S(1)}, f32[32,128]{1,0:T(8,128)S(1)}, u32[]{:S(2)}, u32[]{:S(2)}) collective-permute-start(f32[32,128]{1,0:T(8,128)S(1)} %rows.9.refs_0_), channel_id=1, source_target_pairs={{0,16},{8,24},{16,0},{24,8},{1,17},{9,25},{17,1},{25,9},{2,18},{10... | collective-permute-start | bytes 49160 | tf_op jit(solution)/shard_map/ppermute | solution.py:394
  80.1 2.3 %collective-permute-start.12 = (f32[32,128]{1,0:T(8,128)S(1)}, f32[32,128]{1,0:T(8,128)S(1)}, u32[]{:S(2)}, u32[]{:S(2)}) collective-permute-start(f32[32,128]{1,0:T(8,128)S(1)} %rows.9.refs_0_), channel_id=1, source_target_pairs={{0,8},{8,0},{16,24},{24,16},{1,9},{9,1},{17,25},{25,17},{2,10},{10... | collective-permute-start | bytes 49160 | tf_op jit(solution)/shard_map/ppermute | solution.py:394
